TPU v7x, 16 devices: a whole 2x2x2 slice. The times are simulated.
16 devices in a mesh: fsdp: 16 (over z, y, x, core).
Axes of the slice: x: 2, y: 2, z: 2, core: 2. Of those that a mesh axis runs over, the one named last changes fastest.
Arguments:
- token_ids: int32 [16, 512], P('fsdp')
- grad_y: bfloat16 [16, 512, 1536], P('fsdp')
- table: bfloat16 [151936, 1536], P('fsdp')
- norm1_gain: bfloat16 [1536], P('fsdp')
- norm2_gain: bfloat16 [1536], P('fsdp')
- w_query: bfloat16 [1536, 12, 128], P('fsdp')
- w_key: bfloat16 [1536, 2, 128], P('fsdp')
- w_value: bfloat16 [1536, 2, 128], P('fsdp')
- w_out: bfloat16 [1536, 1536], P('fsdp')
- w_gate: bfloat16 [1536, 8960], P('fsdp')
- w_up: bfloat16 [1536, 8960], P('fsdp')
- w_down: bfloat16 [8960, 1536], P('fsdp')
Outputs:
- output 1: bfloat16 [16, 512, 1536], P('fsdp')
- output 2: bfloat16 [151936, 1536], P('fsdp')
- output 3: bfloat16 [1536], P('fsdp')
- output 4: bfloat16 [1536], P('fsdp')
- output 5: bfloat16 [1536, 12, 128], P('fsdp')
- output 6: bfloat16 [1536, 2, 128], P('fsdp')
- output 7: bfloat16 [1536, 2, 128], P('fsdp')
- output 8: bfloat16 [1536, 1536], P('fsdp')
- output 9: bfloat16 [1536, 8960], P('fsdp')
- output 10: bfloat16 [1536, 8960], P('fsdp')
- output 11: bfloat16 [8960, 1536], P('fsdp')
All inputs are finite; a program needn't handle non-finite values.
Results may differ from a plain program's by a relative error of at most 0.0153617.
Values are sent between devices in bfloat16 or wider.
A program may use at most 1 GiB of HBM per device.

v0:
```python
import jax
import jax.numpy as jnp
from jax import lax
from jax.sharding import PartitionSpec as P

AXIS_NAME = "fsdp"
NORM_EPS = 1e-5
ROPE_THETA = 500000.0


def rms_norm(x_f32, gain_f32):
    inv_rms = lax.rsqrt(jnp.mean(x_f32 * x_f32, axis=-1, keepdims=True) + NORM_EPS)
    return (x_f32 * inv_rms * gain_f32).astype(jnp.bfloat16)


def rotary(x_f32):
    head_dim = x_f32.shape[-1]
    half_dim = head_dim // 2
    seq_len = x_f32.shape[-3]
    inv_freq = ROPE_THETA ** (-2.0 * jnp.arange(half_dim, dtype=jnp.float32) / head_dim)
    angles = jnp.arange(seq_len, dtype=jnp.float32)[:, None] * inv_freq[None, :]
    cos_tab = jnp.cos(angles)[:, None, :]
    sin_tab = jnp.sin(angles)[:, None, :]
    lo_half = x_f32[..., :half_dim]
    hi_half = x_f32[..., half_dim:]
    return jnp.concatenate([lo_half * cos_tab - hi_half * sin_tab, hi_half * cos_tab + lo_half * sin_tab], axis=-1)


def attend(q_f32, k_f32, v_bf16):
    batch_loc, seq_len, q_heads, head_dim = q_f32.shape
    kv_heads = k_f32.shape[2]
    q_rot = rotary(q_f32).astype(jnp.bfloat16).reshape(batch_loc, seq_len, kv_heads, q_heads // kv_heads, head_dim)
    k_rot = rotary(k_f32).astype(jnp.bfloat16)
    scores = jnp.einsum("bqkgd,bskd->bkgqs", q_rot, k_rot, preferred_element_type=jnp.float32) * head_dim ** -0.5
    positions = jnp.arange(seq_len)
    causal = positions[:, None] >= positions[None, :]
    scores = jnp.where(causal, scores, -1e30)
    prob_bf = jax.nn.softmax(scores, axis=-1).astype(jnp.bfloat16)
    attn_out = jnp.einsum("bkgqs,bskd->bqkgd", prob_bf, v_bf16, preferred_element_type=jnp.float32)
    return attn_out.astype(jnp.bfloat16).reshape(batch_loc, seq_len, q_heads * head_dim)


def gated(gate_f32, up_f32):
    return (jax.nn.silu(gate_f32) * up_f32).astype(jnp.bfloat16)


def layer_pass(emb_rows, grad_y, norm1_gain, norm2_gain, w_query, w_key, w_value, w_out, w_gate, w_up, w_down):
    x_f32 = emb_rows.astype(jnp.float32)
    h_one, norm1_pull = jax.vjp(rms_norm, x_f32, norm1_gain.astype(jnp.float32))
    q_f32 = jnp.einsum("bsd,dhe->bshe", h_one, w_query, preferred_element_type=jnp.float32)
    k_f32 = jnp.einsum("bsd,dhe->bshe", h_one, w_key, preferred_element_type=jnp.float32)
    v_bf16 = jnp.einsum("bsd,dhe->bshe", h_one, w_value, preferred_element_type=jnp.float32).astype(jnp.bfloat16)
    attn_out, attn_pull = jax.vjp(attend, q_f32, k_f32, v_bf16)
    resid_f32 = x_f32 + jnp.einsum("bse,ed->bsd", attn_out, w_out, preferred_element_type=jnp.float32)
    resid_two = resid_f32.astype(jnp.bfloat16).astype(jnp.float32)
    h_two, norm2_pull = jax.vjp(rms_norm, resid_two, norm2_gain.astype(jnp.float32))
    gate_f32 = jnp.einsum("bsd,df->bsf", h_two, w_gate, preferred_element_type=jnp.float32)
    up_f32 = jnp.einsum("bsd,df->bsf", h_two, w_up, preferred_element_type=jnp.float32)
    act_bf16, act_pull = jax.vjp(gated, gate_f32, up_f32)
    layer_out = (resid_two + jnp.einsum("bsf,fd->bsd", act_bf16, w_down, preferred_element_type=jnp.float32)).astype(jnp.bfloat16)
    g_down = jnp.einsum("bsf,bsd->fd", act_bf16, grad_y, preferred_element_type=jnp.float32)
    d_act = jnp.einsum("bsd,fd->bsf", grad_y, w_down, preferred_element_type=jnp.float32).astype(jnp.bfloat16)
    d_gate, d_up = act_pull(d_act)
    d_gate = d_gate.astype(jnp.bfloat16)
    d_up = d_up.astype(jnp.bfloat16)
    g_gate = jnp.einsum("bsd,bsf->df", h_two, d_gate, preferred_element_type=jnp.float32)
    g_up = jnp.einsum("bsd,bsf->df", h_two, d_up, preferred_element_type=jnp.float32)
    d_h_two = (jnp.einsum("bsf,df->bsd", d_gate, w_gate, preferred_element_type=jnp.float32) + jnp.einsum("bsf,df->bsd", d_up, w_up, preferred_element_type=jnp.float32)).astype(jnp.bfloat16)
    d_resid_two, g_norm2 = norm2_pull(d_h_two)
    d_resid = (grad_y.astype(jnp.float32) + d_resid_two).astype(jnp.bfloat16)
    g_out = jnp.einsum("bse,bsd->ed", attn_out, d_resid, preferred_element_type=jnp.float32)
    d_attn = jnp.einsum("bsd,ed->bse", d_resid, w_out, preferred_element_type=jnp.float32).astype(jnp.bfloat16)
    d_query, d_key, d_value = attn_pull(d_attn)
    d_query = d_query.astype(jnp.bfloat16)
    d_key = d_key.astype(jnp.bfloat16)
    g_query = jnp.einsum("bsd,bshe->dhe", h_one, d_query, preferred_element_type=jnp.float32)
    g_key = jnp.einsum("bsd,bshe->dhe", h_one, d_key, preferred_element_type=jnp.float32)
    g_value = jnp.einsum("bsd,bshe->dhe", h_one, d_value, preferred_element_type=jnp.float32)
    d_h_one = (jnp.einsum("bshe,dhe->bsd", d_query, w_query, preferred_element_type=jnp.float32) + jnp.einsum("bshe,dhe->bsd", d_key, w_key, preferred_element_type=jnp.float32) + jnp.einsum("bshe,dhe->bsd", d_value, w_value, preferred_element_type=jnp.float32)).astype(jnp.bfloat16)
    d_x, g_norm1 = norm1_pull(d_h_one)
    d_emb = (d_resid.astype(jnp.float32) + d_x).astype(jnp.bfloat16)
    return layer_out, d_emb, (g_norm1, g_norm2, g_query, g_key, g_value, g_out, g_gate, g_up, g_down)


def solution(mesh):
    spec_1d = P(AXIS_NAME)
    spec_2d = P(AXIS_NAME, None)
    spec_3d = P(AXIS_NAME, None, None)
    in_specs = (spec_2d, spec_3d, spec_2d, spec_1d, spec_1d, spec_3d, spec_3d, spec_3d, spec_2d, spec_2d, spec_2d, spec_2d)
    out_specs = (spec_3d, spec_2d, spec_1d, spec_1d, spec_3d, spec_3d, spec_3d, spec_2d, spec_2d, spec_2d, spec_2d)

    def device_step(token_ids, grad_y, table, *weight_shards):
        ids_all = lax.all_gather(token_ids, AXIS_NAME, axis=0, tiled=True)
        rows_dev = table.shape[0]
        rel_ids = ids_all - lax.axis_index(AXIS_NAME) * rows_dev
        owned = (rel_ids >= 0) & (rel_ids < rows_dev)
        picked = jnp.take(table, jnp.where(owned, rel_ids, 0), axis=0)
        part_emb = jnp.where(owned[:, :, None], picked, jnp.zeros((), jnp.bfloat16))
        emb_rows = lax.psum_scatter(part_emb, AXIS_NAME, scatter_dimension=0, tiled=True)
        full_weights = [lax.all_gather(w_shard, AXIS_NAME, axis=0, tiled=True) for w_shard in weight_shards]
        layer_out, d_emb, partials = layer_pass(emb_rows, grad_y, *full_weights)
        grads = [lax.psum_scatter(part_grad, AXIS_NAME, scatter_dimension=0, tiled=True).astype(jnp.bfloat16) for part_grad in partials]
        d_emb_all = lax.all_gather(d_emb, AXIS_NAME, axis=0, tiled=True)
        seg_ids = jnp.where(owned, rel_ids, rows_dev).reshape(-1)
        d_rows = jax.ops.segment_sum(d_emb_all.reshape(-1, d_emb_all.shape[-1]).astype(jnp.float32), seg_ids, num_segments=rows_dev)
        return tuple([layer_out, d_rows.astype(jnp.bfloat16)] + grads)

    return jax.shard_map(device_step, mesh=mesh, in_specs=in_specs, out_specs=out_specs, check_vma=False)
```

profile of v0, /device:TPU:0, one launch (start us, length us, event | category | flops | bytes accessed | tf_op | source)
XLA Modules:
  0.0 1970.2 jit_solution(1527246688013933943)
XLA Ops:
  7.2 14.6 all-gather
  22.5 62.3 %gather_fusion = bf16[8192,1536]{1,0:T(8,128)(2,1)} fusion(bf16[9496,1536]{1,0:T(8,128)(2,1)} %param.14, s32[8192]{0:T(1024)S(1)} %broadcast_clamp_fusion.1), kind=kCustom, calls=%fused_computation | custom fusion | bytes 50364416 | tf_op jit(solution)/shard_map/jit(_take)/gather | solution.py:97
  84.8 17.4 select_select_fusion
  106.0 31.9 %all-reduce.9 = (bf16[1536]{0:T(1024)(128)(2,1)S(1)}, bf16[1536]{0:T(1024)(128)(2,1)S(1)}) all-reduce(bf16[1536]{0:T(1024)(128)(2,1)S(1)} %dynamic-update-slice, bf16[1536]{0:T(1024)(128)(2,1)S(1)} %dynamic-update-slice.1), channel_id=1, replica_groups=mesh['fsdp'=16] {'fsdp'}, use_global_device_ids=true, to_apply=%add.4 | all-reduce | flops 3072 | bytes 12288
  138.6 16.0 all_gather.35
  154.6 15.9 all_gather.36
  170.5 73.9 %reduce-scatter.9.cloned.1.call-done = bf16[1,512,1536]{2,1,0:T(8,128)(2,1)} async-done(((bf16[16,512,1536]{2,1,0:T(8,128)(2,1)}), bf16[1,512,1536]{2,1,0:T(8,128)(2,1)}) %reduce-scatter.9.cloned.1.call-update) | async-done | bytes 1572880 | tf_op jit(solution)/shard_map/reduce_scatter | solution.py:99
  244.4 1.8 fusion.49
  246.2 37.1 %all-gather.8.cloned.1.call-done = bf16[1536,12,128]{2,0,1:T(8,128)(2,1)} async-done(((bf16[96,12,128]{2,0,1:T(8,128)(2,1)}), bf16[1536,12,128]{2,0,1:T(8,128)(2,1)}) %all-gather.8.cloned.1.call-update) | async-done | bytes 4718608 | tf_op jit(solution)/shard_map/all_gather | solution.py:100
  283.4 5.4 convolution_bitcast_fusion.5
  288.8 1.7 subtract_convert_fusion
  290.5 1.9 copy.68
  292.4 2.8 copy.67
  295.3 2.0 convolution_bitcast_fusion.6
  297.4 1.3 fusion.86
  298.8 3.5 fusion.20
  302.3 2.6 fusion.99
  305.0 1.8 copy-done
  306.8 4.8 fusion.60
  311.7 10.6 all-gather.10.cloned.1.call-done
  322.3 5.7 fusion.52
  328.8 107.1 %all-gather.14.cloned.1.call-done = bf16[1536,8960]{1,0:T(8,128)(2,1)} async-done(((bf16[96,8960]{1,0:T(8,128)(2,1)}), bf16[1536,8960]{1,0:T(8,128)(2,1)}) %all-gather.14.cloned.1.call-update) | async-done | bytes 27525136 | tf_op jit(solution)/shard_map/all_gather | solution.py:100
  435.9 23.8 %fusion.134 = f32[512,8960]{1,0:T(8,128)} fusion(bf16[1536,8960]{1,0:T(8,128)(2,1)} %all-gather.14.cloned.1.call-done, bf16[1,512,1536]{2,1,0:T(8,128)(2,1)S(1)} %get-tuple-element.73, f32[1536]{0:T(1024)S(1)} %convert_element_type.216, f32[512]{0:T(512)S(1)} %fusion.116), kind=kOutput, calls=%fused_computation.176 | convolution fusion | flops 14096007168 | bytes 47456256 | tf_op jit(solution)/shard_map/bsd,df->bsf/dot_general | solution.py:58
  459.8 89.8 %all-gather.16.cloned.1.call-done = bf16[8960,1536]{1,0:T(8,128)(2,1)} async-done(((bf16[560,1536]{1,0:T(8,128)(2,1)}), bf16[8960,1536]{1,0:T(8,128)(2,1)}) %all-gather.16.cloned.1.call-update) | async-done | bytes 27525136 | tf_op jit(solution)/shard_map/all_gather | solution.py:100
  549.6 20.5 %convolution_convert_fusion = bf16[512,8960]{1,0:T(8,128)(2,1)} fusion(bf16[8960,1536]{1,0:T(8,128)(2,1)} %all-gather.16.cloned.1.call-done, bf16[1,512,1536]{2,1,0:T(8,128)(2,1)S(1)} %copy-done.19), kind=kOutput, calls=%fused_computation.20 | convolution fusion | flops 14097448960 | bytes 38273024 | tf_op jit(solution)/shard_map/bsd,fd->bsf/dot_general | solution.py:62
  570.1 93.1 %all-gather.12.cloned.1.call-done = bf16[1536,8960]{1,0:T(8,128)(2,1)} async-done(((bf16[96,8960]{1,0:T(8,128)(2,1)}), bf16[1536,8960]{1,0:T(8,128)(2,1)}) %all-gather.12.cloned.1.call-update) | async-done | bytes 27525136 | tf_op jit(solution)/shard_map/all_gather | solution.py:100
  663.2 38.8 %fusion.9 = (bf16[512,8960]{1,0:T(8,128)(2,1)}, bf16[512,8960]{1,0:T(8,128)(2,1)}, f32[512,8960]{1,0:T(8,128)}) fusion(f32[512,8960]{1,0:T(8,128)} %fusion.134, bf16[512,8960]{1,0:T(8,128)(2,1)} %convolution_convert_fusion, bf16[1536,8960]{1,0:T(8,128)(2,1)} %all-gather.12.cloned.1.call-done, bf16[1,512,1536]{2,1,0:T(8,128)(2,1)S(1)} %get-tuple-element.73, ...), kind=kOutput, calls=%fused_computation.14 | convolution fusion | flops 14164819968 | bytes 93331456 | tf_op jit(solution)/shard_map/bsd,df->bsf/dot_general | solution.py:57
  702.0 22.0 %fusion.147 = f32[512,1536]{1,0:T(8,128)} fusion(bf16[512,8960]{1,0:T(8,128)(2,1)} %get-tuple-element.54, bf16[1536,8960]{1,0:T(8,128)(2,1)} %all-gather.12.cloned.1.call-done), kind=kOutput, calls=%fused_computation.179 | convolution fusion | flops 14092861440 | bytes 39845888 | tf_op jit(solution)/shard_map/bsf,df->bsd/dot_general | solution.py:68
  724.0 25.8 %fusion.40 = (f32[1536]{0:T(1024)}, f32[512]{0:T(512)S(1)}, bf16[512,1536]{1,0:T(8,128)(2,1)}) fusion(bf16[1,512,1536]{2,1,0:T(8,128)(2,1)S(1)} %get-tuple-element.73, f32[512]{0:T(512)S(1)} %fusion.116, f32[1536]{0:T(1024)S(1)} %convert_element_type.216, f32[512,1536]{1,0:T(8,128)} %fusion.147, bf16[1536,8960]{1,0:T(8,128)(2,1)} %all-gather.14.cloned.1.call-done, ...), kind=kOutput, calls=%fused_computation.74 | convolution fusion | flops 14132836352 | bytes 61358080 | tf_op jit(solution)/shard_map/bsf,df->bsd/dot_general | solution.py:68
  749.8 3.0 fusion.46
  753.1 2.7 convolution_convert_fusion.2
  755.8 1.6 copy.72
  757.4 8.8 fusion.96
  766.9 1.9 fusion.138
  769.0 7.8 fusion.19
  777.5 10.5 fusion.93
  788.9 1.9 fusion.109
  790.9 9.6 bitcast_convert_fusion.1
  802.6 5.5 fusion.102
  808.2 6.5 fusion.66
  815.7 1.9 convolution_bitcast_fusion.1
  819.5 5.8 fusion.42
  825.3 2.2 fusion.48
  827.5 30.6 %fusion.130 = f32[1536,8960]{1,0:T(8,128)} fusion(bf16[1,512,1536]{2,1,0:T(8,128)(2,1)} %copy-done.7, f32[1536]{0:T(1024)S(1)} %convert_element_type.216, f32[512]{0:T(512)S(1)} %fusion.116, bf16[512,8960]{1,0:T(8,128)(2,1)} %convolution_convert_fusion, f32[512,8960]{1,0:T(8,128)} %get-tuple-element.74), kind=kOutput, calls=%fused_computation.174 | convolution fusion | flops 14128119808 | bytes 84156416 | tf_op jit(solution)/shard_map/bsd,bsf->df/dot_general | solution.py:67
  858.4 1.2 copy-done.8
  859.6 26.3 %fusion.132 = f32[1536,8960]{1,0:T(8,128)} fusion(bf16[512,8960]{1,0:T(8,128)(2,1)} %get-tuple-element.54, bf16[1,512,1536]{2,1,0:T(8,128)(2,1)S(1)} %copy-done.8, f32[1536]{0:T(1024)S(1)} %convert_element_type.216, f32[512]{0:T(512)S(1)} %fusion.116), kind=kOutput, calls=%fused_computation.175 | convolution fusion | flops 14096007168 | bytes 65806336 | tf_op jit(solution)/shard_map/bsd,bsf->df/dot_general | solution.py:66
  885.9 1.3 copy-done.21
  887.2 26.5 %fusion.69 = f32[8960,1536]{1,0:T(8,128)} fusion(bf16[512,8960]{1,0:T(8,128)(2,1)} %get-tuple-element.55, bf16[1,512,1536]{2,1,0:T(8,128)(2,1)S(1)} %copy-done.21), kind=kOutput, calls=%fused_computation.104 | convolution fusion | flops 14092861440 | bytes 65798144 | tf_op jit(solution)/shard_map/bsf,bsd->fd/dot_general | solution.py:61
  914.6 5.9 sort
  920.5 32.7 %all-reduce.8 = (bf16[1536]{0:T(1024)(128)(2,1)S(1)}, bf16[1536]{0:T(1024)(128)(2,1)S(1)}) all-reduce(f32[1536]{0:T(1024)S(1)} %get-tuple-element.48, f32[1536]{0:T(1024)S(1)} %copy-done.56), channel_id=3, replica_groups=mesh['fsdp'=16] {'fsdp'}, use_global_device_ids=true, to_apply=%region_10.11.clone | all-reduce | flops 3072 | bytes 18432
  954.4 21.7 %fusion.53 = bf16[1,512,1536]{2,1,0:T(8,128)(2,1)} fusion(bf16[1,512,1536]{2,1,0:T(8,128)(2,1)S(1)} %copy-done.8, bf16[512,8960]{1,0:T(8,128)(2,1)} %get-tuple-element.55, bf16[8960,1536]{1,0:T(8,128)(2,1)} %all-gather.16.cloned.1.call-done), kind=kOutput, calls=%fused_computation.87 | convolution fusion | flops 14095220736 | bytes 39845888 | tf_op jit(solution)/shard_map/bsf,fd->bsd/dot_general | solution.py:60
  979.3 1.8 convert_element_type.256
  981.1 59.9 %reduce-scatter.17.cloned.1.call-done = f32[96,1536]{1,0:T(8,128)} async-done(((f32[1536,1536]{1,0:T(8,128)}), f32[96,1536]{1,0:T(8,128)}) %reduce-scatter.17.cloned.1.call-update) | async-done | bytes 589840 | tf_op jit(solution)/shard_map/reduce_scatter | solution.py:102
  1040.9 1.8 convert_element_type.259
  1042.8 104.4 %all-gather.18.cloned.1.call-done = bf16[16,512,1536]{2,1,0:T(8,128)(2,1)} async-done(((bf16[1,512,1536]{2,1,0:T(8,128)(2,1)}), bf16[16,512,1536]{2,1,0:T(8,128)(2,1)}) %all-gather.18.cloned.1.call-update) | async-done | bytes 25165840 | tf_op jit(solution)/shard_map/all_gather | solution.py:103
  1147.1 27.7 %bitcast_convert_fusion = f32[8192,1536]{1,0:T(8,128)} fusion(bf16[16,512,1536]{2,1,0:T(8,128)(2,1)} %all-gather.18.cloned.1.call-done), kind=kLoop, calls=%fused_computation.7 | loop fusion | flops 12582912 | bytes 75497472 | tf_op jit(solution)/shard_map/convert_element_type | solution.py:105
  1174.8 193.4 %scatter_custom_fusion = f32[9496,1536]{1,0:T(8,128)} fusion(s32[8192]{0:T(1024)S(1)} %get-tuple-element.44, f32[8192,1536]{1,0:T(8,128)} %bitcast_convert_fusion, s32[8192]{0:T(1024)S(1)} %broadcast_clamp_fusion, f32[]{:T(128)} %constant.22.clone.1), kind=kCustom, calls=%fused_computation.3 | custom fusion | flops 12582912 | bytes 58343936 | tf_op jit(solution)/shard_map/scatter-add | solution.py:105
  1368.2 28.2 %convert_element_type.251 = bf16[9496,1536]{1,0:T(8,128)(2,1)} convert(f32[9496,1536]{1,0:T(8,128)} %scatter_custom_fusion) | non-fusion elementwise | flops 14585856 | bytes 87515136 | tf_op jit(solution)/shard_map/convert_element_type | solution.py:106
  1396.5 21.5 %reduce-scatter.21.cloned.1.call-done = f32[96,8960]{1,0:T(8,128)} async-done(((f32[1536,8960]{1,0:T(8,128)}), f32[96,8960]{1,0:T(8,128)}) %reduce-scatter.21.cloned.1.call-update) | async-done | bytes 3440656 | tf_op jit(solution)/shard_map/reduce_scatter | solution.py:102
  1418.0 3.3 convert_element_type.261
  1421.3 267.7 %reduce-scatter.19.cloned.1.call-done = f32[96,8960]{1,0:T(8,128)} async-done(((f32[1536,8960]{1,0:T(8,128)}), f32[96,8960]{1,0:T(8,128)}) %reduce-scatter.19.cloned.1.call-update) | async-done | bytes 3440656 | tf_op jit(solution)/shard_map/reduce_scatter | solution.py:102
  1689.0 3.3 convert_element_type.260
  1692.4 267.6 %reduce-scatter.23.cloned.1.call-done = f32[560,1536]{1,0:T(8,128)} async-done(((f32[8960,1536]{1,0:T(8,128)}), f32[560,1536]{1,0:T(8,128)}) %reduce-scatter.23.cloned.1.call-update) | async-done | bytes 3440656 | tf_op jit(solution)/shard_map/reduce_scatter | solution.py:102
  1959.9 3.4 convert_element_type.262
  (187 shorter events, 19.1 us)
Async XLA Ops:
  7.2 237.3 %reduce-scatter.9.cloned.1.call-start = ((), (), s32[]{:S(2)}) async-start(), calls=%async_computation.8 | async-start | bytes 26738688 | tf_op jit(solution)/shard_map/reduce_scatter | solution.py:99
  102.2 3.3 copy-start.58
  102.2 3.6 copy-start.59
  102.2 35.7 %copy-start.40 = (bf16[96,2,128]{2,1,0:T(2,128)(2,1)S(1)}, bf16[96,2,128]{2,1,0:T(2,128)(2,1)}, u32[]{:S(2)}) copy-start(bf16[96,2,128]{2,1,0:T(2,128)(2,1)} %param.18) | copy-start | bytes 147460
  102.2 35.7 %copy-start.41 = (bf16[96,2,128]{2,1,0:T(2,128)(2,1)S(1)}, bf16[96,2,128]{2,1,0:T(2,128)(2,1)}, u32[]{:S(2)}) copy-start(bf16[96,2,128]{2,1,0:T(2,128)(2,1)} %param.19) | copy-start | bytes 147460
  102.2 181.2 %all-gather.8.cloned.1.call-start = ((), (), s32[]{:S(2)}) async-start(), calls=%async_computation.9 | async-start | bytes 5013504 | tf_op jit(solution)/shard_map/all_gather | solution.py:100
  103.0 219.3 %all-gather.10.cloned.1.call-start = ((), (), s32[]{:S(2)}) async-start(), calls=%async_computation.10 | async-start | bytes 5013504 | tf_op jit(solution)/shard_map/all_gather | solution.py:100
  103.7 332.3 %all-gather.14.cloned.1.call-start = ((), (), s32[]{:S(2)}) async-start(), calls=%async_computation.12 | async-start | bytes 29245440 | tf_op jit(solution)/shard_map/all_gather | solution.py:100
  104.3 445.3 %all-gather.16.cloned.1.call-start = ((), (), s32[]{:S(2)}) async-start(), calls=%async_computation.13 | async-start | bytes 29245440 | tf_op jit(solution)/shard_map/all_gather | solution.py:100
  104.9 558.4 %all-gather.12.cloned.1.call-start = ((), (), s32[]{:S(2)}) async-start(), calls=%async_computation.11 | async-start | bytes 29245440 | tf_op jit(solution)/shard_map/all_gather | solution.py:100
  105.4 870.7 %reduce-scatter.15.cloned.1.call-start = ((), (), s32[]{:S(2)}) async-start(), calls=%async_computation.17 | async-start | bytes 1671168 | tf_op jit(solution)/shard_map/reduce_scatter | solution.py:102
  137.9 159.5 %copy-start.42 = (f32[1536]{0:T(1024)}, f32[1536]{0:T(1024)S(1)}, u32[]{:S(2)}) copy-start(f32[1536]{0:T(1024)S(1)} %convert_element_type.207) | copy-start | bytes 18436
  138.1 166.9 %copy-start.9 = (pred[512,512]{0,1:T(8,128)(4,1)}, pred[512,512]{0,1:T(8,128)(4,1)S(1)}, u32[]{:S(2)}) copy-start(pred[512,512]{0,1:T(8,128)(4,1)S(1)} %iota_compare_fusion) | copy-start | bytes 786436
  138.6 150.2 %copy-start.13 = (f32[512,64]{0,1:T(8,128)}, f32[512,64]{0,1:T(8,128)S(1)}, u32[]{:S(2)}) copy-start(f32[512,64]{0,1:T(8,128)S(1)} %get-tuple-element.69) | copy-start | bytes 393220
  138.6 158.6 %copy-start.11 = (f32[512,64]{0,1:T(8,128)}, f32[512,64]{0,1:T(8,128)S(1)}, u32[]{:S(2)}) copy-start(f32[512,64]{0,1:T(8,128)S(1)} %get-tuple-element.68) | copy-start | bytes 393220
  246.2 42.5 %copy-start.49 = (f32[512]{0:T(512)}, f32[512]{0:T(512)S(1)}, u32[]{:S(2)}) copy-start(f32[512]{0:T(512)S(1)} %fusion.49) | copy-start | bytes 6148
  246.2 42.5 %copy-start.51 = (f32[512]{0:T(512)}, f32[512]{0:T(512)S(1)}, u32[]{:S(2)}) copy-start(f32[512]{0:T(512)S(1)} %fusion.115) | copy-start | bytes 6148
  290.5 4.8 copy-start.1
  292.4 6.4 copy-start.3
  295.2 2.0 copy-start.14
  295.2 2.1 copy-start.17
  295.3 2.1 copy-start.52
  297.4 4.9 copy-start.29
  297.4 4.9 copy-start.30
  302.3 4.5 copy-start
  302.3 4.5 copy-start.33
  302.3 4.5 copy-start.61
  306.8 21.2 %copy-start.36 = (f32[2,6,512]{2,1,0:T(8,128)}, f32[2,6,512]{2,1,0:T(8,128)S(1)}, u32[]{:S(2)}) copy-start(f32[2,6,512]{2,1,0:T(8,128)S(1)} %fusion.99) | copy-start | bytes 73732
  328.0 131.7 %copy-start.54 = (f32[512]{0:T(512)}, f32[512]{0:T(512)S(1)}, u32[]{:S(2)}) copy-start(f32[512]{0:T(512)S(1)} %get-tuple-element.72) | copy-start | bytes 6148
  328.0 396.0 %copy-start.7 = (bf16[1,512,1536]{2,1,0:T(8,128)(2,1)}, bf16[1,512,1536]{2,1,0:T(8,128)(2,1)S(1)}, u32[]{:S(2)}) copy-start(bf16[1,512,1536]{2,1,0:T(8,128)(2,1)S(1)} %get-tuple-element.73) | copy-start | bytes 4718596
  435.9 113.6 %copy-start.19 = (bf16[1,512,1536]{2,1,0:T(8,128)(2,1)S(1)}, bf16[1,512,1536]{2,1,0:T(8,128)(2,1)}, u32[]{:S(2)}) copy-start(bf16[1,512,1536]{2,1,0:T(8,128)(2,1)} %param.13) | copy-start | bytes 4718596
  724.0 25.8 %copy-start.55 = (f32[512]{0:T(512)S(1)}, f32[512]{0:T(512)}, u32[]{:S(2)}) copy-start(f32[512]{0:T(512)} %copy-done.54) | copy-start | bytes 6148
  724.0 25.8 %copy-start.20 = (bf16[1,512,1536]{2,1,0:T(8,128)(2,1)S(1)}, bf16[1,512,1536]{2,1,0:T(8,128)(2,1)}, u32[]{:S(2)}) copy-start(bf16[1,512,1536]{2,1,0:T(8,128)(2,1)} %param.13) | copy-start | bytes 4718596
  749.8 3.3 copy-start.57
  755.8 1.6 copy-start.10
  755.8 1.6 copy-start.34
  757.4 9.5 copy-start.2
  757.4 9.5 copy-start.43
  757.4 9.5 copy-start.53
  766.9 2.0 copy-start.47
  768.9 208.9 %reduce-scatter.13.cloned.1.call-start = ((), (), s32[]{:S(2)}) async-start(), calls=%async_computation.16 | async-start | bytes 1671168 | tf_op jit(solution)/shard_map/reduce_scatter | solution.py:102
  768.9 8.5 copy-start.4
  768.9 8.5 copy-start.6
  768.9 8.5 copy-start.35
  769.0 8.5 copy-start.38
  776.7 11.2 copy-start.60
  777.4 10.5 copy-start.12
  777.4 10.5 copy-start.15
  777.5 11.4 copy-start.44
  790.8 188.5 %reduce-scatter.11.cloned.1.call-start = ((), (), s32[]{:S(2)}) async-start(), calls=%async_computation.15 | async-start | bytes 10027008 | tf_op jit(solution)/shard_map/reduce_scatter | solution.py:102
  790.9 9.6 copy-start.16
  800.5 2.1 copy-start.45
  801.0 1.7 copy-start.24
  808.2 232.8 %reduce-scatter.17.cloned.1.call-start = ((), (), s32[]{:S(2)}) async-start(), calls=%async_computation.18 | async-start | bytes 10027008 | tf_op jit(solution)/shard_map/reduce_scatter | solution.py:102
  814.7 332.4 %all-gather.18.cloned.1.call-start = ((), (), s32[]{:S(2)}) async-start(), calls=%async_computation.14 | async-start | bytes 26738688 | tf_op jit(solution)/shard_map/all_gather | solution.py:103
  815.7 1.9 copy-start.18
  815.7 1.9 copy-start.32
  817.6 1.9 copy-start.25
  817.6 1.9 copy-start.46
  819.5 5.8 copy-start.50
  827.5 590.5 %reduce-scatter.21.cloned.1.call-start = ((), (), s32[]{:S(2)}) async-start(), calls=%async_computation.20 | async-start | bytes 58490880 | tf_op jit(solution)/shard_map/reduce_scatter | solution.py:102
  858.2 830.9 %reduce-scatter.19.cloned.1.call-start = ((), (), s32[]{:S(2)}) async-start(), calls=%async_computation.19 | async-start | bytes 58490880 | tf_op jit(solution)/shard_map/reduce_scatter | solution.py:102
  885.9 1074.1 %reduce-scatter.23.cloned.1.call-start = ((), (), s32[]{:S(2)}) async-start(), calls=%async_computation.21 | async-start | bytes 58490880 | tf_op jit(solution)/shard_map/reduce_scatter | solution.py:102
  913.8 6.7 copy-start.56
  (12 other events, 13.0 us)
Sparse Core Ops, SparseCore 0:
  102.3 142.1 reduce-scatter.8
  246.7 36.6 all-gather.7
  285.6 36.6 all-gather.9
  324.4 111.5 all-gather.13
  438.0 111.4 all-gather.15
  551.7 111.4 all-gather.11
  769.0 49.3 reduce-scatter.14
  822.4 49.3 reduce-scatter.12
  876.5 80.4 reduce-scatter.10
  961.5 79.3 reduce-scatter.16
  1043.8 103.3 all-gather.17
  1152.3 265.7 reduce-scatter.20
  1423.3 265.7 reduce-scatter.18
  1694.2 265.7 reduce-scatter.22
where the time goes:
time: 1980 us; the launch traced here: 1970 us
  waiting for transfers between devices  1140 us (58%)
  matrix products  322 us (16%)
  other arithmetic  302 us (15%)
  blocking collectives  111 us (6%)
  local copies, waits for them, and re-layouts  82.6 us (4%)
    reduce_scatter x7, waiting for transfers between devices, device_step(): lax.psum_scatter(part_grad, AXIS_NAME, scatter_dimension=0, tiled=True)  617 us
    all_gather x5, waiting for transfers between devices, device_step(): lax.all_gather(w_shard, AXIS_NAME, axis=0, tiled=True)  338 us
    scatter-add x3, other arithmetic, device_step(): jax.ops.segment_sum(d_emb_all.reshape(-1, d_emb_all.shape[-1]).astype(jnp...  199 us
    all_gather x1, waiting for transfers between devices, device_step(): d_emb_all = lax.all_gather(d_emb, AXIS_NAME, axis=0, tiled=True)  104 us
    reduce_scatter x1, waiting for transfers between devices, device_step(): lax.psum_scatter(part_emb, AXIS_NAME, scatter_dimension=0, tiled=True)  73.9 us
    unnamed x2, blocking collectives  64.6 us
    gather x1, local copies, waits for them, and re-layouts, device_step(): picked = jnp.take(table, jnp.where(owned, rel_ids, 0), axis=0)  62.3 us
  transfers between devices with their start and end apart: 14, of which 11 were waited for; matrix products, arithmetic and copies ran while one was open for 26% of the time, Pallas kernels for 0%

commit v1 on v0

v1 whole, which is shorter than its diff:
```python
import jax
import jax.numpy as jnp
from jax import lax
from jax.experimental import pallas as pl
from jax.experimental.pallas import tpu as pltpu
from jax.sharding import PartitionSpec as P


ALL = ("z", "y", "x", "c")
PLANE = ("z", "y")
N_DEV = 16
NORM_EPS = 1e-5
ROPE_THETA = 500000.0
SLOTS = 48
ROW_BLOCK = 128
F32 = jnp.float32
BF16 = jnp.bfloat16


def rms_norm(x_f32, gain_f32):
    inv_rms = lax.rsqrt(jnp.mean(x_f32 * x_f32, axis=-1, keepdims=True) + NORM_EPS)
    return (x_f32 * inv_rms * gain_f32).astype(BF16)


def rotary(x_f32):
    head_dim = x_f32.shape[-1]
    half_dim = head_dim // 2
    seq_len = x_f32.shape[-3]
    inv_freq = ROPE_THETA ** (-2.0 * jnp.arange(half_dim, dtype=F32) / head_dim)
    angles = jnp.arange(seq_len, dtype=F32)[:, None] * inv_freq[None, :]
    cos_tab = jnp.cos(angles)[:, None, :]
    sin_tab = jnp.sin(angles)[:, None, :]
    lo_half = x_f32[..., :half_dim]
    hi_half = x_f32[..., half_dim:]
    return jnp.concatenate([lo_half * cos_tab - hi_half * sin_tab, hi_half * cos_tab + lo_half * sin_tab], axis=-1)


def attend(q_f32, k_f32, v_bf16):
    batch_loc, seq_len, q_heads, head_dim = q_f32.shape
    kv_heads = k_f32.shape[2]
    q_rot = rotary(q_f32).astype(BF16).reshape(batch_loc, seq_len, kv_heads, q_heads // kv_heads, head_dim)
    k_rot = rotary(k_f32).astype(BF16)
    scores = jnp.einsum("bqkgd,bskd->bkgqs", q_rot, k_rot, preferred_element_type=F32) * head_dim ** -0.5
    positions = jnp.arange(seq_len)
    causal = positions[:, None] >= positions[None, :]
    scores = jnp.where(causal, scores, -1e30)
    prob_bf = jax.nn.softmax(scores, axis=-1).astype(BF16)
    attn_out = jnp.einsum("bkgqs,bskd->bqkgd", prob_bf, v_bf16, preferred_element_type=F32)
    return attn_out.astype(BF16).reshape(batch_loc, seq_len, q_heads * head_dim)


def gated(gate_f32, up_f32):
    return (jax.nn.silu(gate_f32) * up_f32).astype(BF16)


def dot(a, b, ca, cb):
    return lax.dot_general(a, b, (((ca,), (cb,)), ((), ())), preferred_element_type=F32)


def flip(a, axis):
    return lax.ppermute(a, axis, [(0, 1), (1, 0)])


def row_sum_kernel(start_ref, slot_ref, row_ref, recv_ref, out_ref, acc):
    blk = pl.program_id(0)
    acc[...] = jnp.zeros_like(acc)

    def add_row(i, carry):
        r = row_ref[i] - blk * ROW_BLOCK
        acc[pl.ds(r, 1), :] += recv_ref[pl.ds(slot_ref[i], 1), :]
        return carry

    lax.fori_loop(start_ref[blk], start_ref[blk + 1], add_row, 0)
    out_ref[...] = acc[...].astype(BF16)


def row_sums(starts, slots, rows, recv, rows_dev):
    width = recv.shape[1]
    n_blk = pl.cdiv(rows_dev, ROW_BLOCK)
    return pl.pallas_call(
        row_sum_kernel,
        out_shape=jax.ShapeDtypeStruct((rows_dev, width), BF16),
        grid_spec=pltpu.PrefetchScalarGridSpec(
            num_scalar_prefetch=3,
            grid=(n_blk,),
            in_specs=[pl.BlockSpec(recv.shape, lambda i, *_: (0, 0))],
            out_specs=pl.BlockSpec((ROW_BLOCK, width), lambda i, *_: (i, 0)),
            scratch_shapes=[pltpu.VMEM((ROW_BLOCK, width), F32)],
        ),
        compiler_params=pltpu.CompilerParams(dimension_semantics=("arbitrary",)),
        cost_estimate=pl.CostEstimate(flops=40_000_000_000, bytes_accessed=40_000_000, transcendentals=0),
    )(starts, slots, rows, recv)


def place_xc(pieces, x_i, c_i, shape, at):
    buf = jnp.zeros(shape, pieces[0].dtype)
    for k, piece in enumerate(pieces):
        px = x_i if k < 2 else 1 - x_i
        pc = c_i if k % 2 == 0 else 1 - c_i
        buf = lax.dynamic_update_slice(buf, piece, at(px, pc))
    return buf


def gather_xc(w):
    wx = flip(w, "x")
    return [w, flip(w, "c"), wx, flip(wx, "c")]


def solution(mesh):
    mesh = jax.sharding.Mesh(mesh.devices.reshape(2, 2, 2, 2), ALL)
    spec_1d = P(ALL)
    spec_2d = P(ALL, None)
    spec_3d = P(ALL, None, None)
    in_specs = (spec_2d, spec_3d, spec_2d, spec_1d, spec_1d, spec_3d, spec_3d, spec_3d, spec_2d, spec_2d, spec_2d, spec_2d)
    out_specs = (spec_3d, spec_2d, spec_1d, spec_1d, spec_3d, spec_3d, spec_3d, spec_2d, spec_2d, spec_2d, spec_2d)

    def step(token_ids, grad_y, table, gain1, gain2, w_query, w_key, w_value, w_out, w_gate, w_up, w_down):
        seq = token_ids.shape[1]
        rows_dev, dim = table.shape
        shard = w_gate.shape[0]
        ffn = w_gate.shape[1]
        ffn_q = ffn // 4
        q_w = w_query.shape[1] * w_query.shape[2]
        kv_w = w_key.shape[1] * w_key.shape[2]
        qkv_w = q_w + 2 * kv_w
        me = lax.axis_index(ALL)
        x_i, c_i = lax.axis_index("x"), lax.axis_index("c")

        small = jnp.concatenate([token_ids.astype(F32), gain1.astype(F32)[None], gain2.astype(F32)[None]], axis=1)
        small = lax.all_gather(small, ALL, axis=0, tiled=True)
        ids_all = small[:, :seq].astype(jnp.int32)
        g1_full = small[:, seq : seq + shard].reshape(-1)
        g2_full = small[:, seq + shard :].reshape(-1)

        owner = ids_all // rows_dev
        pos = jnp.arange(seq)
        before = pos[None, :] < pos[:, None]
        same = ids_all[:, :, None] == ids_all[:, None, :]
        first = jnp.logical_not(jnp.any(same & before[None], axis=2))
        mine = first & (owner == me)
        owner_is = (owner[:, :, None] == jnp.arange(N_DEV)) & first[:, :, None]
        overflow = jnp.max(jnp.sum(owner_is.astype(jnp.int32), axis=1)) > SLOTS
        rank = jnp.einsum("bt,st->bs", mine.astype(BF16), before.astype(BF16), preferred_element_type=F32).astype(jnp.int32)
        in_slot = mine[:, None, :] & (rank[:, None, :] == jnp.arange(SLOTS)[None, :, None])
        rel = ids_all - me * rows_dev
        slot_row = jnp.sum(jnp.where(in_slot, rel[:, None, :], 0), axis=2)
        slot_used = jnp.any(in_slot, axis=2)
        ids_me = token_ids[0]
        own_me = ids_me // rows_dev
        same_me = ids_me[:, None] == ids_me[None, :]
        first_me = jnp.logical_not(jnp.any(same_me & before, axis=1))
        rank_me = jnp.sum(((own_me[:, None] == own_me[None, :]) & before & first_me[None, :]).astype(jnp.int32), axis=1)
        slot_first = own_me * SLOTS + rank_me
        slot_tok = jnp.sum(jnp.where(same_me & first_me[None, :], slot_first[None, :], 0), axis=1)
        pick = (slot_tok[:, None] == jnp.arange(N_DEV * SLOTS)[None, :]).astype(BF16)

        sent = jnp.take(table, slot_row.reshape(-1), axis=0).reshape(N_DEV, SLOTS, dim)
        got = lax.all_to_all(sent, ALL, 0, 0, tiled=True)
        emb_fast = dot(pick, got.reshape(-1, dim), 1, 0).astype(BF16)

        def emb_dense():
            owned = owner == me
            picked = jnp.take(table, jnp.where(owned, rel, 0), axis=0)
            part = lax.all_to_all(jnp.where(owned[:, :, None], picked, jnp.zeros((), BF16)), ALL, 0, 0, tiled=True)
            return jnp.sum(part.astype(F32), axis=0).astype(BF16)

        emb = lax.cond(overflow, emb_dense, lambda: emb_fast)

        attn_w = jnp.concatenate([w_query.reshape(shard, -1), w_key.reshape(shard, -1), w_value.reshape(shard, -1), w_out], axis=1)
        attn_w = lax.all_gather(attn_w, ALL, axis=0, tiled=True)
        w_qkv, w_o = attn_w[:, :qkv_w], attn_w[:, qkv_w:]
        dy = grad_y[0]
        dy_all = lax.all_gather(dy, PLANE, axis=0, tiled=True)
        cols = jnp.stack([w_gate, w_up]).reshape(2, shard, 4, ffn_q).transpose(2, 0, 1, 3)
        cols = lax.all_to_all(cols, PLANE, 0, 0, tiled=True)
        wide = []
        for k in range(2):
            pieces = [p[:, None] for p in gather_xc(cols[:, k])]
            buf = place_xc([p[:, :, None] for p in pieces], x_i, c_i, (4, 2, 2, shard, ffn_q), lambda px, pc: (0, px, pc, 0, 0))
            wide.append(buf.reshape(dim, ffn_q))
        w_g, w_u = wide
        w_d = place_xc([p[None, None] for p in gather_xc(w_down)], x_i, c_i, (2, 2) + w_down.shape, lambda px, pc: (px, pc, 0, 0)).reshape(ffn_q, dim)

        x_f32 = emb.astype(F32)
        h_one, norm1_pull = jax.vjp(rms_norm, x_f32, g1_full)
        qkv = dot(h_one, w_qkv, 1, 0)
        q_f32 = qkv[:, :q_w].reshape(1, seq, -1, 128)
        k_f32 = qkv[:, q_w : q_w + kv_w].reshape(1, seq, -1, 128)
        v_bf16 = qkv[:, q_w + kv_w :].astype(BF16).reshape(1, seq, -1, 128)
        attn_out, attn_pull = jax.vjp(attend, q_f32, k_f32, v_bf16)
        o_bf = attn_out[0]
        resid_bf = (x_f32 + dot(o_bf, w_o, 1, 0)).astype(BF16)
        resid_two = resid_bf.astype(F32)
        h_two, norm2_pull = jax.vjp(rms_norm, resid_two, g2_full)

        h_all = lax.all_gather(h_two, PLANE, axis=0, tiled=True)
        d_act = dot(dy_all, w_d, 1, 1).astype(BF16)
        gate_f32 = dot(h_all, w_g, 1, 0)
        up_f32 = dot(h_all, w_u, 1, 0)
        act, act_pull = jax.vjp(gated, gate_f32, up_f32)
        d_gate, d_up = act_pull(d_act)
        d_gate, d_up = d_gate.astype(BF16), d_up.astype(BF16)
        d_h_part = dot(d_gate, w_g, 1, 1) + dot(d_up, w_u, 1, 1)
        d_h_two = lax.psum_scatter(d_h_part, PLANE, scatter_dimension=0, tiled=True).astype(BF16)
        y_part = dot(act, w_d, 1, 0)
        y_sum = lax.psum_scatter(y_part, PLANE, scatter_dimension=0, tiled=True)
        y_sum, resid_y = lax.optimization_barrier((y_sum, resid_bf))
        layer_out = (resid_y.astype(F32) + y_sum).astype(BF16)

        def reduce_xc(part, c_dim, x_dim):
            keep = lax.dynamic_index_in_dim(part, c_i, c_dim, keepdims=False)
            give = lax.dynamic_index_in_dim(part, 1 - c_i, c_dim, keepdims=False)
            got_c = flip(give, "c")
            half = keep + got_c
            keep = lax.dynamic_index_in_dim(half, x_i, x_dim, keepdims=False)
            give = lax.dynamic_index_in_dim(half, 1 - x_i, x_dim, keepdims=False)
            got_x = flip(give, "x")
            return (keep + got_x).astype(BF16)

        g_gate = dot(h_all, d_gate, 0, 0)
        g_up = dot(h_all, d_up, 0, 0)
        g_down = dot(act, dy_all, 0, 0)
        g_gate = reduce_xc(g_gate.reshape(4, 2, 2, shard, ffn_q), 2, 1)
        g_up = reduce_xc(g_up.reshape(4, 2, 2, shard, ffn_q), 2, 1)
        g_down = reduce_xc(g_down.reshape(2, 2, ffn // N_DEV, dim), 1, 0)
        back = lax.all_to_all(jnp.stack([g_gate, g_up], axis=1), PLANE, 0, 0, tiled=True)
        back = back.transpose(1, 2, 0, 3).reshape(2, shard, ffn)

        d_resid_two, g_norm2 = norm2_pull(d_h_two)
        d_resid = (dy.astype(F32) + d_resid_two).astype(BF16)
        g_out = dot(o_bf, d_resid, 0, 0)
        g_out = lax.psum_scatter(g_out, ALL, scatter_dimension=0, tiled=True).astype(BF16)
        d_attn = dot(d_resid, w_o, 1, 1).astype(BF16)
        d_query, d_key, d_value = attn_pull(d_attn[None])
        d_qkv = jnp.concatenate([d_query.astype(BF16).reshape(seq, -1), d_key.astype(BF16).reshape(seq, -1), d_value.reshape(seq, -1)], axis=1)
        g_qkv = dot(h_one, d_qkv, 0, 0)
        g_qkv = lax.psum_scatter(g_qkv, ALL, scatter_dimension=0, tiled=True).astype(BF16)
        d_h_one = dot(d_qkv, w_qkv, 1, 1).astype(BF16)
        d_x, g_norm1 = norm1_pull(d_h_one)
        d_emb = (d_resid.astype(F32) + d_x).astype(BF16)

        d_slot = dot(pick, d_emb, 0, 0).reshape(N_DEV, SLOTS, dim)
        extra = jnp.broadcast_to(jnp.concatenate([g_norm1[None], g_norm2[None], jnp.zeros((6, dim), F32)])[None], (N_DEV, 8, dim))
        d_got = lax.all_to_all(jnp.concatenate([d_slot, extra], axis=1), ALL, 0, 0, tiled=True)
        gains = lax.dynamic_slice_in_dim(jnp.sum(d_got[:, SLOTS : SLOTS + 2], axis=0), me * shard, shard, axis=1).astype(BF16)
        stride = SLOTS + 8
        n_slot = N_DEV * stride
        key = jnp.pad(jnp.where(slot_used, slot_row, rows_dev), ((0, 0), (0, 8)), constant_values=rows_dev).reshape(-1)
        key_sorted, order = lax.sort((key, jnp.arange(n_slot, dtype=jnp.int32)), num_keys=1)
        edges = jnp.minimum(jnp.arange(pl.cdiv(rows_dev, ROW_BLOCK) + 1) * ROW_BLOCK, rows_dev)
        starts = jnp.sum((key[None, :] < edges[:, None]).astype(jnp.int32), axis=1)

        def rows_dense():
            d_all = lax.all_to_all(jnp.broadcast_to(d_emb[None], (N_DEV, seq, dim)), ALL, 0, 0, tiled=True).reshape(-1, dim)
            seg = jnp.where(owner == me, rel, rows_dev).reshape(-1)
            return jax.ops.segment_sum(d_all.astype(F32), seg, num_segments=rows_dev).astype(BF16)

        d_rows = lax.cond(overflow, rows_dense, lambda: row_sums(starts, order, key_sorted, d_got.reshape(-1, dim), rows_dev))
        g_q = g_qkv[:, :q_w].reshape(w_query.shape)
        g_k = g_qkv[:, q_w : q_w + kv_w].reshape(w_key.shape)
        g_v = g_qkv[:, q_w + kv_w :].reshape(w_value.shape)
        return layer_out[None], d_rows, gains[0], gains[1], g_q, g_k, g_v, g_out, back[0], back[1], g_down


    return jax.shard_map(step, mesh=mesh, in_specs=in_specs, out_specs=out_specs, check_vma=False)
```

time: 1980 us -> 1020 us (0.52)
  waiting for transfers between devices: 1140 us -> 387 us
  other arithmetic: 302 us -> 83.3 us
  blocking collectives: 111 us -> 14.7 us
  local copies, waits for them, and re-layouts: 82.6 us -> 155 us
  matrix products: 322 us -> 280 us
  Pallas kernels: 0 us -> 37 us
  starting transfers between devices: 1.14 us -> 36.5 us
    reduce_scatter x8 -> x4, waiting for transfers between devices: 691 us -> 42.2 us  [the longest x1 42.2 us: step(): lax.psum_scatter(d_h_part, PLANE, scatter_dimension=0, tiled=True)]
    all_gather x6 -> x3, waiting for transfers between devices: 442 us -> 0.55 us  [the longest x1 0.54 us: step(): h_all = lax.all_gather(h_two, PLANE, axis=0, tiled=True)]
    ppermute x0 -> x15, waiting for transfers between devices: none -> 227 us  [flip(): return lax.ppermute(a, axis, [(0, 1), (1, 0)])]
    scatter-add x3 -> x0, other arithmetic: 199 us -> none  [device_step(): jax.ops.segment_sum(d_emb_all.reshape(-1, d_emb_all.shape[-1]).astype(jnp...]
    all_to_all x0 -> x4, waiting for transfers between devices: none -> 116 us  [the longest x1 38.7 us: step(): lax.all_to_all(jnp.stack([g_gate, g_up], axis=1), PLANE, 0, 0, tiled=True)]
    convert_element_type x13 -> x10, other arithmetic: 76.6 us -> 11.7 us  [the longest x1 4.69 us: reduce_xc(): return (keep + got_x).astype(BF16)]
    unnamed x2 -> x0, blocking collectives: 64.6 us -> none
    gather x1, local copies, waits for them, and re-layouts: 62.3 us -> 18.2 us  [step(): jnp.take(table, slot_row.reshape(-1), axis=0).reshape(N_DEV, SLOTS, dim)]
  transfers between devices with their start and end apart: 14 -> 26, of which waited for: 11 -> 11; matrix products, arithmetic and copies ran while one was open for 26% -> 39% of each run, Pallas kernels for 0% -> 4%
where the time goes in v1:
time: 1020 us; the launch traced here: 1010 us
  waiting for transfers between devices  387 us (38%)
  matrix products  280 us (27%)
  local copies, waits for them, and re-layouts  155 us (15%)
  other arithmetic  83.3 us (8%)
  Pallas kernels  37 us (4%)
  starting transfers between devices  36.5 us (4%)
  between operations  16.4 us (2%)
  blocking collectives  14.7 us (1%)
    dot_general x17, matrix products, dot(): lax.dot_general(a, b, (((ca,), (cb,)), ((), ())), preferred_element_type=...  236 us
    ppermute x15, waiting for transfers between devices, flip(): return lax.ppermute(a, axis, [(0, 1), (1, 0)])  227 us
    reduce_scatter x1, waiting for transfers between devices, step(): lax.psum_scatter(d_h_part, PLANE, scatter_dimension=0, tiled=True)  42.2 us
    all_to_all x1, waiting for transfers between devices, step(): lax.all_to_all(jnp.stack([g_gate, g_up], axis=1), PLANE, 0, 0, tiled=True)  38.7 us
    pallas_call x1, Pallas kernels, row_sums(): pl.pallas_call(row_sum_kernel, out_shape=jax.ShapeDtypeStruct((rows_dev,...  37 us
    all_to_all x1, waiting for transfers between devices, step(): lax.all_to_all(jnp.concatenate([d_slot, extra], axis=1), ALL, 0, 0, tiled...  36.7 us
    dynamic_update_slice x12, local copies, waits for them, and re-layouts, place_xc(): buf = lax.dynamic_update_slice(buf, piece, at(px, pc))  31.4 us
    all_to_all x1, waiting for transfers between devices, step(): cols = lax.all_to_all(cols, PLANE, 0, 0, tiled=True)  28.2 us
  transfers between devices with their start and end apart: 26, of which 11 were waited for; matrix products, arithmetic and copies ran while one was open for 39% of the time, Pallas kernels for 4%

profile of v1, /device:TPU:0, one launch (start us, length us, event | category | flops | bytes accessed | tf_op | source)
XLA Modules:
  0.0 1011.3 jit_solution(17107768854532262368)
XLA Ops:
  12.4 14.7 %all-gather.1 = f32[16,1,704]{2,1,0:T(1,128)S(1)} all-gather(f32[1,1,704]{2,1,0:T(1,128)S(1)} %maximum_bitcast_fusion.4), channel_id=1, replica_groups=mesh['z'=2,'y'=2,'x'=2,'c'=2] {'z','y','x','c'}, dimensions={0}, use_global_device_ids=true | all-gather | bytes 47872 | tf_op jit(solution)/shard_map/all_gather | solution.py:130
  27.3 4.2 and_reduce_fusion
  32.4 18.2 %gather_fusion.1 = bf16[768,1536]{1,0:T(8,128)(2,1)S(1)} fusion(bf16[9496,1536]{1,0:T(8,128)(2,1)} %param.18, s32[1024]{0:T(1024)S(1)} %pad_clamp_fusion), kind=kCustom, calls=%fused_computation.1 | custom fusion | bytes 4721664 | tf_op jit(solution)/shard_map/jit(_take)/gather | solution.py:157
  52.3 13.2 %all-to-all-start.2 = ((bf16[16,48,1536]{2,1,0:T(8,128)(2,1)}), bf16[16,48,1536]{2,1,0:T(8,128)(2,1)}, u32[]{:S(2)}, u32[]{:S(2)}) async-start(bf16[16,48,1536]{2,1,0:T(8,128)(2,1)} %broadcast_select_fusion), calls=%async_computation.2 | async-start | bytes 4718592 | tf_op jit(solution)/shard_map/all_to_all | solution.py:158
  69.1 3.5 stack.18
  72.6 4.6 stack.19
  77.2 4.1 maximum_bitcast_fusion
  84.0 12.7 %all-to-all-done.2 = bf16[16,48,1536]{2,1,0:T(8,128)(2,1)} async-done(((bf16[16,48,1536]{2,1,0:T(8,128)(2,1)}), bf16[16,48,1536]{2,1,0:T(8,128)(2,1)}, u32[]{:S(2)}, u32[]{:S(2)}) %all-to-all-start.2) | async-done | bytes 2359328 | tf_op jit(solution)/shard_map/all_to_all | solution.py:158
  99.9 5.3 conditional.2
  105.2 5.1 all-to-all-start.3
  115.6 3.4 broadcast_in_dim.195
  122.0 12.9 %collective-permute-done.7 = bf16[560,1536]{1,0:T(8,128)(2,1)} collective-permute-done((bf16[560,1536]{1,0:T(8,128)(2,1)}, bf16[560,1536]{1,0:T(8,128)(2,1)}, u32[]{:S(2)}, u32[]{:S(2)}) %collective-permute-start.7) | collective-permute-done | bytes 1720352 | tf_op jit(solution)/shard_map/ppermute | solution.py:61
  140.6 28.2 %all-to-all-done.3 = bf16[4,2,96,2240]{3,2,1,0:T(8,128)(2,1)} async-done(((bf16[4,2,96,2240]{3,2,1,0:T(8,128)(2,1)}), bf16[4,2,96,2240]{3,2,1,0:T(8,128)(2,1)}, u32[]{:S(2)}, u32[]{:S(2)}) %all-to-all-start.3) | async-done | bytes 3440672 | tf_op jit(solution)/shard_map/all_to_all | solution.py:175
  168.7 4.5 slice_bitcast_fusion.1
  175.5 5.6 fusion.31
  199.6 3.4 fusion.21
  207.5 3.8 fusion.75
  211.4 5.9 fusion.59
  220.3 3.5 broadcast.241.clone
  226.9 3.7 broadcast.241.clone.1
  236.5 14.3 %collective-permute-done.4 = bf16[4,96,2240]{2,1,0:T(8,128)(2,1)} collective-permute-done((bf16[4,96,2240]{2,1,0:T(8,128)(2,1)}, bf16[4,96,2240]{2,1,0:T(8,128)(2,1)}, u32[]{:S(2)}, u32[]{:S(2)}) %collective-permute-start.4) | collective-permute-done | bytes 1720352 | tf_op jit(solution)/shard_map/ppermute | solution.py:61
  265.0 20.1 %convolution_convert_fusion = bf16[2240,2048]{1,0:T(8,128)(2,1)} fusion(bf16[2240,1536]{1,0:T(8,128)(2,1)} %bitcast.51, bf16[1,2048,1536]{2,1,0:T(8,128)(2,1)} %all-gather.10.cloned.1.call-done), kind=kOutput, calls=%fused_computation.43 | convolution fusion | flops 14097448960 | bytes 22347776 | tf_op jit(solution)/shard_map/dot_general | solution.py:57
  285.6 20.8 %fusion.139 = f32[2048,2240]{0,1:T(8,128)} fusion(bf16[2048,1536]{1,0:T(8,128)(2,1)} %all-gather.8.cloned.1.call-done, bf16[1536,2240]{1,0:T(8,128)(2,1)} %bitcast.46), kind=kOutput, calls=%fused_computation.244 | convolution fusion | flops 14092861440 | bytes 31522816 | tf_op jit(solution)/shard_map/dot_general | solution.py:57
  306.4 34.4 %fusion.9 = (bf16[2048,2240]{0,1:T(8,128)(2,1)}, bf16[2048,2240]{0,1:T(8,128)(2,1)}, bf16[2048,2240]{0,1:T(8,128)(2,1)}) fusion(f32[2048,2240]{0,1:T(8,128)} %fusion.139, bf16[2240,2048]{1,0:T(8,128)(2,1)} %convolution_convert_fusion, bf16[2048,1536]{1,0:T(8,128)(2,1)} %all-gather.8.cloned.1.call-done, bf16[1536,2240]{1,0:T(8,128)(2,1)} %bitcast.36), kind=kOutput, calls=%fused_computation.21 | convolution fusion | flops 14170849280 | bytes 68222976 | tf_op jit(solution)/shard_map/dot_general | solution.py:57
  340.8 21.0 %fusion.141 = f32[2048,1536]{1,0:T(8,128)S(1)} fusion(bf16[2048,2240]{0,1:T(8,128)(2,1)} %get-tuple-element.167, bf16[1536,2240]{1,0:T(8,128)(2,1)} %bitcast.46), kind=kOutput, calls=%fused_computation.246 | convolution fusion | flops 14092861440 | bytes 28639232 | tf_op jit(solution)/shard_map/dot_general | solution.py:57
  361.8 21.2 %convolution_add_fusion = f32[2048,1536]{1,0:T(8,128)} fusion(f32[2048,1536]{1,0:T(8,128)S(1)} %fusion.141, bf16[2048,2240]{0,1:T(8,128)(2,1)} %get-tuple-element.165, bf16[1536,2240]{1,0:T(8,128)(2,1)} %bitcast.36), kind=kOutput, calls=%fused_computation.45 | convolution fusion | flops 14096007168 | bytes 41222144 | tf_op jit(solution)/shard_map/dot_general | solution.py:57
  383.1 21.0 %fusion.140 = f32[2048,1536]{1,0:T(8,128)} fusion(bf16[2048,2240]{0,1:T(8,128)(2,1)} %get-tuple-element.166, bf16[2240,1536]{1,0:T(8,128)(2,1)} %bitcast.51), kind=kOutput, calls=%fused_computation.245 | convolution fusion | flops 14092861440 | bytes 28639232 | tf_op jit(solution)/shard_map/dot_general | solution.py:57
  405.5 19.1 %fusion.22 = f32[2240,1536]{1,0:T(8,128)S(1)} fusion(bf16[2048,2240]{0,1:T(8,128)(2,1)} %get-tuple-element.166, bf16[1,2048,1536]{2,1,0:T(8,128)(2,1)} %all-gather.10.cloned.1.call-done), kind=kOutput, calls=%fused_computation.52 | convolution fusion | flops 14092861440 | bytes 29229056 | tf_op jit(solution)/shard_map/dot_general | solution.py:57
  424.6 3.7 dynamic-slice_bitcast_fusion.2
  428.3 3.7 copy-done.8
  432.0 17.4 %fusion.144 = f32[1536,2240]{1,0:T(8,128)S(1)} fusion(bf16[2048,1536]{1,0:T(8,128)(2,1)S(1)} %bitcast.376, bf16[2048,2240]{0,1:T(8,128)(2,1)} %get-tuple-element.167), kind=kOutput, calls=%fused_computation.249 | convolution fusion | flops 14092861440 | bytes 29229056 | tf_op jit(solution)/shard_map/dot_general | solution.py:57
  449.5 3.5 dynamic-slice_bitcast_fusion
  453.0 4.0 copy-done.6
  457.9 42.2 %reduce-scatter.7.cloned.1.call-done = f32[512,1536]{1,0:T(8,128)} async-done(((f32[2048,1536]{1,0:T(8,128)}), f32[512,1536]{1,0:T(8,128)}) %reduce-scatter.7.cloned.1.call-update) | async-done | bytes 3145744 | tf_op jit(solution)/shard_map/reduce_scatter | solution.py:204
  500.1 3.6 fusion.60
  505.8 5.5 fusion.142
  511.4 19.3 %fusion.143 = f32[1536,2240]{1,0:T(8,128)S(1)} fusion(bf16[2048,1536]{1,0:T(8,128)(2,1)} %all-gather.8.cloned.1.call-done, bf16[2048,2240]{0,1:T(8,128)(2,1)} %get-tuple-element.165), kind=kOutput, calls=%fused_computation.248 | convolution fusion | flops 14092861440 | bytes 29229056 | tf_op jit(solution)/shard_map/dot_general | solution.py:57
  534.0 4.7 copy-done.7
  538.8 5.0 fusion.64
  544.6 7.7 fusion.20
  552.4 11.4 %fusion.102 = f32[1,512,2,128]{3,1,2,0:T(8,128)S(1)} fusion(bf16[2,6,512,512]{2,3,1,0:T(8,128)(2,1)S(1)} %get-tuple-element.198, f32[2,6,512]{2,1,0:T(8,128)S(1)} %neg.18, f32[2,6,512]{2,1,0:T(8,128)S(1)} %copy-done.47, pred[512,512]{0,1:T(8,128)(4,1)S(1)} %copy-done.25, f32[2,512,512,6]{2,1,3,0:T(8,128)} %copy-done.2, f32[2,6,512]{2,1,0:T(8,128)S(1)} %copy-done.44, ...), kind=kOutput, calls=%fused_computation.155 | convolution fusion | flops 837025792 | bytes 21307392 | tf_op jit(solution)/shard_map/transpose(jvp(bqkgd,bskd->bkgqs))/dot_general | solution.py:43
  564.9 9.9 bitcast_convert_fusion.1
  575.5 7.3 fusion.90
  582.9 8.0 fusion.106
  590.9 6.5 bitcast_add_fusion
  601.0 6.5 bitcast_add_fusion.1
  610.2 9.5 bitcast_add_fusion.2
  619.6 3.9 dynamic-slice_bitcast_fusion.5
  625.0 71.1 %collective-permute-done.12 = f32[4,96,2240]{2,1,0:T(8,128)} collective-permute-done((f32[4,96,2240]{2,1,0:T(8,128)}, f32[4,96,2240]{2,1,0:T(8,128)}, u32[]{:S(2)}, u32[]{:S(2)}) %collective-permute-start.12) | collective-permute-done | bytes 3440672 | tf_op jit(solution)/shard_map/ppermute | solution.py:61
  698.4 96.0 %collective-permute-done.10 = f32[4,96,2240]{2,1,0:T(8,128)} collective-permute-done((f32[4,96,2240]{2,1,0:T(8,128)}, f32[4,96,2240]{2,1,0:T(8,128)}, u32[]{:S(2)}, u32[]{:S(2)}) %collective-permute-start.10) | collective-permute-done | bytes 3440672 | tf_op jit(solution)/shard_map/ppermute | solution.py:61
  799.2 5.3 all-to-all-start.5
  804.5 7.4 fusion.52
  817.6 38.7 %all-to-all-done.5 = bf16[4,2,96,2240]{3,2,1,0:T(8,128)(2,1)} async-done(((bf16[4,2,96,2240]{3,2,1,0:T(8,128)(2,1)}), bf16[4,2,96,2240]{3,2,1,0:T(8,128)(2,1)}, u32[]{:S(2)}, u32[]{:S(2)}) %all-to-all-start.5) | async-done | bytes 3440672 | tf_op jit(solution)/shard_map/all_to_all | solution.py:226
  856.3 4.0 all-to-all-start.4
  860.8 3.8 sort.15
  864.7 32.9 %collective-permute-done.14 = f32[560,1536]{1,0:T(8,128)} collective-permute-done((f32[560,1536]{1,0:T(8,128)}, f32[560,1536]{1,0:T(8,128)}, u32[]{:S(2)}, u32[]{:S(2)}) %collective-permute-start.14) | collective-permute-done | bytes 3440672 | tf_op jit(solution)/shard_map/ppermute | solution.py:61
  897.6 4.7 fusion.47
  902.3 3.4 fusion.135
  909.7 4.2 copy.225
  913.9 4.2 squeeze.75
  918.2 3.5 fusion.78
  921.7 36.7 %all-to-all-done.4 = f32[16,56,1536]{2,1,0:T(8,128)} async-done(((f32[16,56,1536]{2,1,0:T(8,128)}), f32[16,56,1536]{2,1,0:T(8,128)}, u32[]{:S(2)}, u32[]{:S(2)}) %all-to-all-start.4) | async-done | bytes 5505056 | tf_op jit(solution)/shard_map/all_to_all | solution.py:244
  958.4 38.9 %conditional.3 = (bf16[9496,1536]{1,0:T(8,128)(2,1)}) conditional(s32[]{:T(128)} %convert_element_type.223, (s32[76,896]{1,0:T(8,128)S(1)}, f32[16,56,1536]{2,1,0:T(8,128)}, s32[896]{0:T(1024)S(1)}, s32[896]{0:T(1024)S(1)}) %tuple.34, (s32[]{:T(128)}, s32[16,512]{1,0:T(8,128)S(1)}, s32[16,512]{1,0:T(8,128)S(1)}, ...), branch_computations={%region_24.26_spmd, %region_26.28_spmd} | conditional | flops 40000069632 | bytes 323985952 | solution.py:258
  959.1 37.0 %branch_0_fun.1 = bf16[9496,1536]{1,0:T(8,128)(2,1)} custom-call(s32[76]{0:T(128)} %reduce_sum.112.start_ref, s32[896]{0:T(1024)S(1)} %get-tuple-element.44.slot_ref, s32[896]{0:T(1024)S(1)} %get-tuple-element.45.row_ref, f32[896,1536]{1,0:T(8,128)} %bitcast.1.recv_ref), custom_call_target="tpu_custom_call" | custom-call | flops 40000000000 | bytes 40000000 | tf_op jit(solution)/shard_map/cond/branch_0_fun/pallas_call | solution.py:80
  (309 shorter events, 130.2 us)
Async XLA Ops:
  7.2 168.3 %all-gather.6.cloned.1.call-start = ((), (), s32[]{:S(2)}) async-start(), calls=%async_computation.10 | async-start | bytes 11698176 | tf_op jit(solution)/shard_map/all_gather | solution.py:170
  31.5 19.1 %copy-start.55 = (pred[16,512]{1,0:T(8,128)(4,1)}, pred[16,512]{1,0:T(8,128)(4,1)S(1)}, u32[]{:S(2)}) copy-start(pred[16,512]{1,0:T(8,128)(4,1)S(1)} %get-tuple-element.163) | copy-start | bytes 24580
  31.5 68.3 %copy-start.38 = (s32[16,512]{1,0:T(8,128)}, s32[16,512]{1,0:T(8,128)S(1)}, u32[]{:S(2)}) copy-start(s32[16,512]{1,0:T(8,128)S(1)} %get-tuple-element.164) | copy-start | bytes 98308
  31.8 18.8 %copy-start.50 = (s32[16,512]{1,0:T(8,128)}, s32[16,512]{1,0:T(8,128)S(1)}, u32[]{:S(2)}) copy-start(s32[16,512]{1,0:T(8,128)S(1)} %convolution_convert_fusion.3) | copy-start | bytes 98308
  31.8 68.0 %copy-start.36 = (s32[16,512]{1,0:T(8,128)}, s32[16,512]{1,0:T(8,128)S(1)}, u32[]{:S(2)}) copy-start(s32[16,512]{1,0:T(8,128)S(1)} %broadcast_subtract_fusion) | copy-start | bytes 98308
  32.3 18.3 %copy-start.48 = (s32[16,48]{1,0:T(8,128)}, s32[16,48]{1,0:T(8,128)S(1)}, u32[]{:S(2)}) copy-start(s32[16,48]{1,0:T(8,128)S(1)} %select_reduce_fusion) | copy-start | bytes 9220
  50.6 16.5 %copy-start.54 = (s32[1,512]{1,0:T(1,128)S(1)}, s32[1,512]{1,0:T(1,128)}, u32[]{:S(2)}) copy-start(s32[1,512]{1,0:T(1,128)} %param.16) | copy-start | bytes 6148
  52.3 44.4 %all-to-all-start.2 = ((bf16[16,48,1536]{2,1,0:T(8,128)(2,1)}), bf16[16,48,1536]{2,1,0:T(8,128)(2,1)}, u32[]{:S(2)}, u32[]{:S(2)}) async-start(bf16[16,48,1536]{2,1,0:T(8,128)(2,1)} %broadcast_select_fusion), calls=%async_computation.2 | async-start | bytes 4718592 | tf_op jit(solution)/shard_map/all_to_all | solution.py:158
  65.6 69.4 %collective-permute-start.7 = (bf16[560,1536]{1,0:T(8,128)(2,1)}, bf16[560,1536]{1,0:T(8,128)(2,1)}, u32[]{:S(2)}, u32[]{:S(2)}) collective-permute-start(bf16[560,1536]{1,0:T(8,128)(2,1)} %param.27), channel_id=1, source_target_pairs={{0,2},{2,0},{1,3},{3,1},{4,6},{6,4},{5,7},{7,5},{8,10},{10,8},{9,1... | collective-permute-start | bytes 5160968 | tf_op jit(solution)/shard_map/ppermute | solution.py:61
  67.1 67.9 %collective-permute-start.6 = (bf16[560,1536]{1,0:T(8,128)(2,1)}, bf16[560,1536]{1,0:T(8,128)(2,1)}, u32[]{:S(2)}, u32[]{:S(2)}) collective-permute-start(bf16[560,1536]{1,0:T(8,128)(2,1)} %param.27), channel_id=1, source_target_pairs={{0,1},{1,0},{2,3},{3,2},{4,5},{5,4},{6,7},{7,6},{8,9},{9,8},{10,11... | collective-permute-start | bytes 5160968 | tf_op jit(solution)/shard_map/ppermute | solution.py:61
  84.0 15.8 %copy-start.69 = (s32[512]{0:T(512)}, s32[512]{0:T(512)S(1)}, u32[]{:S(2)}) copy-start(s32[512]{0:T(512)S(1)} %select_reduce_fusion.1) | copy-start | bytes 6148
  105.2 35.4 %copy-start.63 = (f32[512]{0:T(512)}, f32[512]{0:T(512)S(1)}, u32[]{:S(2)}) copy-start(f32[512]{0:T(512)S(1)} %get-tuple-element.69) | copy-start | bytes 6148
  105.2 70.3 %copy-start.9 = (f32[512,1536]{1,0:T(8,128)}, f32[512,1536]{1,0:T(8,128)S(1)}, u32[]{:S(2)}) copy-start(f32[512,1536]{1,0:T(8,128)S(1)} %get-tuple-element.68) | copy-start | bytes 9437188
  105.2 63.5 %all-to-all-start.3 = ((bf16[4,2,96,2240]{3,2,1,0:T(8,128)(2,1)}), bf16[4,2,96,2240]{3,2,1,0:T(8,128)(2,1)}, u32[]{:S(2)}, u32[]{:S(2)}) async-start(bf16[4,2,96,2240]{3,2,1,0:T(8,128)(2,1)} %copy.206), calls=%async_computation.3 | async-start | bytes 7077888 | tf_op jit(solution)/shard_map/all_to_all | solution.py:175
  110.3 154.7 %all-gather.10.cloned.1.call-start = ((), (), s32[]{:S(2)}) async-start(), calls=%async_computation.16 | async-start | bytes 7864320 | tf_op jit(solution)/shard_map/all_gather | solution.py:173
  111.0 174.6 %all-gather.8.cloned.1.call-start = ((), (), s32[]{:S(2)}) async-start(), calls=%async_computation.11 | async-start | bytes 7864320 | tf_op jit(solution)/shard_map/all_gather | solution.py:196
  111.2 106.1 %copy-start.52 = (f32[1536]{0:T(1024)}, f32[1536]{0:T(1024)S(1)}, u32[]{:S(2)}) copy-start(f32[1536]{0:T(1024)S(1)} %mul.492) | copy-start | bytes 18436
  111.3 64.1 %copy-start.59 = (f32[1536]{0:T(1024)}, f32[1536]{0:T(1024)S(1)}, u32[]{:S(2)}) copy-start(f32[1536]{0:T(1024)S(1)} %mul.468) | copy-start | bytes 18436
  115.6 90.2 %copy-start.24 = (pred[512,512]{0,1:T(8,128)(4,1)}, pred[512,512]{0,1:T(8,128)(4,1)S(1)}, u32[]{:S(2)}) copy-start(pred[512,512]{0,1:T(8,128)(4,1)S(1)} %iota_compare_fusion.4) | copy-start | bytes 786436
  135.0 98.4 %collective-permute-start.8 = (bf16[560,1536]{1,0:T(8,128)(2,1)}, bf16[560,1536]{1,0:T(8,128)(2,1)}, u32[]{:S(2)}, u32[]{:S(2)}) collective-permute-start(bf16[560,1536]{1,0:T(8,128)(2,1)} %collective-permute-done.7), channel_id=1, source_target_pairs={{0,1},{1,0},{2,3},{3,2},{4,5},{5,4},{6,7},{7,6},{8,9},{9,8},{10,11... | collective-permute-start | bytes 5160968 | tf_op jit(solution)/shard_map/ppermute | solution.py:61
  140.6 40.5 %copy-start.67 = (f32[512]{0:T(512)}, f32[512]{0:T(512)S(1)}, u32[]{:S(2)}) copy-start(f32[512]{0:T(512)S(1)} %fusion.121) | copy-start | bytes 6148
  173.2 63.0 %collective-permute-start.1 = (bf16[4,96,2240]{2,1,0:T(8,128)(2,1)}, bf16[4,96,2240]{2,1,0:T(8,128)(2,1)}, u32[]{:S(2)}, u32[]{:S(2)}) collective-permute-start(bf16[4,96,2240]{2,1,0:T(8,128)(2,1)} %get-tuple-element.170), channel_id=1, source_target_pairs={{0,2},{2,0},{1,3},{3,1},{4,6},{6,4},{5,7},{7,5},{8,10},{10,8},{9,1... | collective-permute-start | bytes 5160968 | tf_op jit(solution)/shard_map/ppermute | solution.py:61
  173.8 82.8 %collective-permute-start = (bf16[4,96,2240]{2,1,0:T(8,128)(2,1)}, bf16[4,96,2240]{2,1,0:T(8,128)(2,1)}, u32[]{:S(2)}, u32[]{:S(2)}) collective-permute-start(bf16[4,96,2240]{2,1,0:T(8,128)(2,1)} %get-tuple-element.170), channel_id=1, source_target_pairs={{0,1},{1,0},{2,3},{3,2},{4,5},{5,4},{6,7},{7,6},{8,9},{9,8},{10,11... | collective-permute-start | bytes 5160968 | tf_op jit(solution)/shard_map/ppermute | solution.py:61
  173.8 77.1 %collective-permute-start.4 = (bf16[4,96,2240]{2,1,0:T(8,128)(2,1)}, bf16[4,96,2240]{2,1,0:T(8,128)(2,1)}, u32[]{:S(2)}, u32[]{:S(2)}) collective-permute-start(bf16[4,96,2240]{2,1,0:T(8,128)(2,1)} %get-tuple-element.171), channel_id=1, source_target_pairs={{0,2},{2,0},{1,3},{3,1},{4,6},{6,4},{5,7},{7,5},{8,10},{10,8},{9,1... | collective-permute-start | bytes 5160968 | tf_op jit(solution)/shard_map/ppermute | solution.py:61
  175.2 75.6 %collective-permute-start.3 = (bf16[4,96,2240]{2,1,0:T(8,128)(2,1)}, bf16[4,96,2240]{2,1,0:T(8,128)(2,1)}, u32[]{:S(2)}, u32[]{:S(2)}) collective-permute-start(bf16[4,96,2240]{2,1,0:T(8,128)(2,1)} %get-tuple-element.171), channel_id=1, source_target_pairs={{0,1},{1,0},{2,3},{3,2},{4,5},{5,4},{6,7},{7,6},{8,9},{9,8},{10,11... | collective-permute-start | bytes 5160968 | tf_op jit(solution)/shard_map/ppermute | solution.py:61
  193.5 9.5 copy-start.14
  220.1 280.0 %reduce-scatter.7.cloned.1.call-start = ((), (), s32[]{:S(2)}) async-start(), calls=%async_computation.13 | async-start | bytes 15728640 | tf_op jit(solution)/shard_map/reduce_scatter | solution.py:204
  236.2 27.4 %collective-permute-start.2 = (bf16[4,96,2240]{2,1,0:T(8,128)(2,1)}, bf16[4,96,2240]{2,1,0:T(8,128)(2,1)S(1)}, u32[]{:S(2)}, u32[]{:S(2)}) collective-permute-start(bf16[4,96,2240]{2,1,0:T(8,128)(2,1)} %collective-permute-done.1), channel_id=1, source_target_pairs={{0,1},{1,0},{2,3},{3,2},{4,5},{5,4},{6,7},{7,6},{8,9},{9,8},{10,11... | collective-permute-start | bytes 5160968 | tf_op jit(solution)/shard_map/ppermute | solution.py:61
  250.8 11.4 %collective-permute-start.5 = (bf16[4,96,2240]{2,1,0:T(8,128)(2,1)}, bf16[4,96,2240]{2,1,0:T(8,128)(2,1)S(1)}, u32[]{:S(2)}, u32[]{:S(2)}) collective-permute-start(bf16[4,96,2240]{2,1,0:T(8,128)(2,1)} %collective-permute-done.4), channel_id=1, source_target_pairs={{0,1},{1,0},{2,3},{3,2},{4,5},{5,4},{6,7},{7,6},{8,9},{9,8},{10,11... | collective-permute-start | bytes 5160968 | tf_op jit(solution)/shard_map/ppermute | solution.py:61
  383.0 535.1 %reduce-scatter.5.cloned.1.call-start = ((), (), s32[]{:S(2)}) async-start(), calls=%async_computation.12 | async-start | bytes 15728640 | tf_op jit(solution)/shard_map/reduce_scatter | solution.py:206
  404.1 27.9 %slice-start = ((s8[6291456]{0:T(1024)(128)(4,1)}), s8[2097152]{0:T(1024)(128)(4,1)S(1)}, s32[]{:S(2)}) async-start(s8[6291456]{0:T(1024)(128)(4,1)} %bitcast.375), calls=%async_computation.17 | async-start | bytes 4194304
  404.1 595.0 %reduce-scatter.11.cloned.1.call-start = ((), (), s32[]{:S(2)}) async-start(), calls=%async_computation.15 | async-start | bytes 10027008 | tf_op jit(solution)/shard_map/reduce_scatter | solution.py:232
  405.5 26.5 %slice-start.1 = ((s8[6291456]{0:T(1024)(128)(4,1)}), s8[4194304]{0:T(1024)(128)(4,1)S(1)}, s32[]{:S(2)}) async-start(s8[6291456]{0:T(1024)(128)(4,1)} %bitcast.375), calls=%async_computation.18 | async-start | bytes 8388608
  432.0 178.1 %collective-permute-start.13 = (f32[2,560,1536]{2,1,0:T(8,128)}, f32[2,560,1536]{2,1,0:T(8,128)}, u32[]{:S(2)}, u32[]{:S(2)}) collective-permute-start(f32[2,560,1536]{2,1,0:T(8,128)} %dynamic-slice_bitcast_fusion.2), channel_id=1, source_target_pairs={{0,1},{1,0},{2,3},{3,2},{4,5},{5,4},{6,7},{7,6},{8,9},{9,8},{10,11... | collective-permute-start | bytes 20643848 | tf_op jit(solution)/shard_map/ppermute | solution.py:61
  449.5 50.6 %copy-start.4 = (bf16[512,1536]{1,0:T(8,128)(2,1)S(1)}, bf16[512,1536]{1,0:T(8,128)(2,1)}, u32[]{:S(2)}) copy-start(bf16[512,1536]{1,0:T(8,128)(2,1)} %copy-done.3) | copy-start | bytes 4718596
  449.5 50.6 %copy-start.53 = (f32[1536]{0:T(1024)S(1)}, f32[1536]{0:T(1024)}, u32[]{:S(2)}) copy-start(f32[1536]{0:T(1024)} %copy-done.52) | copy-start | bytes 18436
  449.5 50.6 %copy-start.62 = (f32[512]{0:T(512)S(1)}, f32[512]{0:T(512)}, u32[]{:S(2)}) copy-start(f32[512]{0:T(512)} %copy-done.61) | copy-start | bytes 6148
  457.0 46.7 %copy-start.66 = (f32[512]{0:T(512)S(1)}, f32[512]{0:T(512)}, u32[]{:S(2)}) copy-start(f32[512]{0:T(512)} %copy-done.65) | copy-start | bytes 6148
  457.0 46.7 %copy-start.20 = (bf16[1,512,1536]{2,1,0:T(8,128)(2,1)S(1)}, bf16[1,512,1536]{2,1,0:T(8,128)(2,1)}, u32[]{:S(2)}) copy-start(bf16[1,512,1536]{2,1,0:T(8,128)(2,1)} %param.17) | copy-start | bytes 4718596
  457.0 133.9 %collective-permute-start.11 = (f32[4,2,96,2240]{3,2,1,0:T(8,128)}, f32[4,2,96,2240]{3,2,1,0:T(8,128)}, u32[]{:S(2)}, u32[]{:S(2)}) collective-permute-start(f32[4,2,96,2240]{3,2,1,0:T(8,128)} %dynamic-slice_bitcast_fusion), channel_id=1, source_target_pairs={{0,1},{1,0},{2,3},{3,2},{4,5},{5,4},{6,7},{7,6},{8,9},{9,8},{10,11... | collective-permute-start | bytes 20643848 | tf_op jit(solution)/shard_map/ppermute | solution.py:61
  511.4 489.6 %reduce-scatter.9.cloned.1.call-start = ((), (), s32[]{:S(2)}) async-start(), calls=%async_computation.14 | async-start | bytes 13369344 | tf_op jit(solution)/shard_map/reduce_scatter | solution.py:237
  530.7 8.1 copy-start.7
  530.7 8.1 copy-start.22
  538.7 62.3 %collective-permute-start.9 = (f32[4,2,96,2240]{3,2,1,0:T(8,128)}, f32[4,2,96,2240]{3,2,1,0:T(8,128)}, u32[]{:S(2)}, u32[]{:S(2)}) collective-permute-start(f32[4,2,96,2240]{3,2,1,0:T(8,128)} %dynamic-slice_bitcast_fusion.1), channel_id=1, source_target_pairs={{0,1},{1,0},{2,3},{3,2},{4,5},{5,4},{6,7},{7,6},{8,9},{9,8},{10,11... | collective-permute-start | bytes 20643848 | tf_op jit(solution)/shard_map/ppermute | solution.py:61
  544.6 7.8 copy-start.15
  552.3 11.5 %copy-start.74 = (bf16[2,6,512,512]{2,3,1,0:T(8,128)(2,1)}, bf16[2,6,512,512]{2,3,1,0:T(8,128)(2,1)S(1)}, u32[]{:S(2)}) copy-start(bf16[2,6,512,512]{2,3,1,0:T(8,128)(2,1)S(1)} %get-tuple-element.198) | copy-start | bytes 18874372
  552.3 11.5 %copy-start.27 = (f32[512,64]{1,0:T(8,128)S(1)}, f32[512,64]{1,0:T(8,128)}, u32[]{:S(2)}) copy-start(f32[512,64]{1,0:T(8,128)} %copy-done.26) | copy-start | bytes 393220
  552.4 11.5 %copy-start.28 = (f32[512,64]{1,0:T(8,128)S(1)}, f32[512,64]{1,0:T(8,128)}, u32[]{:S(2)}) copy-start(f32[512,64]{1,0:T(8,128)} %get-tuple-element.192) | copy-start | bytes 393220
  564.9 18.0 %copy-start.41 = (bf16[1,512,2,128]{1,3,2,0:T(8,128)(2,1)}, bf16[1,512,2,128]{1,3,2,0:T(8,128)(2,1)S(1)}, u32[]{:S(2)}) copy-start(bf16[1,512,2,128]{1,3,2,0:T(8,128)(2,1)S(1)} %copy.220) | copy-start | bytes 786436
  564.9 9.9 copy-start.30
  564.9 9.9 copy-start.31
  582.8 8.1 copy-start.73
  599.5 96.6 %collective-permute-start.12 = (f32[4,96,2240]{2,1,0:T(8,128)}, f32[4,96,2240]{2,1,0:T(8,128)}, u32[]{:S(2)}, u32[]{:S(2)}) collective-permute-start(f32[4,96,2240]{2,1,0:T(8,128)} %dynamic-slice_bitcast_fusion.3), channel_id=1, source_target_pairs={{0,2},{2,0},{1,3},{3,1},{4,6},{6,4},{5,7},{7,5},{8,10},{10,8},{9,1... | collective-permute-start | bytes 10321928 | tf_op jit(solution)/shard_map/ppermute | solution.py:61
  609.5 184.9 %collective-permute-start.10 = (f32[4,96,2240]{2,1,0:T(8,128)}, f32[4,96,2240]{2,1,0:T(8,128)}, u32[]{:S(2)}, u32[]{:S(2)}) collective-permute-start(f32[4,96,2240]{2,1,0:T(8,128)} %dynamic-slice_bitcast_fusion.4), channel_id=1, source_target_pairs={{0,2},{2,0},{1,3},{3,1},{4,6},{6,4},{5,7},{7,5},{8,10},{10,8},{9,1... | collective-permute-start | bytes 10321928 | tf_op jit(solution)/shard_map/ppermute | solution.py:61
  623.5 274.1 %collective-permute-start.14 = (f32[560,1536]{1,0:T(8,128)}, f32[560,1536]{1,0:T(8,128)}, u32[]{:S(2)}, u32[]{:S(2)}) collective-permute-start(f32[560,1536]{1,0:T(8,128)} %dynamic-slice_bitcast_fusion.5), channel_id=1, source_target_pairs={{0,2},{2,0},{1,3},{3,1},{4,6},{6,4},{5,7},{7,5},{8,10},{10,8},{9,1... | collective-permute-start | bytes 10321928 | tf_op jit(solution)/shard_map/ppermute | solution.py:61
  799.2 57.1 %all-to-all-start.5 = ((bf16[4,2,96,2240]{3,2,1,0:T(8,128)(2,1)}), bf16[4,2,96,2240]{3,2,1,0:T(8,128)(2,1)}, u32[]{:S(2)}, u32[]{:S(2)}) async-start(bf16[4,2,96,2240]{3,2,1,0:T(8,128)(2,1)} %copy.224), calls=%async_computation.9 | async-start | bytes 7077888 | tf_op jit(solution)/shard_map/all_to_all | solution.py:226
  817.6 42.7 %copy-start.51 = (s32[16,512]{1,0:T(8,128)S(1)}, s32[16,512]{1,0:T(8,128)}, u32[]{:S(2)}) copy-start(s32[16,512]{1,0:T(8,128)} %copy-done.50) | copy-start | bytes 98308
  817.6 42.7 %copy-start.56 = (pred[16,512]{1,0:T(8,128)(4,1)S(1)}, pred[16,512]{1,0:T(8,128)(4,1)}, u32[]{:S(2)}) copy-start(pred[16,512]{1,0:T(8,128)(4,1)} %copy-done.55) | copy-start | bytes 24580
  817.6 43.1 %copy-start.49 = (s32[16,48]{1,0:T(8,128)S(1)}, s32[16,48]{1,0:T(8,128)}, u32[]{:S(2)}) copy-start(s32[16,48]{1,0:T(8,128)} %copy-done.48) | copy-start | bytes 9220
  856.3 102.1 %all-to-all-start.4 = ((f32[16,56,1536]{2,1,0:T(8,128)}), f32[16,56,1536]{2,1,0:T(8,128)}, u32[]{:S(2)}, u32[]{:S(2)}) async-start(f32[16,56,1536]{2,1,0:T(8,128)} %pad_maximum_fusion), calls=%async_computation.6 | async-start | bytes 11010048 | tf_op jit(solution)/shard_map/all_to_all | solution.py:244
  909.7 8.4 copy-start.5
  913.9 44.5 %copy-start.19 = (bf16[512,1536]{1,0:T(8,128)(2,1)S(1)}, bf16[512,1536]{1,0:T(8,128)(2,1)}, u32[]{:S(2)}) copy-start(bf16[512,1536]{1,0:T(8,128)(2,1)} %copy-done.18) | copy-start | bytes 4718596
  913.9 44.5 %copy-start.37 = (s32[16,512]{1,0:T(8,128)S(1)}, s32[16,512]{1,0:T(8,128)}, u32[]{:S(2)}) copy-start(s32[16,512]{1,0:T(8,128)} %copy-done.36) | copy-start | bytes 98308
  913.9 44.5 %copy-start.39 = (s32[16,512]{1,0:T(8,128)S(1)}, s32[16,512]{1,0:T(8,128)}, u32[]{:S(2)}) copy-start(s32[16,512]{1,0:T(8,128)} %copy-done.38) | copy-start | bytes 98308
  (39 other events, 189.8 us)
Sparse Core Ops, SparseCore 0:
  11.0 67.6 all-gather.5
  112.9 94.8 all-gather.9
  220.2 65.3 all-gather.7
  383.2 116.8 reduce-scatter.6
  503.0 116.8 reduce-scatter.4
  624.4 109.7 reduce-scatter.10
  738.8 145.4 reduce-scatter.8

commit v2 on v1

--- a/solution.py
+++ b/solution.py
@@ -12,6 +12,7 @@
 NORM_EPS = 1e-5
 ROPE_THETA = 500000.0
 SLOTS = 48
+USABLE = SLOTS - 2
 ROW_BLOCK = 128
 F32 = jnp.float32
 BF16 = jnp.bfloat16
@@ -101,11 +102,6 @@
     return buf
 
 
-def gather_xc(w):
-    wx = flip(w, "x")
-    return [w, flip(w, "c"), wx, flip(wx, "c")]
-
-
 def solution(mesh):
     mesh = jax.sharding.Mesh(mesh.devices.reshape(2, 2, 2, 2), ALL)
     spec_1d = P(ALL)
@@ -139,12 +135,14 @@
         first = jnp.logical_not(jnp.any(same & before[None], axis=2))
         mine = first & (owner == me)
         owner_is = (owner[:, :, None] == jnp.arange(N_DEV)) & first[:, :, None]
-        overflow = jnp.max(jnp.sum(owner_is.astype(jnp.int32), axis=1)) > SLOTS
+        overflow = jnp.max(jnp.sum(owner_is.astype(jnp.int32), axis=1)) > USABLE
         rank = jnp.einsum("bt,st->bs", mine.astype(BF16), before.astype(BF16), preferred_element_type=F32).astype(jnp.int32)
         in_slot = mine[:, None, :] & (rank[:, None, :] == jnp.arange(SLOTS)[None, :, None])
         rel = ids_all - me * rows_dev
         slot_row = jnp.sum(jnp.where(in_slot, rel[:, None, :], 0), axis=2)
         slot_used = jnp.any(in_slot, axis=2)
+        spread = (jnp.arange(N_DEV * SLOTS).reshape(N_DEV, SLOTS) * 12) % rows_dev
+        fetch_row = jnp.where(slot_used, slot_row, spread)
         ids_me = token_ids[0]
         own_me = ids_me // rows_dev
         same_me = ids_me[:, None] == ids_me[None, :]
@@ -154,15 +152,19 @@
         slot_tok = jnp.sum(jnp.where(same_me & first_me[None, :], slot_first[None, :], 0), axis=1)
         pick = (slot_tok[:, None] == jnp.arange(N_DEV * SLOTS)[None, :]).astype(BF16)
 
-        sent = jnp.take(table, slot_row.reshape(-1), axis=0).reshape(N_DEV, SLOTS, dim)
+        sent = table.at[fetch_row.reshape(-1)].get(mode="promise_in_bounds").reshape(N_DEV, SLOTS, dim)
         got = lax.all_to_all(sent, ALL, 0, 0, tiled=True)
         emb_fast = dot(pick, got.reshape(-1, dim), 1, 0).astype(BF16)
 
         def emb_dense():
             owned = owner == me
             picked = jnp.take(table, jnp.where(owned, rel, 0), axis=0)
-            part = lax.all_to_all(jnp.where(owned[:, :, None], picked, jnp.zeros((), BF16)), ALL, 0, 0, tiled=True)
-            return jnp.sum(part.astype(F32), axis=0).astype(BF16)
+            part = jnp.where(owned[:, :, None], picked, jnp.zeros((), BF16))
+            total = lax.dynamic_index_in_dim(part, me, 0, keepdims=False)
+            for k in range(1, N_DEV):
+                out = lax.dynamic_index_in_dim(part, (me + k) % N_DEV, 0, keepdims=False)
+                total += lax.ppermute(out, ALL, [(d, (d + k) % N_DEV) for d in range(N_DEV)])
+            return total
 
         emb = lax.cond(overflow, emb_dense, lambda: emb_fast)
 
@@ -171,15 +173,20 @@
         w_qkv, w_o = attn_w[:, :qkv_w], attn_w[:, qkv_w:]
         dy = grad_y[0]
         dy_all = lax.all_gather(dy, PLANE, axis=0, tiled=True)
-        cols = jnp.stack([w_gate, w_up]).reshape(2, shard, 4, ffn_q).transpose(2, 0, 1, 3)
-        cols = lax.all_to_all(cols, PLANE, 0, 0, tiled=True)
-        wide = []
-        for k in range(2):
-            pieces = [p[:, None] for p in gather_xc(cols[:, k])]
-            buf = place_xc([p[:, :, None] for p in pieces], x_i, c_i, (4, 2, 2, shard, ffn_q), lambda px, pc: (0, px, pc, 0, 0))
-            wide.append(buf.reshape(dim, ffn_q))
-        w_g, w_u = wide
+
+        def gather_xc(w):
+            wx = flip(w, "x")
+            return [w, flip(w, "c"), wx, flip(wx, "c")]
+
+        def wide(w):
+            cols = jnp.stack([w[:, k * ffn_q : (k + 1) * ffn_q] for k in range(4)])
+            cols = lax.all_to_all(cols, PLANE, 0, 0, tiled=True)
+            pieces = [p[:, None, None] for p in gather_xc(cols)]
+            return place_xc(pieces, x_i, c_i, (4, 2, 2, shard, ffn_q), lambda px, pc: (0, px, pc, 0, 0)).reshape(dim, ffn_q)
+
         w_d = place_xc([p[None, None] for p in gather_xc(w_down)], x_i, c_i, (2, 2) + w_down.shape, lambda px, pc: (px, pc, 0, 0)).reshape(ffn_q, dim)
+        w_g = wide(w_gate)
+        w_u = wide(w_up)
 
         x_f32 = emb.astype(F32)
         h_one, norm1_pull = jax.vjp(rms_norm, x_f32, g1_full)
@@ -240,19 +247,21 @@
         d_emb = (d_resid.astype(F32) + d_x).astype(BF16)
 
         d_slot = dot(pick, d_emb, 0, 0).reshape(N_DEV, SLOTS, dim)
-        extra = jnp.broadcast_to(jnp.concatenate([g_norm1[None], g_norm2[None], jnp.zeros((6, dim), F32)])[None], (N_DEV, 8, dim))
-        d_got = lax.all_to_all(jnp.concatenate([d_slot, extra], axis=1), ALL, 0, 0, tiled=True)
-        gains = lax.dynamic_slice_in_dim(jnp.sum(d_got[:, SLOTS : SLOTS + 2], axis=0), me * shard, shard, axis=1).astype(BF16)
-        stride = SLOTS + 8
-        n_slot = N_DEV * stride
-        key = jnp.pad(jnp.where(slot_used, slot_row, rows_dev), ((0, 0), (0, 8)), constant_values=rows_dev).reshape(-1)
+        place = jnp.arange(SLOTS)[None, :, None]
+        d_slot = jnp.where(place == USABLE, g_norm1, jnp.where(place == USABLE + 1, g_norm2, d_slot))
+        d_got = lax.all_to_all(d_slot, ALL, 0, 0, tiled=True)
+        gains = lax.dynamic_slice_in_dim(jnp.sum(d_got[:, USABLE:], axis=0), me * shard, shard, axis=1).astype(BF16)
+        n_slot = N_DEV * SLOTS
+        key = jnp.where(slot_used, slot_row, rows_dev).reshape(-1)
         key_sorted, order = lax.sort((key, jnp.arange(n_slot, dtype=jnp.int32)), num_keys=1)
         edges = jnp.minimum(jnp.arange(pl.cdiv(rows_dev, ROW_BLOCK) + 1) * ROW_BLOCK, rows_dev)
         starts = jnp.sum((key[None, :] < edges[:, None]).astype(jnp.int32), axis=1)
 
         def rows_dense():
-            d_all = lax.all_to_all(jnp.broadcast_to(d_emb[None], (N_DEV, seq, dim)), ALL, 0, 0, tiled=True).reshape(-1, dim)
-            seg = jnp.where(owner == me, rel, rows_dev).reshape(-1)
+            d_all = [d_emb] + [lax.ppermute(d_emb, ALL, [(d, (d + k) % N_DEV) for d in range(N_DEV)]) for k in range(1, N_DEV)]
+            d_all = jnp.concatenate(d_all, axis=0)
+            origin = (me - jnp.arange(N_DEV)) % N_DEV
+            seg = jnp.where(owner == me, rel, rows_dev)[origin].reshape(-1)
             return jax.ops.segment_sum(d_all.astype(F32), seg, num_segments=rows_dev).astype(BF16)
 
         d_rows = lax.cond(overflow, rows_dense, lambda: row_sums(starts, order, key_sorted, d_got.reshape(-1, dim), rows_dev))

time: 1020 us -> 1010 us (level)
  blocking collectives: 14.7 us -> 34.5 us
  local copies, waits for them, and re-layouts: 155 us -> 144 us
  waiting for transfers between devices: 387 us -> 376 us
    all_to_all x2 -> x3, waiting for transfers between devices: 64.9 us -> 40.9 us  [the longest x1 26.9 us: step(): d_got = lax.all_to_all(d_slot, ALL, 0, 0, tiled=True)]
    all_gather x1, blocking collectives: 14.7 us -> 34.5 us  [step(): small = lax.all_gather(small, ALL, axis=0, tiled=True)]
    all_to_all x1, waiting for transfers between devices: 12.7 us -> 28.9 us  [step(): got = lax.all_to_all(sent, ALL, 0, 0, tiled=True)]
    all_to_all x1, starting transfers between devices: 13.2 us -> 2.5 us  [step(): got = lax.all_to_all(sent, ALL, 0, 0, tiled=True)]
    unnamed x156 -> x166, local copies, waits for them, and re-layouts: 19.5 us -> 22.4 us
  transfers between devices with their start and end apart: 26 -> 27, of which waited for: 11 -> 9; matrix products, arithmetic and copies ran while one was open for 39% -> 37% of each run, Pallas kernels for 4% -> 4%
where the time goes in v2:
time: 1010 us; the launch traced here: 1000 us
  waiting for transfers between devices  376 us (37%)
  matrix products  274 us (27%)
  local copies, waits for them, and re-layouts  144 us (14%)
  other arithmetic  80 us (8%)
  starting transfers between devices  37.6 us (4%)
  Pallas kernels  36.7 us (4%)
  blocking collectives  34.5 us (3%)
  between operations  16.6 us (2%)
    dot_general x17, matrix products, dot(): lax.dot_general(a, b, (((ca,), (cb,)), ((), ())), preferred_element_type=...  234 us
    ppermute x15, waiting for transfers between devices, flip(): return lax.ppermute(a, axis, [(0, 1), (1, 0)])  221 us
    reduce_scatter x1, waiting for transfers between devices, step(): lax.psum_scatter(d_h_part, PLANE, scatter_dimension=0, tiled=True)  43.8 us
    all_to_all x1, waiting for transfers between devices, step(): lax.all_to_all(jnp.stack([g_gate, g_up], axis=1), PLANE, 0, 0, tiled=True)  40.1 us
    pallas_call x1, Pallas kernels, row_sums(): pl.pallas_call(row_sum_kernel, out_shape=jax.ShapeDtypeStruct((rows_dev,...  36.7 us
    all_gather x1, blocking collectives, step(): small = lax.all_gather(small, ALL, axis=0, tiled=True)  34.5 us
    all_to_all x1, waiting for transfers between devices, step(): got = lax.all_to_all(sent, ALL, 0, 0, tiled=True)  28.9 us
    all_to_all x1, waiting for transfers between devices, step(): d_got = lax.all_to_all(d_slot, ALL, 0, 0, tiled=True)  26.9 us
  transfers between devices with their start and end apart: 27, of which 9 were waited for; matrix products, arithmetic and copies ran while one was open for 37% of the time, Pallas kernels for 4%

profile of v2, /device:TPU:0, one launch (start us, length us, event | category | flops | bytes accessed | tf_op | source)
XLA Modules:
  0.0 1000.9 jit_solution(13272189902631910206)
XLA Ops:
  12.8 5.5 all-to-all-start.2
  18.4 34.5 %all-gather.1 = f32[16,1,704]{2,1,0:T(1,128)S(1)} all-gather(f32[1,1,704]{2,1,0:T(1,128)S(1)} %maximum_bitcast_fusion.3), channel_id=1, replica_groups=mesh['z'=2,'y'=2,'x'=2,'c'=2] {'z','y','x','c'}, dimensions={0}, use_global_device_ids=true | all-gather | bytes 47872 | tf_op jit(solution)/shard_map/all_gather | solution.py:126
  53.0 4.2 and_reduce_fusion
  58.7 21.0 %gather_fusion.2 = bf16[768,1536]{1,0:T(8,128)(2,1)} fusion(bf16[9496,1536]{1,0:T(8,128)(2,1)} %param.18, s32[1024]{0:T(1024)S(1)} %pad_clamp_fusion.1), kind=kCustom, calls=%fused_computation.2 | custom fusion | bytes 4721664 | tf_op jit(solution)/shard_map/gather | solution.py:155
  88.8 28.9 %all-to-all-done = bf16[16,48,1536]{2,1,0:T(8,128)(2,1)S(1)} async-done(((bf16[16,48,1536]{2,1,0:T(8,128)(2,1)}), bf16[16,48,1536]{2,1,0:T(8,128)(2,1)S(1)}, u32[]{:S(2)}, u32[]{:S(2)}) %all-to-all-start) | async-done | bytes 2359328 | tf_op jit(solution)/shard_map/all_to_all | solution.py:156
  117.7 4.4 all-to-all-start.1
  123.9 5.1 conditional.2
  129.1 5.8 collective-permute-start.37
  139.5 3.4 broadcast_in_dim.221
  144.6 14.0 %all-to-all-done.1 = bf16[4,96,2240]{2,1,0:T(8,128)(2,1)} async-done(((bf16[4,96,2240]{2,1,0:T(8,128)(2,1)}), bf16[4,96,2240]{2,1,0:T(8,128)(2,1)}, u32[]{:S(2)}, u32[]{:S(2)}) %all-to-all-start.1) | async-done | bytes 1720352 | tf_op jit(solution)/shard_map/all_to_all | solution.py:183
  158.6 4.5 collective-permute-start.31
  163.1 3.6 broadcast.378.clone
  169.6 5.6 fusion.45
  193.5 3.4 fusion.35
  201.8 3.8 fusion.89
  205.6 5.9 fusion.73
  214.7 3.6 broadcast.378.clone.1
  218.4 3.1 bitcast_dynamic-update-slice_fusion.7
  227.7 21.4 %collective-permute-done.31 = bf16[4,96,2240]{2,1,0:T(8,128)(2,1)} collective-permute-done((bf16[4,96,2240]{2,1,0:T(8,128)(2,1)}, bf16[4,96,2240]{2,1,0:T(8,128)(2,1)}, u32[]{:S(2)}, u32[]{:S(2)}) %collective-permute-start.31) | collective-permute-done | bytes 1720352 | tf_op jit(solution)/shard_map/ppermute | solution.py:62
  263.0 20.1 %convolution_convert_fusion = bf16[2240,2048]{1,0:T(8,128)(2,1)} fusion(bf16[2240,1536]{1,0:T(8,128)(2,1)} %bitcast.72, bf16[1,2048,1536]{2,1,0:T(8,128)(2,1)} %all-gather.10.cloned.1.call-done), kind=kOutput, calls=%fused_computation.95 | convolution fusion | flops 14097448960 | bytes 22347776 | tf_op jit(solution)/shard_map/dot_general | solution.py:58
  283.1 20.8 %fusion.154 = f32[2048,2240]{0,1:T(8,128)} fusion(bf16[2048,1536]{1,0:T(8,128)(2,1)} %all-gather.8.cloned.1.call-done, bf16[1536,2240]{1,0:T(8,128)(2,1)} %bitcast.67), kind=kOutput, calls=%fused_computation.304 | convolution fusion | flops 14092861440 | bytes 31522816 | tf_op jit(solution)/shard_map/dot_general | solution.py:58
  303.9 34.4 %fusion.23 = (bf16[2048,2240]{0,1:T(8,128)(2,1)}, bf16[2048,2240]{0,1:T(8,128)(2,1)}, bf16[2048,2240]{0,1:T(8,128)(2,1)}) fusion(f32[2048,2240]{0,1:T(8,128)} %fusion.154, bf16[2240,2048]{1,0:T(8,128)(2,1)} %convolution_convert_fusion, bf16[2048,1536]{1,0:T(8,128)(2,1)} %all-gather.8.cloned.1.call-done, bf16[1536,2240]{1,0:T(8,128)(2,1)} %bitcast.54), kind=kOutput, calls=%fused_computation.73 | convolution fusion | flops 14170849280 | bytes 68222976 | tf_op jit(solution)/shard_map/dot_general | solution.py:58
  338.3 20.8 %fusion.156 = f32[2048,1536]{1,0:T(8,128)S(1)} fusion(bf16[2048,2240]{0,1:T(8,128)(2,1)} %get-tuple-element.171, bf16[1536,2240]{1,0:T(8,128)(2,1)} %bitcast.67), kind=kOutput, calls=%fused_computation.306 | convolution fusion | flops 14092861440 | bytes 28639232 | tf_op jit(solution)/shard_map/dot_general | solution.py:58
  359.1 21.2 %convolution_add_fusion = f32[2048,1536]{1,0:T(8,128)} fusion(f32[2048,1536]{1,0:T(8,128)S(1)} %fusion.156, bf16[2048,2240]{0,1:T(8,128)(2,1)} %get-tuple-element.169, bf16[1536,2240]{1,0:T(8,128)(2,1)} %bitcast.54), kind=kOutput, calls=%fused_computation.97 | convolution fusion | flops 14096007168 | bytes 41222144 | tf_op jit(solution)/shard_map/dot_general | solution.py:58
  380.4 21.3 %fusion.155 = f32[2048,1536]{1,0:T(8,128)} fusion(bf16[2048,2240]{0,1:T(8,128)(2,1)} %get-tuple-element.170, bf16[2240,1536]{1,0:T(8,128)(2,1)} %bitcast.72), kind=kOutput, calls=%fused_computation.305 | convolution fusion | flops 14092861440 | bytes 28639232 | tf_op jit(solution)/shard_map/dot_general | solution.py:58
  403.0 18.9 %fusion.36 = f32[2240,1536]{1,0:T(8,128)S(1)} fusion(bf16[2048,2240]{0,1:T(8,128)(2,1)} %get-tuple-element.170, bf16[1,2048,1536]{2,1,0:T(8,128)(2,1)} %all-gather.10.cloned.1.call-done), kind=kOutput, calls=%fused_computation.104 | convolution fusion | flops 14092861440 | bytes 29229056 | tf_op jit(solution)/shard_map/dot_general | solution.py:58
  421.9 3.7 dynamic-slice_bitcast_fusion.17
  425.6 3.7 copy-done.8
  430.1 17.4 %fusion.159 = f32[1536,2240]{1,0:T(8,128)S(1)} fusion(bf16[2048,1536]{1,0:T(8,128)(2,1)S(1)} %bitcast.446, bf16[2048,2240]{0,1:T(8,128)(2,1)} %get-tuple-element.171), kind=kOutput, calls=%fused_computation.309 | convolution fusion | flops 14092861440 | bytes 29229056 | tf_op jit(solution)/shard_map/dot_general | solution.py:58
  447.6 3.5 dynamic-slice_bitcast_fusion.15
  451.0 4.1 copy-done.6
  455.1 43.8 %reduce-scatter.7.cloned.1.call-done = f32[512,1536]{1,0:T(8,128)} async-done(((f32[2048,1536]{1,0:T(8,128)}), f32[512,1536]{1,0:T(8,128)}) %reduce-scatter.7.cloned.1.call-update) | async-done | bytes 3145744 | tf_op jit(solution)/shard_map/reduce_scatter | solution.py:211
  498.9 3.6 fusion.67
  504.7 5.3 fusion.157
  510.0 19.3 %fusion.158 = f32[1536,2240]{1,0:T(8,128)S(1)} fusion(bf16[2048,1536]{1,0:T(8,128)(2,1)} %all-gather.8.cloned.1.call-done, bf16[2048,2240]{0,1:T(8,128)(2,1)} %get-tuple-element.169), kind=kOutput, calls=%fused_computation.308 | convolution fusion | flops 14092861440 | bytes 29229056 | tf_op jit(solution)/shard_map/dot_general | solution.py:58
  529.3 3.3 dynamic-slice_bitcast_fusion.16
  532.7 4.8 copy-done.7
  537.4 5.0 fusion.78
  543.3 9.6 fusion.34
  553.0 10.4 %fusion.116 = f32[1,512,2,128]{3,1,2,0:T(8,128)S(1)} fusion(bf16[2,6,512,512]{2,3,1,0:T(8,128)(2,1)} %get-tuple-element.208, f32[2,6,512]{2,1,0:T(8,128)S(1)} %neg.18, f32[2,6,512]{2,1,0:T(8,128)S(1)} %copy-done.60, pred[512,512]{0,1:T(8,128)(4,1)S(1)} %copy-done.25, f32[2,512,512,6]{2,1,3,0:T(8,128)} %copy-done.2, f32[2,6,512]{2,1,0:T(8,128)S(1)} %copy-done.57, ...), kind=kOutput, calls=%fused_computation.205 | convolution fusion | flops 837025792 | bytes 21307392 | tf_op jit(solution)/shard_map/transpose(jvp(bqkgd,bskd->bkgqs))/dot_general | solution.py:44
  563.4 7.9 bitcast_convert_fusion
  571.4 4.2 fusion.104
  582.3 8.2 fusion.120
  590.5 6.5 bitcast_add_fusion.1
  600.4 6.5 bitcast_add_fusion.2
  609.6 9.5 bitcast_add_fusion.3
  619.0 4.0 dynamic-slice_bitcast_fusion.20
  624.4 71.0 %collective-permute-done.42 = f32[4,96,2240]{2,1,0:T(8,128)} collective-permute-done((f32[4,96,2240]{2,1,0:T(8,128)}, f32[4,96,2240]{2,1,0:T(8,128)}, u32[]{:S(2)}, u32[]{:S(2)}) %collective-permute-start.42) | collective-permute-done | bytes 3440672 | tf_op jit(solution)/shard_map/ppermute | solution.py:62
  698.0 96.0 %collective-permute-done.40 = f32[4,96,2240]{2,1,0:T(8,128)} collective-permute-done((f32[4,96,2240]{2,1,0:T(8,128)}, f32[4,96,2240]{2,1,0:T(8,128)}, u32[]{:S(2)}, u32[]{:S(2)}) %collective-permute-start.40) | collective-permute-done | bytes 3440672 | tf_op jit(solution)/shard_map/ppermute | solution.py:62
  798.7 5.0 all-to-all-start.4
  803.8 7.4 fusion.68
  813.8 2.9 select_select_fusion.1
  816.6 40.1 %all-to-all-done.4 = bf16[4,2,96,2240]{3,2,1,0:T(8,128)(2,1)} async-done(((bf16[4,2,96,2240]{3,2,1,0:T(8,128)(2,1)}), bf16[4,2,96,2240]{3,2,1,0:T(8,128)(2,1)}, u32[]{:S(2)}, u32[]{:S(2)}) %all-to-all-start.4) | async-done | bytes 3440672 | tf_op jit(solution)/shard_map/all_to_all | solution.py:233
  856.7 3.5 all-to-all-start.3
  860.3 3.8 sort.15
  864.2 32.8 %collective-permute-done.44 = f32[560,1536]{1,0:T(8,128)} collective-permute-done((f32[560,1536]{1,0:T(8,128)}, f32[560,1536]{1,0:T(8,128)}, u32[]{:S(2)}, u32[]{:S(2)}) %collective-permute-start.44) | collective-permute-done | bytes 3440672 | tf_op jit(solution)/shard_map/ppermute | solution.py:62
  897.0 4.7 fusion.61
  901.7 3.4 fusion.150
  909.1 4.2 copy.189
  913.3 4.1 squeeze.116
  917.4 3.6 fusion.92
  921.0 26.9 %all-to-all-done.3 = f32[16,48,1536]{2,1,0:T(8,128)} async-done(((f32[16,48,1536]{2,1,0:T(8,128)}), f32[16,48,1536]{2,1,0:T(8,128)}, u32[]{:S(2)}, u32[]{:S(2)}) %all-to-all-start.3) | async-done | bytes 4718624 | tf_op jit(solution)/shard_map/all_to_all | solution.py:252
  948.0 38.7 %conditional.3 = (bf16[9496,1536]{1,0:T(8,128)(2,1)}) conditional(s32[]{:T(128)} %convert_element_type.218, (s32[76,768]{1,0:T(8,128)S(1)}, f32[16,48,1536]{2,1,0:T(8,128)}, s32[768]{0:T(1024)S(1)}, s32[768]{0:T(1024)S(1)}) %tuple.34, (s32[]{:T(128)}, s32[16,512]{1,0:T(8,128)S(1)}, s32[16,512]{1,0:T(8,128)S(1)}, ...), branch_computations={%region_23.25_spmd, %region_25.27_spmd} | conditional | flops 40000057344 | bytes 366523680 | solution.py:267
  948.6 36.7 %branch_0_fun.1 = bf16[9496,1536]{1,0:T(8,128)(2,1)} custom-call(s32[76]{0:T(128)} %reduce_sum.90.start_ref, s32[768]{0:T(1024)S(1)} %get-tuple-element.44.slot_ref, s32[768]{0:T(1024)S(1)} %get-tuple-element.45.row_ref, f32[768,1536]{1,0:T(8,128)} %bitcast.17.recv_ref), custom_call_target="tpu_custom_call" | custom-call | flops 40000000000 | bytes 40000000 | tf_op jit(solution)/shard_map/cond/branch_0_fun/pallas_call | solution.py:81
  (316 shorter events, 118.7 us)
Async XLA Ops:
  7.2 162.4 %all-gather.6.cloned.1.call-start = ((), (), s32[]{:S(2)}) async-start(), calls=%async_computation.9 | async-start | bytes 11698176 | tf_op jit(solution)/shard_map/all_gather | solution.py:172
  12.8 66.9 %all-to-all-start.2 = ((bf16[4,96,2240]{2,1,0:T(8,128)(2,1)}), bf16[4,96,2240]{2,1,0:T(8,128)(2,1)}, u32[]{:S(2)}, u32[]{:S(2)}) async-start(bf16[4,96,2240]{2,1,0:T(8,128)(2,1)} %pad_maximum_fusion.3), calls=%async_computation.2 | async-start | bytes 3538944 | tf_op jit(solution)/shard_map/all_to_all | solution.py:183
  57.4 66.5 %copy-start.52 = (s32[16,512]{1,0:T(8,128)}, s32[16,512]{1,0:T(8,128)S(1)}, u32[]{:S(2)}) copy-start(s32[16,512]{1,0:T(8,128)S(1)} %get-tuple-element.153) | copy-start | bytes 98308
  57.7 66.3 %copy-start.50 = (s32[16,512]{1,0:T(8,128)}, s32[16,512]{1,0:T(8,128)S(1)}, u32[]{:S(2)}) copy-start(s32[16,512]{1,0:T(8,128)S(1)} %broadcast_subtract_fusion) | copy-start | bytes 98308
  58.1 21.6 %copy-start.63 = (s32[16,48]{1,0:T(8,128)}, s32[16,48]{1,0:T(8,128)S(1)}, u32[]{:S(2)}) copy-start(s32[16,48]{1,0:T(8,128)S(1)} %select_reduce_fusion) | copy-start | bytes 9220
  58.6 21.1 %copy-start.74 = (pred[16,48]{1,0:T(8,128)(4,1)}, pred[16,48]{1,0:T(8,128)(4,1)S(1)}, u32[]{:S(2)}) copy-start(pred[16,48]{1,0:T(8,128)(4,1)S(1)} %fusion.95) | copy-start | bytes 2308
  79.7 38.0 %all-to-all-start = ((bf16[16,48,1536]{2,1,0:T(8,128)(2,1)}), bf16[16,48,1536]{2,1,0:T(8,128)(2,1)S(1)}, u32[]{:S(2)}, u32[]{:S(2)}) async-start(bf16[16,48,1536]{2,1,0:T(8,128)(2,1)} %bitcast.26), calls=%async_computation | async-start | bytes 4718592 | tf_op jit(solution)/shard_map/all_to_all | solution.py:156
  82.2 180.8 %all-gather.10.cloned.1.call-start = ((), (), s32[]{:S(2)}) async-start(), calls=%async_computation.15 | async-start | bytes 7864320 | tf_op jit(solution)/shard_map/all_gather | solution.py:175
  83.9 38.6 %copy-start.80 = (s32[512]{0:T(512)}, s32[512]{0:T(512)S(1)}, u32[]{:S(2)}) copy-start(s32[512]{0:T(512)S(1)} %select_reduce_fusion.1) | copy-start | bytes 6148
  117.7 41.0 %all-to-all-start.1 = ((bf16[4,96,2240]{2,1,0:T(8,128)(2,1)}), bf16[4,96,2240]{2,1,0:T(8,128)(2,1)}, u32[]{:S(2)}, u32[]{:S(2)}) async-start(bf16[4,96,2240]{2,1,0:T(8,128)(2,1)} %pad_maximum_fusion.2), calls=%async_computation.1 | async-start | bytes 3538944 | tf_op jit(solution)/shard_map/all_to_all | solution.py:183
  122.1 161.0 %all-gather.8.cloned.1.call-start = ((), (), s32[]{:S(2)}) async-start(), calls=%async_computation.10 | async-start | bytes 7864320 | tf_op jit(solution)/shard_map/all_gather | solution.py:203
  129.1 40.5 %copy-start.72 = (f32[512]{0:T(512)}, f32[512]{0:T(512)S(1)}, u32[]{:S(2)}) copy-start(f32[512]{0:T(512)S(1)} %get-tuple-element.69) | copy-start | bytes 6148
  129.1 40.5 %copy-start.9 = (f32[512,1536]{1,0:T(8,128)}, f32[512,1536]{1,0:T(8,128)S(1)}, u32[]{:S(2)}) copy-start(f32[512,1536]{1,0:T(8,128)S(1)} %get-tuple-element.68) | copy-start | bytes 9437188
  129.1 92.4 %collective-permute-start.37 = (bf16[560,1536]{1,0:T(8,128)(2,1)}, bf16[560,1536]{1,0:T(8,128)(2,1)}, u32[]{:S(2)}, u32[]{:S(2)}) collective-permute-start(bf16[560,1536]{1,0:T(8,128)(2,1)} %param.27), channel_id=1, source_target_pairs={{0,2},{2,0},{1,3},{3,1},{4,6},{6,4},{5,7},{7,5},{8,10},{10,8},{9,1... | collective-permute-start | bytes 5160968 | tf_op jit(solution)/shard_map/ppermute | solution.py:62
  134.9 86.6 %collective-permute-start.36 = (bf16[560,1536]{1,0:T(8,128)(2,1)}, bf16[560,1536]{1,0:T(8,128)(2,1)}, u32[]{:S(2)}, u32[]{:S(2)}) collective-permute-start(bf16[560,1536]{1,0:T(8,128)(2,1)} %param.27), channel_id=1, source_target_pairs={{0,1},{1,0},{2,3},{3,2},{4,5},{5,4},{6,7},{7,6},{8,9},{9,8},{10,11... | collective-permute-start | bytes 5160968 | tf_op jit(solution)/shard_map/ppermute | solution.py:62
  135.2 76.4 %copy-start.61 = (f32[1536]{0:T(1024)}, f32[1536]{0:T(1024)S(1)}, u32[]{:S(2)}) copy-start(f32[1536]{0:T(1024)S(1)} %mul.509) | copy-start | bytes 18436
  135.2 34.4 %copy-start.68 = (f32[1536]{0:T(1024)}, f32[1536]{0:T(1024)S(1)}, u32[]{:S(2)}) copy-start(f32[1536]{0:T(1024)S(1)} %mul.485) | copy-start | bytes 18436
  139.5 60.2 %copy-start.24 = (pred[512,512]{0,1:T(8,128)(4,1)}, pred[512,512]{0,1:T(8,128)(4,1)S(1)}, u32[]{:S(2)}) copy-start(pred[512,512]{0,1:T(8,128)(4,1)S(1)} %iota_compare_fusion.4) | copy-start | bytes 786436
  144.2 83.3 %collective-permute-start.34 = (bf16[4,96,2240]{2,1,0:T(8,128)(2,1)}, bf16[4,96,2240]{2,1,0:T(8,128)(2,1)}, u32[]{:S(2)}, u32[]{:S(2)}) collective-permute-start(bf16[4,96,2240]{2,1,0:T(8,128)(2,1)} %all-to-all-done.2), channel_id=1, source_target_pairs={{0,2},{2,0},{1,3},{3,1},{4,6},{6,4},{5,7},{7,5},{8,10},{10,8},{9,1... | collective-permute-start | bytes 5160968 | tf_op jit(solution)/shard_map/ppermute | solution.py:62
  144.6 104.6 %collective-permute-start.33 = (bf16[4,96,2240]{2,1,0:T(8,128)(2,1)}, bf16[4,96,2240]{2,1,0:T(8,128)(2,1)}, u32[]{:S(2)}, u32[]{:S(2)}) collective-permute-start(bf16[4,96,2240]{2,1,0:T(8,128)(2,1)} %all-to-all-done.2), channel_id=1, source_target_pairs={{0,1},{1,0},{2,3},{3,2},{4,5},{5,4},{6,7},{7,6},{8,9},{9,8},{10,11... | collective-permute-start | bytes 5160968 | tf_op jit(solution)/shard_map/ppermute | solution.py:62
  158.6 90.5 %collective-permute-start.31 = (bf16[4,96,2240]{2,1,0:T(8,128)(2,1)}, bf16[4,96,2240]{2,1,0:T(8,128)(2,1)}, u32[]{:S(2)}, u32[]{:S(2)}) collective-permute-start(bf16[4,96,2240]{2,1,0:T(8,128)(2,1)} %all-to-all-done.1), channel_id=1, source_target_pairs={{0,2},{2,0},{1,3},{3,1},{4,6},{6,4},{5,7},{7,5},{8,10},{10,8},{9,1... | collective-permute-start | bytes 5160968 | tf_op jit(solution)/shard_map/ppermute | solution.py:62
  187.7 9.3 copy-start.14
  214.2 284.7 %reduce-scatter.7.cloned.1.call-start = ((), (), s32[]{:S(2)}) async-start(), calls=%async_computation.12 | async-start | bytes 15728640 | tf_op jit(solution)/shard_map/reduce_scatter | solution.py:211
  221.5 33.4 %collective-permute-start.30 = (bf16[4,96,2240]{2,1,0:T(8,128)(2,1)}, bf16[4,96,2240]{2,1,0:T(8,128)(2,1)S(1)}, u32[]{:S(2)}, u32[]{:S(2)}) collective-permute-start(bf16[4,96,2240]{2,1,0:T(8,128)(2,1)} %all-to-all-done.1), channel_id=1, source_target_pairs={{0,1},{1,0},{2,3},{3,2},{4,5},{5,4},{6,7},{7,6},{8,9},{9,8},{10,11... | collective-permute-start | bytes 5160968 | tf_op jit(solution)/shard_map/ppermute | solution.py:62
  221.5 37.5 %collective-permute-start.38 = (bf16[560,1536]{1,0:T(8,128)(2,1)}, bf16[560,1536]{1,0:T(8,128)(2,1)S(1)}, u32[]{:S(2)}, u32[]{:S(2)}) collective-permute-start(bf16[560,1536]{1,0:T(8,128)(2,1)} %collective-permute-done.37), channel_id=1, source_target_pairs={{0,1},{1,0},{2,3},{3,2},{4,5},{5,4},{6,7},{7,6},{8,9},{9,8},{10,11... | collective-permute-start | bytes 5160968 | tf_op jit(solution)/shard_map/ppermute | solution.py:62
  227.6 32.8 %collective-permute-start.35 = (bf16[4,96,2240]{2,1,0:T(8,128)(2,1)}, bf16[4,96,2240]{2,1,0:T(8,128)(2,1)S(1)}, u32[]{:S(2)}, u32[]{:S(2)}) collective-permute-start(bf16[4,96,2240]{2,1,0:T(8,128)(2,1)} %collective-permute-done.34), channel_id=1, source_target_pairs={{0,1},{1,0},{2,3},{3,2},{4,5},{5,4},{6,7},{7,6},{8,9},{9,8},{10,11... | collective-permute-start | bytes 5160968 | tf_op jit(solution)/shard_map/ppermute | solution.py:62
  249.2 12.5 %collective-permute-start.32 = (bf16[4,96,2240]{2,1,0:T(8,128)(2,1)}, bf16[4,96,2240]{2,1,0:T(8,128)(2,1)S(1)}, u32[]{:S(2)}, u32[]{:S(2)}) collective-permute-start(bf16[4,96,2240]{2,1,0:T(8,128)(2,1)} %collective-permute-done.31), channel_id=1, source_target_pairs={{0,1},{1,0},{2,3},{3,2},{4,5},{5,4},{6,7},{7,6},{8,9},{9,8},{10,11... | collective-permute-start | bytes 5160968 | tf_op jit(solution)/shard_map/ppermute | solution.py:62
  380.3 537.1 %reduce-scatter.5.cloned.1.call-start = ((), (), s32[]{:S(2)}) async-start(), calls=%async_computation.11 | async-start | bytes 15728640 | tf_op jit(solution)/shard_map/reduce_scatter | solution.py:213
  401.7 28.4 %slice-start.3 = ((s8[6291456]{0:T(1024)(128)(4,1)}), s8[2097152]{0:T(1024)(128)(4,1)S(1)}, s32[]{:S(2)}) async-start(s8[6291456]{0:T(1024)(128)(4,1)} %bitcast.445), calls=%async_computation.19 | async-start | bytes 4194304
  401.7 586.9 %reduce-scatter.11.cloned.1.call-start = ((), (), s32[]{:S(2)}) async-start(), calls=%async_computation.14 | async-start | bytes 10027008 | tf_op jit(solution)/shard_map/reduce_scatter | solution.py:239
  403.0 27.1 %slice-start.4 = ((s8[6291456]{0:T(1024)(128)(4,1)}), s8[4194304]{0:T(1024)(128)(4,1)S(1)}, s32[]{:S(2)}) async-start(s8[6291456]{0:T(1024)(128)(4,1)} %bitcast.445), calls=%async_computation.20 | async-start | bytes 8388608
  429.3 180.2 %collective-permute-start.43 = (f32[2,560,1536]{2,1,0:T(8,128)}, f32[2,560,1536]{2,1,0:T(8,128)}, u32[]{:S(2)}, u32[]{:S(2)}) collective-permute-start(f32[2,560,1536]{2,1,0:T(8,128)} %dynamic-slice_bitcast_fusion.17), channel_id=1, source_target_pairs={{0,1},{1,0},{2,3},{3,2},{4,5},{5,4},{6,7},{7,6},{8,9},{9,8},{10,11... | collective-permute-start | bytes 20643848 | tf_op jit(solution)/shard_map/ppermute | solution.py:62
  447.5 7.6 copy-start.6
  447.5 51.4 %copy-start.4 = (bf16[512,1536]{1,0:T(8,128)(2,1)S(1)}, bf16[512,1536]{1,0:T(8,128)(2,1)}, u32[]{:S(2)}) copy-start(bf16[512,1536]{1,0:T(8,128)(2,1)} %copy-done.3) | copy-start | bytes 4718596
  447.5 51.4 %copy-start.62 = (f32[1536]{0:T(1024)S(1)}, f32[1536]{0:T(1024)}, u32[]{:S(2)}) copy-start(f32[1536]{0:T(1024)} %copy-done.61) | copy-start | bytes 18436
  447.5 51.4 %copy-start.71 = (f32[512]{0:T(512)S(1)}, f32[512]{0:T(512)}, u32[]{:S(2)}) copy-start(f32[512]{0:T(512)} %copy-done.70) | copy-start | bytes 6148
  455.1 47.4 %copy-start.77 = (f32[512]{0:T(512)S(1)}, f32[512]{0:T(512)}, u32[]{:S(2)}) copy-start(f32[512]{0:T(512)} %copy-done.76) | copy-start | bytes 6148
  455.1 47.4 %copy-start.18 = (bf16[1,512,1536]{2,1,0:T(8,128)(2,1)S(1)}, bf16[1,512,1536]{2,1,0:T(8,128)(2,1)}, u32[]{:S(2)}) copy-start(bf16[1,512,1536]{2,1,0:T(8,128)(2,1)} %param.17) | copy-start | bytes 4718596
  455.1 135.4 %collective-permute-start.41 = (f32[4,2,96,2240]{3,2,1,0:T(8,128)}, f32[4,2,96,2240]{3,2,1,0:T(8,128)}, u32[]{:S(2)}, u32[]{:S(2)}) collective-permute-start(f32[4,2,96,2240]{3,2,1,0:T(8,128)} %dynamic-slice_bitcast_fusion.15), channel_id=1, source_target_pairs={{0,1},{1,0},{2,3},{3,2},{4,5},{5,4},{6,7},{7,6},{8,9},{9,8},{10,11... | collective-permute-start | bytes 20643848 | tf_op jit(solution)/shard_map/ppermute | solution.py:62
  510.0 480.4 %reduce-scatter.9.cloned.1.call-start = ((), (), s32[]{:S(2)}) async-start(), calls=%async_computation.13 | async-start | bytes 13369344 | tf_op jit(solution)/shard_map/reduce_scatter | solution.py:244
  529.3 8.1 copy-start.7
  529.3 8.1 copy-start.22
  537.4 63.0 %collective-permute-start.39 = (f32[4,2,96,2240]{3,2,1,0:T(8,128)}, f32[4,2,96,2240]{3,2,1,0:T(8,128)}, u32[]{:S(2)}, u32[]{:S(2)}) collective-permute-start(f32[4,2,96,2240]{3,2,1,0:T(8,128)} %dynamic-slice_bitcast_fusion.16), channel_id=1, source_target_pairs={{0,1},{1,0},{2,3},{3,2},{4,5},{5,4},{6,7},{7,6},{8,9},{9,8},{10,11... | collective-permute-start | bytes 20643848 | tf_op jit(solution)/shard_map/ppermute | solution.py:62
  543.2 9.7 copy-start.31
  543.2 9.7 copy-start.15
  543.3 9.7 copy-start.17
  543.3 9.7 copy-start.60
  543.3 20.1 %slice-start = ((s8[12582912]{0:T(1024)(128)(4,1)}), s8[4194304]{0:T(1024)(128)(4,1)S(1)}, s32[]{:S(2)}) async-start(s8[12582912]{0:T(1024)(128)(4,1)} %bitcast.406), calls=%async_computation.16 | async-start | bytes 8388608
  553.0 10.4 %slice-start.1 = ((s8[12582912]{0:T(1024)(128)(4,1)}), s8[4194304]{0:T(1024)(128)(4,1)S(1)}, s32[]{:S(2)}) async-start(s8[12582912]{0:T(1024)(128)(4,1)} %bitcast.406), calls=%async_computation.17 | async-start | bytes 8388608
  553.0 10.4 %slice-start.2 = ((s8[12582912]{0:T(1024)(128)(4,1)}), s8[4194304]{0:T(1024)(128)(4,1)S(1)}, s32[]{:S(2)}) async-start(s8[12582912]{0:T(1024)(128)(4,1)} %bitcast.406), calls=%async_computation.18 | async-start | bytes 8388608
  553.0 10.4 %copy-start.47 = (bf16[512,2,64]{2,0,1:T(8,128)(2,1)S(1)}, bf16[512,2,64]{2,0,1:T(8,128)(2,1)}, u32[]{:S(2)}) copy-start(bf16[512,2,64]{2,0,1:T(8,128)(2,1)} %copy-done.46) | copy-start | bytes 393220
  553.0 10.4 %copy-start.49 = (bf16[512,2,64]{2,0,1:T(8,128)(2,1)S(1)}, bf16[512,2,64]{2,0,1:T(8,128)(2,1)}, u32[]{:S(2)}) copy-start(bf16[512,2,64]{2,0,1:T(8,128)(2,1)} %copy-done.48) | copy-start | bytes 393220
  563.4 7.9 copy-start.32
  599.0 96.4 %collective-permute-start.42 = (f32[4,96,2240]{2,1,0:T(8,128)}, f32[4,96,2240]{2,1,0:T(8,128)}, u32[]{:S(2)}, u32[]{:S(2)}) collective-permute-start(f32[4,96,2240]{2,1,0:T(8,128)} %dynamic-slice_bitcast_fusion.18), channel_id=1, source_target_pairs={{0,2},{2,0},{1,3},{3,1},{4,6},{6,4},{5,7},{7,5},{8,10},{10,8},{9,1... | collective-permute-start | bytes 10321928 | tf_op jit(solution)/shard_map/ppermute | solution.py:62
  608.9 185.2 %collective-permute-start.40 = (f32[4,96,2240]{2,1,0:T(8,128)}, f32[4,96,2240]{2,1,0:T(8,128)}, u32[]{:S(2)}, u32[]{:S(2)}) collective-permute-start(f32[4,96,2240]{2,1,0:T(8,128)} %dynamic-slice_bitcast_fusion.19), channel_id=1, source_target_pairs={{0,2},{2,0},{1,3},{3,1},{4,6},{6,4},{5,7},{7,5},{8,10},{10,8},{9,1... | collective-permute-start | bytes 10321928 | tf_op jit(solution)/shard_map/ppermute | solution.py:62
  623.0 273.9 %collective-permute-start.44 = (f32[560,1536]{1,0:T(8,128)}, f32[560,1536]{1,0:T(8,128)}, u32[]{:S(2)}, u32[]{:S(2)}) collective-permute-start(f32[560,1536]{1,0:T(8,128)} %dynamic-slice_bitcast_fusion.20), channel_id=1, source_target_pairs={{0,2},{2,0},{1,3},{3,1},{4,6},{6,4},{5,7},{7,5},{8,10},{10,8},{9,1... | collective-permute-start | bytes 10321928 | tf_op jit(solution)/shard_map/ppermute | solution.py:62
  798.7 58.0 %all-to-all-start.4 = ((bf16[4,2,96,2240]{3,2,1,0:T(8,128)(2,1)}), bf16[4,2,96,2240]{3,2,1,0:T(8,128)(2,1)}, u32[]{:S(2)}, u32[]{:S(2)}) async-start(bf16[4,2,96,2240]{3,2,1,0:T(8,128)(2,1)} %copy.188), calls=%async_computation.8 | async-start | bytes 7077888 | tf_op jit(solution)/shard_map/all_to_all | solution.py:233
  816.6 43.6 %copy-start.64 = (s32[16,48]{1,0:T(8,128)S(1)}, s32[16,48]{1,0:T(8,128)}, u32[]{:S(2)}) copy-start(s32[16,48]{1,0:T(8,128)} %copy-done.63) | copy-start | bytes 9220
  816.6 43.6 %copy-start.75 = (pred[16,48]{1,0:T(8,128)(4,1)S(1)}, pred[16,48]{1,0:T(8,128)(4,1)}, u32[]{:S(2)}) copy-start(pred[16,48]{1,0:T(8,128)(4,1)} %copy-done.74) | copy-start | bytes 2308
  856.7 91.2 %all-to-all-start.3 = ((f32[16,48,1536]{2,1,0:T(8,128)}), f32[16,48,1536]{2,1,0:T(8,128)}, u32[]{:S(2)}, u32[]{:S(2)}) async-start(f32[16,48,1536]{2,1,0:T(8,128)} %select_select_fusion.1), calls=%async_computation.5 | async-start | bytes 9437184 | tf_op jit(solution)/shard_map/all_to_all | solution.py:252
  909.1 8.3 copy-start.5
  917.4 30.6 %copy-start.20 = (bf16[512,1536]{1,0:T(8,128)(2,1)S(1)}, bf16[512,1536]{1,0:T(8,128)(2,1)}, u32[]{:S(2)}) copy-start(bf16[512,1536]{1,0:T(8,128)(2,1)} %copy-done.19) | copy-start | bytes 4718596
  917.4 30.6 %copy-start.51 = (s32[16,512]{1,0:T(8,128)S(1)}, s32[16,512]{1,0:T(8,128)}, u32[]{:S(2)}) copy-start(s32[16,512]{1,0:T(8,128)} %copy-done.50) | copy-start | bytes 98308
  917.4 30.6 %copy-start.53 = (s32[16,512]{1,0:T(8,128)S(1)}, s32[16,512]{1,0:T(8,128)}, u32[]{:S(2)}) copy-start(s32[16,512]{1,0:T(8,128)} %copy-done.52) | copy-start | bytes 98308
  (45 other events, 189.6 us)
Sparse Core Ops, SparseCore 0:
  11.0 73.3 all-gather.5
  86.2 95.3 all-gather.9
  214.4 65.3 all-gather.7
  380.5 118.3 reduce-scatter.6
  501.8 116.8 reduce-scatter.4
  623.3 109.7 reduce-scatter.10
  737.7 145.4 reduce-scatter.8

commit v3 on v2

--- a/solution.py
+++ b/solution.py
@@ -14,6 +14,7 @@
 SLOTS = 48
 USABLE = SLOTS - 2
 ROW_BLOCK = 128
+CHUNKS = 2
 F32 = jnp.float32
 BF16 = jnp.bfloat16
 
@@ -173,6 +174,7 @@
         w_qkv, w_o = attn_w[:, :qkv_w], attn_w[:, qkv_w:]
         dy = grad_y[0]
         dy_all = lax.all_gather(dy, PLANE, axis=0, tiled=True)
+        dy_all = dy_all.reshape(4, CHUNKS, -1, dim).transpose(1, 0, 2, 3).reshape(-1, dim)
 
         def gather_xc(w):
             wx = flip(w, "x")
@@ -200,19 +202,31 @@
         resid_two = resid_bf.astype(F32)
         h_two, norm2_pull = jax.vjp(rms_norm, resid_two, g2_full)
 
-        h_all = lax.all_gather(h_two, PLANE, axis=0, tiled=True)
-        d_act = dot(dy_all, w_d, 1, 1).astype(BF16)
-        gate_f32 = dot(h_all, w_g, 1, 0)
-        up_f32 = dot(h_all, w_u, 1, 0)
-        act, act_pull = jax.vjp(gated, gate_f32, up_f32)
-        d_gate, d_up = act_pull(d_act)
-        d_gate, d_up = d_gate.astype(BF16), d_up.astype(BF16)
-        d_h_part = dot(d_gate, w_g, 1, 1) + dot(d_up, w_u, 1, 1)
-        d_h_two = lax.psum_scatter(d_h_part, PLANE, scatter_dimension=0, tiled=True).astype(BF16)
-        y_part = dot(act, w_d, 1, 0)
-        y_sum = lax.psum_scatter(y_part, PLANE, scatter_dimension=0, tiled=True)
-        y_sum, resid_y = lax.optimization_barrier((y_sum, resid_bf))
+        step_t = seq // CHUNKS
+        h_own = h_two.reshape(CHUNKS, step_t, dim)
+        hs, acts, d_gates, d_ups, d_hs = [], [], [], [], []
+        for k in range(CHUNKS):
+            d_act = dot(lax.slice_in_dim(dy_all, k * 4 * step_t, (k + 1) * 4 * step_t), w_d, 1, 1).astype(BF16)
+            h_k = lax.all_gather(h_own[k], PLANE, axis=0, tiled=True)
+            gate_f32 = dot(h_k, w_g, 1, 0)
+            up_f32 = dot(h_k, w_u, 1, 0)
+            act_k, act_pull = jax.vjp(gated, gate_f32, up_f32)
+            d_gate, d_up = act_pull(d_act)
+            act_k, d_gate, d_up = lax.optimization_barrier((act_k, d_gate.astype(BF16), d_up.astype(BF16)))
+            d_h_part = dot(d_gate, w_g, 1, 1) + dot(d_up, w_u, 1, 1)
+            d_hs.append(lax.psum_scatter(d_h_part, PLANE, scatter_dimension=0, tiled=True).astype(BF16))
+            hs.append(h_k)
+            acts.append(act_k)
+            d_gates.append(d_gate)
+            d_ups.append(d_up)
+        d_h_two = jnp.concatenate(d_hs)
+        y_sums = []
+        for k in range(CHUNKS):
+            y_part = dot(acts[k], w_d, 1, 0)
+            y_sums.append(lax.psum_scatter(y_part, PLANE, scatter_dimension=0, tiled=True))
+        y_sum, resid_y = lax.optimization_barrier((jnp.concatenate(y_sums), resid_bf))
         layer_out = (resid_y.astype(F32) + y_sum).astype(BF16)
+        h_all, act, d_gate, d_up = (jnp.concatenate(v) for v in (hs, acts, d_gates, d_ups))
 
         def reduce_xc(part, c_dim, x_dim):
             keep = lax.dynamic_index_in_dim(part, c_i, c_dim, keepdims=False)

time: 1010 us -> 1070 us (1.059)
  matrix products: 274 us -> 306 us
  local copies, waits for them, and re-layouts: 144 us -> 161 us
  waiting for transfers between devices: 376 us -> 390 us
    ppermute x15, waiting for transfers between devices: 221 us -> 286 us  [flip(): return lax.ppermute(a, axis, [(0, 1), (1, 0)])]
    reduce_scatter x1 -> x2, waiting for transfers between devices: 43.8 us -> 0.04 us  [step(): lax.psum_scatter(d_h_part, PLANE, scatter_dimension=0, tiled=True)]
    dot_general x17 -> x23, matrix products: 234 us -> 266 us  [dot(): lax.dot_general(a, b, (((ca,), (cb,)), ((), ())), preferred_element_type=...]
    all_gather x1 -> x2, waiting for transfers between devices: 0.01 us -> 13.5 us  [step(): h_k = lax.all_gather(h_own[k], PLANE, axis=0, tiled=True)]
    concatenate x0 -> x2, other arithmetic: none -> 12 us  [the longest x1 9.79 us: step(): jnp.concatenate(v)]
    unnamed x166 -> x185, local copies, waits for them, and re-layouts: 22.4 us -> 26 us
  transfers between devices with their start and end apart: 27 -> 30, of which waited for: 9 -> 11; matrix products, arithmetic and copies ran while one was open for 37% -> 49% of each run, Pallas kernels for 4% -> 3%
where the time goes in v3:
time: 1070 us; the launch traced here: 1060 us
  waiting for transfers between devices  390 us (36%)
  matrix products  306 us (29%)
  local copies, waits for them, and re-layouts  161 us (15%)
  other arithmetic  89.6 us (8%)
  Pallas kernels  36.7 us (3%)
  blocking collectives  33.6 us (3%)
  starting transfers between devices  28.4 us (3%)
  between operations  16.5 us (2%)
    ppermute x15, waiting for transfers between devices, flip(): return lax.ppermute(a, axis, [(0, 1), (1, 0)])  286 us
    dot_general x23, matrix products, dot(): lax.dot_general(a, b, (((ca,), (cb,)), ((), ())), preferred_element_type=...  266 us
    pallas_call x1, Pallas kernels, row_sums(): pl.pallas_call(row_sum_kernel, out_shape=jax.ShapeDtypeStruct((rows_dev,...  36.7 us
    all_to_all x1, waiting for transfers between devices, step(): lax.all_to_all(jnp.stack([g_gate, g_up], axis=1), PLANE, 0, 0, tiled=True)  35.5 us
    all_gather x1, blocking collectives, step(): small = lax.all_gather(small, ALL, axis=0, tiled=True)  33.6 us
    dynamic_update_slice x12, local copies, waits for them, and re-layouts, place_xc(): buf = lax.dynamic_update_slice(buf, piece, at(px, pc))  29.6 us
    unnamed x185, local copies, waits for them, and re-layouts  26 us
    all_to_all x1, waiting for transfers between devices, step(): d_got = lax.all_to_all(d_slot, ALL, 0, 0, tiled=True)  25.6 us
  transfers between devices with their start and end apart: 30, of which 11 were waited for; matrix products, arithmetic and copies ran while one was open for 49% of the time, Pallas kernels for 3%

profile of v3, /device:TPU:0, one launch (start us, length us, event | category | flops | bytes accessed | tf_op | source)
XLA Modules:
  0.0 1063.0 jit_solution(14351343484809636776)
XLA Ops:
  14.2 5.5 all-to-all-start.2
  19.8 33.6 %all-gather.1 = f32[16,1,704]{2,1,0:T(1,128)S(1)} all-gather(f32[1,1,704]{2,1,0:T(1,128)S(1)} %maximum_bitcast_fusion.3), channel_id=1, replica_groups=mesh['z'=2,'y'=2,'x'=2,'c'=2] {'z','y','x','c'}, dimensions={0}, use_global_device_ids=true | all-gather | bytes 47872 | tf_op jit(solution)/shard_map/all_gather | solution.py:127
  53.5 4.2 and_reduce_fusion
  59.2 21.0 %gather_fusion.2 = bf16[768,1536]{1,0:T(8,128)(2,1)} fusion(bf16[9496,1536]{1,0:T(8,128)(2,1)} %param.18, s32[1024]{0:T(1024)S(1)} %pad_clamp_fusion.1), kind=kCustom, calls=%fused_computation.2 | custom fusion | bytes 4721664 | tf_op jit(solution)/shard_map/gather | solution.py:156
  89.3 24.7 %all-to-all-done = bf16[16,48,1536]{2,1,0:T(8,128)(2,1)} async-done(((bf16[16,48,1536]{2,1,0:T(8,128)(2,1)}), bf16[16,48,1536]{2,1,0:T(8,128)(2,1)}, u32[]{:S(2)}, u32[]{:S(2)}) %all-to-all-start) | async-done | bytes 2359328 | tf_op jit(solution)/shard_map/all_to_all | solution.py:157
  114.0 4.6 all-to-all-start.1
  121.9 5.1 conditional.2
  138.9 4.2 all-to-all-done.1
  143.2 3.6 broadcast.379.clone
  148.1 3.6 broadcast.379.clone.1
  154.5 13.3 %collective-permute-done.37 = bf16[560,1536]{1,0:T(8,128)(2,1)} collective-permute-done((bf16[560,1536]{1,0:T(8,128)(2,1)}, bf16[560,1536]{1,0:T(8,128)(2,1)}, u32[]{:S(2)}, u32[]{:S(2)}) %collective-permute-start.37) | collective-permute-done | bytes 1720352 | tf_op jit(solution)/shard_map/ppermute | solution.py:63
  173.9 31.9 %collective-permute-done.34 = bf16[4,96,2240]{2,1,0:T(8,128)(2,1)} collective-permute-done((bf16[4,96,2240]{2,1,0:T(8,128)(2,1)}, bf16[4,96,2240]{2,1,0:T(8,128)(2,1)}, u32[]{:S(2)}, u32[]{:S(2)}) %collective-permute-start.34) | collective-permute-done | bytes 1720352 | tf_op jit(solution)/shard_map/ppermute | solution.py:63
  205.7 36.4 %collective-permute-done.31 = bf16[4,96,2240]{2,1,0:T(8,128)(2,1)} collective-permute-done((bf16[4,96,2240]{2,1,0:T(8,128)(2,1)}, bf16[4,96,2240]{2,1,0:T(8,128)(2,1)}, u32[]{:S(2)}, u32[]{:S(2)}) %collective-permute-start.31) | collective-permute-done | bytes 1720352 | tf_op jit(solution)/shard_map/ppermute | solution.py:63
  252.0 5.6 fusion.55
  284.4 3.8 fusion.99
  288.2 5.9 fusion.83
  306.0 3.5 copy.252
  313.0 11.9 %convolution_convert_fusion = bf16[2240,1024]{1,0:T(8,128)(2,1)} fusion(bf16[2240,1536]{1,0:T(8,128)(2,1)} %bitcast.72, bf16[1024,1536]{1,0:T(8,128)(2,1)S(1)} %bitcast.453), kind=kOutput, calls=%fused_computation.125 | convolution fusion | flops 7048724480 | bytes 14614528 | tf_op jit(solution)/shard_map/dot_general | solution.py:59
  325.0 13.5 %all-gather.11.cloned.1.call-done = bf16[1024,1536]{1,0:T(8,128)(2,1)} async-done(((bf16[256,1536]{1,0:T(8,128)(2,1)}), bf16[1024,1536]{1,0:T(8,128)(2,1)}) %all-gather.11.cloned.1.call-update) | async-done | bytes 3145744 | tf_op jit(solution)/shard_map/all_gather | solution.py:210
  338.5 13.3 %fusion.171 = f32[1024,2240]{0,1:T(8,128)} fusion(bf16[1024,1536]{1,0:T(8,128)(2,1)} %all-gather.11.cloned.1.call-done, bf16[1536,2240]{1,0:T(8,128)(2,1)} %bitcast.67), kind=kOutput, calls=%fused_computation.334 | convolution fusion | flops 7046430720 | bytes 19202048 | tf_op jit(solution)/shard_map/dot_general | solution.py:59
  351.8 20.2 %fusion.36 = (bf16[1024,2240]{0,1:T(8,128)(2,1)}, bf16[1024,2240]{0,1:T(8,128)(2,1)}, bf16[1024,2240]{0,1:T(8,128)(2,1)}) fusion(f32[1024,2240]{0,1:T(8,128)} %fusion.171, bf16[2240,1024]{1,0:T(8,128)(2,1)} %convolution_convert_fusion, bf16[1024,1536]{1,0:T(8,128)(2,1)S(1)} %copy-done.31, bf16[1536,2240]{1,0:T(8,128)(2,1)} %bitcast.54), kind=kOutput, calls=%fused_computation.93 | convolution fusion | flops 7085424640 | bytes 37552128 | tf_op jit(solution)/shard_map/dot_general | solution.py:59
  372.1 11.6 %fusion.174 = f32[1024,1536]{1,0:T(8,128)S(1)} fusion(bf16[1024,2240]{0,1:T(8,128)(2,1)} %get-tuple-element.83, bf16[1536,2240]{1,0:T(8,128)(2,1)} %bitcast.67), kind=kOutput, calls=%fused_computation.337 | convolution fusion | flops 7046430720 | bytes 17760256 | tf_op jit(solution)/shard_map/dot_general | solution.py:59
  383.7 11.7 %convolution_add_fusion = f32[1024,1536]{1,0:T(8,128)} fusion(f32[1024,1536]{1,0:T(8,128)S(1)} %fusion.174, bf16[1024,2240]{0,1:T(8,128)(2,1)S(1)} %copy-done.95, bf16[1536,2240]{1,0:T(8,128)(2,1)} %bitcast.54), kind=kOutput, calls=%fused_computation.138 | convolution fusion | flops 7048003584 | bytes 24051712 | tf_op jit(solution)/shard_map/dot_general | solution.py:59
  397.3 12.8 %convolution_convert_fusion.1 = bf16[2240,1024]{1,0:T(8,128)(2,1)} fusion(bf16[2240,1536]{1,0:T(8,128)(2,1)} %bitcast.72, bf16[1024,1536]{1,0:T(8,128)(2,1)S(1)} %bitcast.452), kind=kOutput, calls=%fused_computation.126 | convolution fusion | flops 7048724480 | bytes 14614528 | tf_op jit(solution)/shard_map/dot_general | solution.py:59
  410.2 13.7 %fusion.169 = f32[1024,2240]{0,1:T(8,128)} fusion(bf16[1024,1536]{1,0:T(8,128)(2,1)} %all-gather.9.cloned.1.call-done, bf16[1536,2240]{1,0:T(8,128)(2,1)} %bitcast.67), kind=kOutput, calls=%fused_computation.332 | convolution fusion | flops 7046430720 | bytes 19202048 | tf_op jit(solution)/shard_map/dot_general | solution.py:59
  423.9 20.7 %fusion.33 = (bf16[1024,2240]{0,1:T(8,128)(2,1)}, bf16[1024,2240]{0,1:T(8,128)(2,1)}, bf16[1024,2240]{0,1:T(8,128)(2,1)}) fusion(f32[1024,2240]{0,1:T(8,128)} %fusion.169, bf16[2240,1024]{1,0:T(8,128)(2,1)} %convolution_convert_fusion.1, bf16[1024,1536]{1,0:T(8,128)(2,1)S(1)} %copy-done.33, bf16[1536,2240]{1,0:T(8,128)(2,1)} %bitcast.54), kind=kOutput, calls=%fused_computation.90 | convolution fusion | flops 7085424640 | bytes 37552128 | tf_op jit(solution)/shard_map/dot_general | solution.py:59
  444.6 11.4 %fusion.173 = f32[1024,1536]{1,0:T(8,128)S(1)} fusion(bf16[1024,2240]{0,1:T(8,128)(2,1)} %get-tuple-element.81, bf16[1536,2240]{1,0:T(8,128)(2,1)} %bitcast.67), kind=kOutput, calls=%fused_computation.336 | convolution fusion | flops 7046430720 | bytes 17760256 | tf_op jit(solution)/shard_map/dot_general | solution.py:59
  456.0 11.9 %convolution_add_fusion.1 = f32[1024,1536]{1,0:T(8,128)} fusion(f32[1024,1536]{1,0:T(8,128)S(1)} %fusion.173, bf16[1024,2240]{0,1:T(8,128)(2,1)S(1)} %copy-done.96, bf16[1536,2240]{1,0:T(8,128)(2,1)} %bitcast.54), kind=kOutput, calls=%fused_computation.139 | convolution fusion | flops 7048003584 | bytes 24051712 | tf_op jit(solution)/shard_map/dot_general | solution.py:59
  468.0 13.0 %fusion.172 = f32[1024,1536]{1,0:T(8,128)} fusion(bf16[1024,2240]{0,1:T(8,128)(2,1)} %get-tuple-element.77, bf16[2240,1536]{1,0:T(8,128)(2,1)} %bitcast.72), kind=kOutput, calls=%fused_computation.335 | convolution fusion | flops 7046430720 | bytes 17760256 | tf_op jit(solution)/shard_map/dot_general | solution.py:59
  481.0 13.0 %fusion.170 = f32[1024,1536]{1,0:T(8,128)} fusion(bf16[1024,2240]{0,1:T(8,128)(2,1)} %get-tuple-element.76, bf16[2240,1536]{1,0:T(8,128)(2,1)} %bitcast.72), kind=kOutput, calls=%fused_computation.333 | convolution fusion | flops 7046430720 | bytes 17760256 | tf_op jit(solution)/shard_map/dot_general | solution.py:59
  495.4 9.8 pad_maximum_fusion
  505.2 17.1 %fusion.176 = f32[2,2,560,1536]{3,2,1,0:T(8,128)S(1)} fusion(bf16[2,2,560,2048]{3,2,1,0:T(8,128)(2,1)} %bitcast.444, bf16[2048,1536,1,1]{1,0,3,2:T(8,128)(2,1)S(1)} %bitcast.438), kind=kOutput, calls=%fused_computation.339 | convolution fusion | flops 14092861440 | bytes 29229056 | tf_op jit(solution)/shard_map/dot_general | solution.py:59
  522.4 3.6 dynamic-slice_bitcast_fusion.17
  526.0 4.3 copy-done.9
  532.4 20.2 %fusion.41 = f32[1536,2240]{1,0:T(8,128)S(1)} fusion(bf16[2048,1536]{1,0:T(8,128)(2,1)S(1)} %constant_dynamic-update-slice_fusion.16, bf16[1024,2240]{0,1:T(8,128)(2,1)} %get-tuple-element.83, bf16[1024,2240]{0,1:T(8,128)(2,1)} %get-tuple-element.81), kind=kOutput, calls=%fused_computation.98 | convolution fusion | flops 14111211520 | bytes 29229056 | tf_op jit(solution)/shard_map/dot_general | solution.py:59
  552.6 3.7 dynamic-slice_bitcast_fusion.15
  556.3 3.9 copy-done.7
  567.7 5.1 fusion.175
  572.8 20.0 %fusion.37 = f32[1536,2240]{1,0:T(8,128)S(1)} fusion(bf16[2048,1536]{1,0:T(8,128)(2,1)} %copy-done.37, bf16[1024,2240]{0,1:T(8,128)(2,1)} %get-tuple-element.82, bf16[1024,2240]{0,1:T(8,128)(2,1)} %get-tuple-element.80), kind=kOutput, calls=%fused_computation.94 | convolution fusion | flops 14111211520 | bytes 29229056 | tf_op jit(solution)/shard_map/dot_general | solution.py:59
  596.3 4.1 copy-done.8
  600.7 5.0 fusion.88
  606.6 10.1 fusion.29
  616.7 11.0 %fusion.126 = f32[1,512,2,128]{3,1,2,0:T(8,128)S(1)} fusion(bf16[2,6,512,512]{2,3,1,0:T(8,128)(2,1)} %get-tuple-element.229, f32[2,6,512]{2,1,0:T(8,128)S(1)} %neg.22, f32[2,6,512]{2,1,0:T(8,128)S(1)} %copy-done.70, pred[512,512]{0,1:T(8,128)(4,1)S(1)} %copy-done.27, f32[2,512,512,6]{2,1,3,0:T(8,128)} %copy-done.2, f32[2,6,512]{2,1,0:T(8,128)S(1)} %copy-done.65, ...), kind=kOutput, calls=%fused_computation.225 | convolution fusion | flops 837025792 | bytes 21307392 | tf_op jit(solution)/shard_map/transpose(jvp(bqkgd,bskd->bkgqs))/dot_general | solution.py:45
  627.8 8.0 bitcast_convert_fusion
  635.8 4.2 fusion.114
  645.6 8.3 fusion.130
  654.0 6.2 bitcast_add_fusion.1
  662.4 6.2 bitcast_add_fusion.2
  672.5 9.4 bitcast_add_fusion.3
  681.8 4.2 dynamic-slice_bitcast_fusion.20
  686.2 77.9 %collective-permute-done.42 = f32[4,96,2240]{2,1,0:T(8,128)} collective-permute-done((f32[4,96,2240]{2,1,0:T(8,128)}, f32[4,96,2240]{2,1,0:T(8,128)}, u32[]{:S(2)}, u32[]{:S(2)}) %collective-permute-start.42) | collective-permute-done | bytes 3440672 | tf_op jit(solution)/shard_map/ppermute | solution.py:63
  766.4 100.4 %collective-permute-done.40 = f32[4,96,2240]{2,1,0:T(8,128)} collective-permute-done((f32[4,96,2240]{2,1,0:T(8,128)}, f32[4,96,2240]{2,1,0:T(8,128)}, u32[]{:S(2)}, u32[]{:S(2)}) %collective-permute-start.40) | collective-permute-done | bytes 3440672 | tf_op jit(solution)/shard_map/ppermute | solution.py:63
  871.6 5.0 all-to-all-start.4
  876.7 8.4 fusion.78
  890.5 35.5 %all-to-all-done.4 = bf16[4,2,96,2240]{3,2,1,0:T(8,128)(2,1)} async-done(((bf16[4,2,96,2240]{3,2,1,0:T(8,128)(2,1)}), bf16[4,2,96,2240]{3,2,1,0:T(8,128)(2,1)}, u32[]{:S(2)}, u32[]{:S(2)}) %all-to-all-start.4) | async-done | bytes 3440672 | tf_op jit(solution)/shard_map/all_to_all | solution.py:247
  926.0 3.7 all-to-all-start.3
  929.8 3.8 sort.15
  933.7 26.5 %collective-permute-done.44 = f32[560,1536]{1,0:T(8,128)} collective-permute-done((f32[560,1536]{1,0:T(8,128)}, f32[560,1536]{1,0:T(8,128)}, u32[]{:S(2)}, u32[]{:S(2)}) %collective-permute-start.44) | collective-permute-done | bytes 3440672 | tf_op jit(solution)/shard_map/ppermute | solution.py:63
  960.3 4.7 fusion.71
  973.8 4.1 squeeze.119
  980.5 4.1 squeeze.118
  984.6 25.6 %all-to-all-done.3 = f32[16,48,1536]{2,1,0:T(8,128)} async-done(((f32[16,48,1536]{2,1,0:T(8,128)}), f32[16,48,1536]{2,1,0:T(8,128)}, u32[]{:S(2)}, u32[]{:S(2)}) %all-to-all-start.3) | async-done | bytes 4718624 | tf_op jit(solution)/shard_map/all_to_all | solution.py:266
  1010.3 38.7 %conditional.3 = (bf16[9496,1536]{1,0:T(8,128)(2,1)}) conditional(s32[]{:T(128)} %convert_element_type.240, (s32[76,768]{1,0:T(8,128)S(1)}, f32[16,48,1536]{2,1,0:T(8,128)}, s32[768]{0:T(1024)S(1)}, s32[768]{0:T(1024)S(1)}) %tuple.39, (s32[]{:T(128)}, s32[16,512]{1,0:T(8,128)S(1)}, s32[16,512]{1,0:T(8,128)S(1)}, ...), branch_computations={%region_25.27_spmd, %region_27.29_spmd} | conditional | flops 40000057344 | bytes 372815168 | solution.py:281
  1010.9 36.7 %branch_0_fun.1 = bf16[9496,1536]{1,0:T(8,128)(2,1)} custom-call(s32[76]{0:T(128)} %reduce_sum.90.start_ref, s32[768]{0:T(1024)S(1)} %get-tuple-element.44.slot_ref, s32[768]{0:T(1024)S(1)} %get-tuple-element.45.row_ref, f32[768,1536]{1,0:T(8,128)} %bitcast.17.recv_ref), custom_call_target="tpu_custom_call" | custom-call | flops 40000000000 | bytes 40000000 | tf_op jit(solution)/shard_map/cond/branch_0_fun/pallas_call | solution.py:82
  (358 shorter events, 160.3 us)
Async XLA Ops:
  7.2 244.8 %all-gather.7.cloned.1.call-start = ((), (), s32[]{:S(2)}) async-start(), calls=%async_computation.11 | async-start | bytes 11698176 | tf_op jit(solution)/shard_map/all_gather | solution.py:173
  14.2 66.1 %all-to-all-start.2 = ((bf16[4,96,2240]{2,1,0:T(8,128)(2,1)}), bf16[4,96,2240]{2,1,0:T(8,128)(2,1)S(1)}, u32[]{:S(2)}, u32[]{:S(2)}) async-start(bf16[4,96,2240]{2,1,0:T(8,128)(2,1)} %pad_maximum_fusion.5), calls=%async_computation.2 | async-start | bytes 3538944 | tf_op jit(solution)/shard_map/all_to_all | solution.py:185
  57.9 64.0 %copy-start.59 = (s32[16,512]{1,0:T(8,128)}, s32[16,512]{1,0:T(8,128)S(1)}, u32[]{:S(2)}) copy-start(s32[16,512]{1,0:T(8,128)S(1)} %get-tuple-element.165) | copy-start | bytes 98308
  58.2 63.7 %copy-start.57 = (s32[16,512]{1,0:T(8,128)}, s32[16,512]{1,0:T(8,128)S(1)}, u32[]{:S(2)}) copy-start(s32[16,512]{1,0:T(8,128)S(1)} %broadcast_subtract_fusion) | copy-start | bytes 98308
  58.6 21.6 %copy-start.71 = (s32[16,48]{1,0:T(8,128)}, s32[16,48]{1,0:T(8,128)S(1)}, u32[]{:S(2)}) copy-start(s32[16,48]{1,0:T(8,128)S(1)} %select_reduce_fusion) | copy-start | bytes 9220
  59.1 21.1 %copy-start.82 = (pred[16,48]{1,0:T(8,128)(4,1)}, pred[16,48]{1,0:T(8,128)(4,1)S(1)}, u32[]{:S(2)}) copy-start(pred[16,48]{1,0:T(8,128)(4,1)S(1)} %fusion.105) | copy-start | bytes 2308
  80.2 9.0 copy-start.14
  80.2 33.7 %all-to-all-start = ((bf16[16,48,1536]{2,1,0:T(8,128)(2,1)}), bf16[16,48,1536]{2,1,0:T(8,128)(2,1)}, u32[]{:S(2)}, u32[]{:S(2)}) async-start(bf16[16,48,1536]{2,1,0:T(8,128)(2,1)} %bitcast.26), calls=%async_computation | async-start | bytes 4718592 | tf_op jit(solution)/shard_map/all_to_all | solution.py:157
  86.1 32.7 %copy-start.88 = (s32[512]{0:T(512)}, s32[512]{0:T(512)S(1)}, u32[]{:S(2)}) copy-start(s32[512]{0:T(512)S(1)} %select_reduce_fusion.1) | copy-start | bytes 6148
  114.0 29.1 %all-to-all-start.1 = ((bf16[4,96,2240]{2,1,0:T(8,128)(2,1)}), bf16[4,96,2240]{2,1,0:T(8,128)(2,1)}, u32[]{:S(2)}, u32[]{:S(2)}) async-start(bf16[4,96,2240]{2,1,0:T(8,128)(2,1)} %pad_maximum_fusion.4), calls=%async_computation.1 | async-start | bytes 3538944 | tf_op jit(solution)/shard_map/all_to_all | solution.py:185
  118.6 187.4 %all-gather.13.cloned.1.call-start = ((), (), s32[]{:S(2)}) async-start(), calls=%async_computation.20 | async-start | bytes 7864320 | tf_op jit(solution)/shard_map/all_gather | solution.py:176
  127.1 46.8 %copy-start.80 = (f32[512]{0:T(512)}, f32[512]{0:T(512)S(1)}, u32[]{:S(2)}) copy-start(f32[512]{0:T(512)S(1)} %get-tuple-element.75) | copy-start | bytes 6148
  127.1 124.9 %copy-start.10 = (f32[512,1536]{1,0:T(8,128)}, f32[512,1536]{1,0:T(8,128)S(1)}, u32[]{:S(2)}) copy-start(f32[512,1536]{1,0:T(8,128)S(1)} %get-tuple-element.74) | copy-start | bytes 9437188
  127.1 40.7 %collective-permute-start.37 = (bf16[560,1536]{1,0:T(8,128)(2,1)}, bf16[560,1536]{1,0:T(8,128)(2,1)}, u32[]{:S(2)}, u32[]{:S(2)}) collective-permute-start(bf16[560,1536]{1,0:T(8,128)(2,1)} %param.27), channel_id=1, source_target_pairs={{0,2},{2,0},{1,3},{3,1},{4,6},{6,4},{5,7},{7,5},{8,10},{10,8},{9,1... | collective-permute-start | bytes 5160968 | tf_op jit(solution)/shard_map/ppermute | solution.py:63
  128.2 39.6 %collective-permute-start.36 = (bf16[560,1536]{1,0:T(8,128)(2,1)}, bf16[560,1536]{1,0:T(8,128)(2,1)}, u32[]{:S(2)}, u32[]{:S(2)}) collective-permute-start(bf16[560,1536]{1,0:T(8,128)(2,1)} %param.27), channel_id=1, source_target_pairs={{0,1},{1,0},{2,3},{3,2},{4,5},{5,4},{6,7},{7,6},{8,9},{9,8},{10,11... | collective-permute-start | bytes 5160968 | tf_op jit(solution)/shard_map/ppermute | solution.py:63
  128.3 210.2 %all-gather.11.cloned.1.call-start = ((), (), s32[]{:S(2)}) async-start(), calls=%async_computation.14 | async-start | bytes 3932160 | tf_op jit(solution)/shard_map/all_gather | solution.py:210
  135.0 159.1 %copy-start.66 = (f32[1536]{0:T(1024)}, f32[1536]{0:T(1024)S(1)}, u32[]{:S(2)}) copy-start(f32[1536]{0:T(1024)S(1)} %mul.533) | copy-start | bytes 18436
  135.1 116.9 %copy-start.78 = (f32[1536]{0:T(1024)}, f32[1536]{0:T(1024)S(1)}, u32[]{:S(2)}) copy-start(f32[1536]{0:T(1024)S(1)} %mul.509) | copy-start | bytes 18436
  137.7 144.6 %copy-start.26 = (pred[512,512]{0,1:T(8,128)(4,1)}, pred[512,512]{0,1:T(8,128)(4,1)S(1)}, u32[]{:S(2)}) copy-start(pred[512,512]{0,1:T(8,128)(4,1)S(1)} %iota_compare_fusion.4) | copy-start | bytes 786436
  137.7 68.0 %collective-permute-start.34 = (bf16[4,96,2240]{2,1,0:T(8,128)(2,1)}, bf16[4,96,2240]{2,1,0:T(8,128)(2,1)}, u32[]{:S(2)}, u32[]{:S(2)}) collective-permute-start(bf16[4,96,2240]{2,1,0:T(8,128)(2,1)} %copy-done.14), channel_id=1, source_target_pairs={{0,2},{2,0},{1,3},{3,1},{4,6},{6,4},{5,7},{7,5},{8,10},{10,8},{9,1... | collective-permute-start | bytes 5160968 | tf_op jit(solution)/shard_map/ppermute | solution.py:63
  138.6 103.5 %collective-permute-start.33 = (bf16[4,96,2240]{2,1,0:T(8,128)(2,1)}, bf16[4,96,2240]{2,1,0:T(8,128)(2,1)}, u32[]{:S(2)}, u32[]{:S(2)}) collective-permute-start(bf16[4,96,2240]{2,1,0:T(8,128)(2,1)} %copy-done.14), channel_id=1, source_target_pairs={{0,1},{1,0},{2,3},{3,2},{4,5},{5,4},{6,7},{7,6},{8,9},{9,8},{10,11... | collective-permute-start | bytes 5160968 | tf_op jit(solution)/shard_map/ppermute | solution.py:63
  143.1 99.1 %collective-permute-start.31 = (bf16[4,96,2240]{2,1,0:T(8,128)(2,1)}, bf16[4,96,2240]{2,1,0:T(8,128)(2,1)}, u32[]{:S(2)}, u32[]{:S(2)}) collective-permute-start(bf16[4,96,2240]{2,1,0:T(8,128)(2,1)} %all-to-all-done.1), channel_id=1, source_target_pairs={{0,2},{2,0},{1,3},{3,1},{4,6},{6,4},{5,7},{7,5},{8,10},{10,8},{9,1... | collective-permute-start | bytes 5160968 | tf_op jit(solution)/shard_map/ppermute | solution.py:63
  167.8 80.0 %collective-permute-start.30 = (bf16[4,96,2240]{2,1,0:T(8,128)(2,1)}, bf16[4,96,2240]{2,1,0:T(8,128)(2,1)S(1)}, u32[]{:S(2)}, u32[]{:S(2)}) collective-permute-start(bf16[4,96,2240]{2,1,0:T(8,128)(2,1)} %all-to-all-done.1), channel_id=1, source_target_pairs={{0,1},{1,0},{2,3},{3,2},{4,5},{5,4},{6,7},{7,6},{8,9},{9,8},{10,11... | collective-permute-start | bytes 5160968 | tf_op jit(solution)/shard_map/ppermute | solution.py:63
  167.8 129.4 %collective-permute-start.38 = (bf16[560,1536]{1,0:T(8,128)(2,1)}, bf16[560,1536]{1,0:T(8,128)(2,1)}, u32[]{:S(2)}, u32[]{:S(2)}) collective-permute-start(bf16[560,1536]{1,0:T(8,128)(2,1)} %collective-permute-done.37), channel_id=1, source_target_pairs={{0,1},{1,0},{2,3},{3,2},{4,5},{5,4},{6,7},{7,6},{8,9},{9,8},{10,11... | collective-permute-start | bytes 5160968 | tf_op jit(solution)/shard_map/ppermute | solution.py:63
  173.9 78.1 %copy-start.86 = (f32[512]{0:T(512)}, f32[512]{0:T(512)S(1)}, u32[]{:S(2)}) copy-start(f32[512]{0:T(512)S(1)} %fusion.146) | copy-start | bytes 6148
  205.7 94.3 %collective-permute-start.35 = (bf16[4,96,2240]{2,1,0:T(8,128)(2,1)}, bf16[4,96,2240]{2,1,0:T(8,128)(2,1)}, u32[]{:S(2)}, u32[]{:S(2)}) collective-permute-start(bf16[4,96,2240]{2,1,0:T(8,128)(2,1)} %collective-permute-done.34), channel_id=1, source_target_pairs={{0,1},{1,0},{2,3},{3,2},{4,5},{5,4},{6,7},{7,6},{8,9},{9,8},{10,11... | collective-permute-start | bytes 5160968 | tf_op jit(solution)/shard_map/ppermute | solution.py:63
  242.1 60.8 %collective-permute-start.32 = (bf16[4,96,2240]{2,1,0:T(8,128)(2,1)}, bf16[4,96,2240]{2,1,0:T(8,128)(2,1)}, u32[]{:S(2)}, u32[]{:S(2)}) collective-permute-start(bf16[4,96,2240]{2,1,0:T(8,128)(2,1)} %collective-permute-done.31), channel_id=1, source_target_pairs={{0,1},{1,0},{2,3},{3,2},{4,5},{5,4},{6,7},{7,6},{8,9},{9,8},{10,11... | collective-permute-start | bytes 5160968 | tf_op jit(solution)/shard_map/ppermute | solution.py:63
  270.1 9.5 copy-start.16
  297.0 113.2 %all-gather.9.cloned.1.call-start = ((), (), s32[]{:S(2)}) async-start(), calls=%async_computation.12 | async-start | bytes 3932160 | tf_op jit(solution)/shard_map/all_gather | solution.py:210
  325.0 235.3 %reduce-scatter.13.cloned.1.call-start = ((), (), s32[]{:S(2)}) async-start(), calls=%async_computation.17 | async-start | bytes 7864320 | tf_op jit(solution)/shard_map/reduce_scatter | solution.py:217
  338.5 13.3 %copy-start.31 = (bf16[1024,1536]{1,0:T(8,128)(2,1)S(1)}, bf16[1024,1536]{1,0:T(8,128)(2,1)}, u32[]{:S(2)}) copy-start(bf16[1024,1536]{1,0:T(8,128)(2,1)} %all-gather.11.cloned.1.call-done) | copy-start | bytes 9437188
  372.1 11.6 %copy-start.95 = (bf16[1024,2240]{0,1:T(8,128)(2,1)S(1)}, bf16[1024,2240]{0,1:T(8,128)(2,1)}, u32[]{:S(2)}) copy-start(bf16[1024,2240]{0,1:T(8,128)(2,1)} %get-tuple-element.82) | copy-start | bytes 13762564
  395.5 166.5 %reduce-scatter.11.cloned.1.call-start = ((), (), s32[]{:S(2)}) async-start(), calls=%async_computation.16 | async-start | bytes 7864320 | tf_op jit(solution)/shard_map/reduce_scatter | solution.py:217
  410.1 13.7 %copy-start.33 = (bf16[1024,1536]{1,0:T(8,128)(2,1)S(1)}, bf16[1024,1536]{1,0:T(8,128)(2,1)}, u32[]{:S(2)}) copy-start(bf16[1024,1536]{1,0:T(8,128)(2,1)} %all-gather.9.cloned.1.call-done) | copy-start | bytes 9437188
  444.6 11.4 %copy-start.96 = (bf16[1024,2240]{0,1:T(8,128)(2,1)S(1)}, bf16[1024,2240]{0,1:T(8,128)(2,1)}, u32[]{:S(2)}) copy-start(bf16[1024,2240]{0,1:T(8,128)(2,1)} %get-tuple-element.80) | copy-start | bytes 13762564
  467.9 497.0 %reduce-scatter.9.cloned.1.call-start = ((), (), s32[]{:S(2)}) async-start(), calls=%async_computation.15 | async-start | bytes 7864320 | tf_op jit(solution)/shard_map/reduce_scatter | solution.py:226
  481.0 484.0 %reduce-scatter.7.cloned.1.call-start = ((), (), s32[]{:S(2)}) async-start(), calls=%async_computation.13 | async-start | bytes 7864320 | tf_op jit(solution)/shard_map/reduce_scatter | solution.py:226
  494.0 11.2 %slice-start.3 = ((s8[6291456]{0:T(1024)(128)(4,1)}), s8[2097152]{0:T(1024)(128)(4,1)S(1)}, s32[]{:S(2)}) async-start(s8[6291456]{0:T(1024)(128)(4,1)} %bitcast.436), calls=%async_computation.24 | async-start | bytes 4194304
  494.1 556.8 %reduce-scatter.17.cloned.1.call-start = ((), (), s32[]{:S(2)}) async-start(), calls=%async_computation.19 | async-start | bytes 10027008 | tf_op jit(solution)/shard_map/reduce_scatter | solution.py:253
  495.4 9.8 slice-start.4
  530.3 142.2 %collective-permute-start.43 = (f32[2,560,1536]{2,1,0:T(8,128)}, f32[2,560,1536]{2,1,0:T(8,128)}, u32[]{:S(2)}, u32[]{:S(2)}) collective-permute-start(f32[2,560,1536]{2,1,0:T(8,128)} %dynamic-slice_bitcast_fusion.17), channel_id=1, source_target_pairs={{0,1},{1,0},{2,3},{3,2},{4,5},{5,4},{6,7},{7,6},{8,9},{9,8},{10,11... | collective-permute-start | bytes 20643848 | tf_op jit(solution)/shard_map/ppermute | solution.py:63
  532.4 20.2 %copy-start.37 = (bf16[2048,1536]{1,0:T(8,128)(2,1)}, bf16[2048,1536]{1,0:T(8,128)(2,1)S(1)}, u32[]{:S(2)}) copy-start(bf16[2048,1536]{1,0:T(8,128)(2,1)S(1)} %constant_dynamic-update-slice_fusion.16) | copy-start | bytes 18874372
  560.2 93.7 %collective-permute-start.41 = (f32[4,2,96,2240]{3,2,1,0:T(8,128)}, f32[4,2,96,2240]{3,2,1,0:T(8,128)}, u32[]{:S(2)}, u32[]{:S(2)}) collective-permute-start(f32[4,2,96,2240]{3,2,1,0:T(8,128)} %dynamic-slice_bitcast_fusion.15), channel_id=1, source_target_pairs={{0,1},{1,0},{2,3},{3,2},{4,5},{5,4},{6,7},{7,6},{8,9},{9,8},{10,11... | collective-permute-start | bytes 20643848 | tf_op jit(solution)/shard_map/ppermute | solution.py:63
  572.8 479.9 %reduce-scatter.15.cloned.1.call-start = ((), (), s32[]{:S(2)}) async-start(), calls=%async_computation.18 | async-start | bytes 13369344 | tf_op jit(solution)/shard_map/reduce_scatter | solution.py:258
  600.4 61.9 %collective-permute-start.39 = (f32[4,2,96,2240]{3,2,1,0:T(8,128)}, f32[4,2,96,2240]{3,2,1,0:T(8,128)}, u32[]{:S(2)}, u32[]{:S(2)}) collective-permute-start(f32[4,2,96,2240]{3,2,1,0:T(8,128)} %dynamic-slice_bitcast_fusion.16), channel_id=1, source_target_pairs={{0,1},{1,0},{2,3},{3,2},{4,5},{5,4},{6,7},{7,6},{8,9},{9,8},{10,11... | collective-permute-start | bytes 20643848 | tf_op jit(solution)/shard_map/ppermute | solution.py:63
  606.5 10.2 copy-start.38
  606.5 10.1 copy-start.17
  606.5 10.1 copy-start.19
  606.5 10.1 copy-start.70
  606.5 21.1 %slice-start = ((s8[12582912]{0:T(1024)(128)(4,1)}), s8[4194304]{0:T(1024)(128)(4,1)S(1)}, s32[]{:S(2)}) async-start(s8[12582912]{0:T(1024)(128)(4,1)} %bitcast.433), calls=%async_computation.21 | async-start | bytes 8388608
  616.7 11.0 %slice-start.1 = ((s8[12582912]{0:T(1024)(128)(4,1)}), s8[4194304]{0:T(1024)(128)(4,1)S(1)}, s32[]{:S(2)}) async-start(s8[12582912]{0:T(1024)(128)(4,1)} %bitcast.433), calls=%async_computation.22 | async-start | bytes 8388608
  616.7 11.0 %slice-start.2 = ((s8[12582912]{0:T(1024)(128)(4,1)}), s8[4194304]{0:T(1024)(128)(4,1)S(1)}, s32[]{:S(2)}) async-start(s8[12582912]{0:T(1024)(128)(4,1)} %bitcast.433), calls=%async_computation.23 | async-start | bytes 8388608
  616.7 11.0 %copy-start.54 = (bf16[512,2,64]{2,0,1:T(8,128)(2,1)S(1)}, bf16[512,2,64]{2,0,1:T(8,128)(2,1)}, u32[]{:S(2)}) copy-start(bf16[512,2,64]{2,0,1:T(8,128)(2,1)} %copy-done.53) | copy-start | bytes 393220
  616.7 11.0 %copy-start.56 = (bf16[512,2,64]{2,0,1:T(8,128)(2,1)S(1)}, bf16[512,2,64]{2,0,1:T(8,128)(2,1)}, u32[]{:S(2)}) copy-start(bf16[512,2,64]{2,0,1:T(8,128)(2,1)} %copy-done.55) | copy-start | bytes 393220
  662.1 101.9 %collective-permute-start.42 = (f32[4,96,2240]{2,1,0:T(8,128)}, f32[4,96,2240]{2,1,0:T(8,128)}, u32[]{:S(2)}, u32[]{:S(2)}) collective-permute-start(f32[4,96,2240]{2,1,0:T(8,128)} %dynamic-slice_bitcast_fusion.18), channel_id=1, source_target_pairs={{0,2},{2,0},{1,3},{3,1},{4,6},{6,4},{5,7},{7,5},{8,10},{10,8},{9,1... | collective-permute-start | bytes 10321928 | tf_op jit(solution)/shard_map/ppermute | solution.py:63
  670.7 196.1 %collective-permute-start.40 = (f32[4,96,2240]{2,1,0:T(8,128)}, f32[4,96,2240]{2,1,0:T(8,128)}, u32[]{:S(2)}, u32[]{:S(2)}) collective-permute-start(f32[4,96,2240]{2,1,0:T(8,128)} %dynamic-slice_bitcast_fusion.19), channel_id=1, source_target_pairs={{0,2},{2,0},{1,3},{3,1},{4,6},{6,4},{5,7},{7,5},{8,10},{10,8},{9,1... | collective-permute-start | bytes 10321928 | tf_op jit(solution)/shard_map/ppermute | solution.py:63
  686.1 274.2 %collective-permute-start.44 = (f32[560,1536]{1,0:T(8,128)}, f32[560,1536]{1,0:T(8,128)}, u32[]{:S(2)}, u32[]{:S(2)}) collective-permute-start(f32[560,1536]{1,0:T(8,128)} %dynamic-slice_bitcast_fusion.20), channel_id=1, source_target_pairs={{0,2},{2,0},{1,3},{3,1},{4,6},{6,4},{5,7},{7,5},{8,10},{10,8},{9,1... | collective-permute-start | bytes 10321928 | tf_op jit(solution)/shard_map/ppermute | solution.py:63
  871.6 54.4 %all-to-all-start.4 = ((bf16[4,2,96,2240]{3,2,1,0:T(8,128)(2,1)}), bf16[4,2,96,2240]{3,2,1,0:T(8,128)(2,1)}, u32[]{:S(2)}, u32[]{:S(2)}) async-start(bf16[4,2,96,2240]{3,2,1,0:T(8,128)(2,1)} %copy.194), calls=%async_computation.10 | async-start | bytes 7077888 | tf_op jit(solution)/shard_map/all_to_all | solution.py:247
  876.7 8.4 copy-start.25
  890.5 39.2 %copy-start.72 = (s32[16,48]{1,0:T(8,128)S(1)}, s32[16,48]{1,0:T(8,128)}, u32[]{:S(2)}) copy-start(s32[16,48]{1,0:T(8,128)} %copy-done.71) | copy-start | bytes 9220
  890.5 39.2 %copy-start.83 = (pred[16,48]{1,0:T(8,128)(4,1)S(1)}, pred[16,48]{1,0:T(8,128)(4,1)}, u32[]{:S(2)}) copy-start(pred[16,48]{1,0:T(8,128)(4,1)} %copy-done.82) | copy-start | bytes 2308
  926.0 84.3 %all-to-all-start.3 = ((f32[16,48,1536]{2,1,0:T(8,128)}), f32[16,48,1536]{2,1,0:T(8,128)}, u32[]{:S(2)}, u32[]{:S(2)}) async-start(f32[16,48,1536]{2,1,0:T(8,128)} %select_select_fusion.1), calls=%async_computation.7 | async-start | bytes 9437184 | tf_op jit(solution)/shard_map/all_to_all | solution.py:266
  977.9 32.3 %copy-start.58 = (s32[16,512]{1,0:T(8,128)S(1)}, s32[16,512]{1,0:T(8,128)}, u32[]{:S(2)}) copy-start(s32[16,512]{1,0:T(8,128)} %copy-done.57) | copy-start | bytes 98308
  978.0 32.3 %copy-start.60 = (s32[16,512]{1,0:T(8,128)S(1)}, s32[16,512]{1,0:T(8,128)}, u32[]{:S(2)}) copy-start(s32[16,512]{1,0:T(8,128)} %copy-done.59) | copy-start | bytes 98308
  (57 other events, 250.1 us)
Sparse Core Ops, SparseCore 0:
  11.0 74.0 all-gather.6
  128.4 68.2 all-gather.12
  297.1 41.3 all-gather.10
  340.7 40.0 all-gather.8
  395.6 66.2 reduce-scatter.12
  468.0 65.8 reduce-scatter.10
  536.9 66.2 reduce-scatter.8
  606.2 66.2 reduce-scatter.6
  677.2 109.7 reduce-scatter.16
  791.5 146.2 reduce-scatter.14

commit v4 on v3

--- a/solution.py
+++ b/solution.py
@@ -94,6 +94,42 @@
     )(starts, slots, rows, recv)
 
 
+def flipped(mask):
+    here = [lax.axis_index(n) for n in ALL]
+    return tuple(1 - v if (mask >> (3 - i)) & 1 else v for i, v in enumerate(here))
+
+
+def share_kernel(in_ref, out_ref, send_sem, recv_sem):
+    me = lax.axis_index(ALL)
+    barrier = pltpu.get_barrier_semaphore()
+    for m in range(1, N_DEV):
+        pl.semaphore_signal(barrier, inc=1, device_id=flipped(m), device_id_type=pl.DeviceIdType.MESH)
+    pl.semaphore_wait(barrier, N_DEV - 1)
+    copies = []
+    for m in range(1, N_DEV):
+        copies.append(
+            pltpu.make_async_remote_copy(
+                src_ref=in_ref, dst_ref=out_ref.at[me], send_sem=send_sem.at[m], recv_sem=recv_sem.at[m], device_id=flipped(m), device_id_type=pl.DeviceIdType.MESH
+            )
+        )
+        copies[-1].start()
+    out_ref[me] = in_ref[...]
+    for copy in copies:
+        copy.wait()
+
+
+def share(small):
+    return pl.pallas_call(
+        share_kernel,
+        out_shape=jax.ShapeDtypeStruct((N_DEV,) + small.shape, small.dtype),
+        in_specs=[pl.BlockSpec(memory_space=pltpu.VMEM)],
+        out_specs=pl.BlockSpec(memory_space=pltpu.VMEM),
+        scratch_shapes=[pltpu.SemaphoreType.DMA((N_DEV,)), pltpu.SemaphoreType.DMA((N_DEV,))],
+        compiler_params=pltpu.CompilerParams(collective_id=0, has_side_effects=True),
+        cost_estimate=pl.CostEstimate(flops=20_000_000, bytes_accessed=100_000, transcendentals=0),
+    )(small)
+
+
 def place_xc(pieces, x_i, c_i, shape, at):
     buf = jnp.zeros(shape, pieces[0].dtype)
     for k, piece in enumerate(pieces):
@@ -123,11 +159,12 @@
         me = lax.axis_index(ALL)
         x_i, c_i = lax.axis_index("x"), lax.axis_index("c")
 
-        small = jnp.concatenate([token_ids.astype(F32), gain1.astype(F32)[None], gain2.astype(F32)[None]], axis=1)
-        small = lax.all_gather(small, ALL, axis=0, tiled=True)
+        small = jnp.concatenate([token_ids[0].astype(F32), gain1.astype(F32), gain2.astype(F32), jnp.zeros((1024 - seq - 2 * shard,), F32)])
+        small = share(small.reshape(8, 128))
+        small = small.reshape(N_DEV, 1024)
         ids_all = small[:, :seq].astype(jnp.int32)
         g1_full = small[:, seq : seq + shard].reshape(-1)
-        g2_full = small[:, seq + shard :].reshape(-1)
+        g2_full = small[:, seq + shard : seq + 2 * shard].reshape(-1)
 
         owner = ids_all // rows_dev
         pos = jnp.arange(seq)
@@ -226,7 +263,8 @@
             y_sums.append(lax.psum_scatter(y_part, PLANE, scatter_dimension=0, tiled=True))
         y_sum, resid_y = lax.optimization_barrier((jnp.concatenate(y_sums), resid_bf))
         layer_out = (resid_y.astype(F32) + y_sum).astype(BF16)
-        h_all, act, d_gate, d_up = (jnp.concatenate(v) for v in (hs, acts, d_gates, d_ups))
+        h_all, d_gate, d_up = (jnp.concatenate(v) for v in (hs, d_gates, d_ups))
+        act = jnp.concatenate(acts)
 
         def reduce_xc(part, c_dim, x_dim):
             keep = lax.dynamic_index_in_dim(part, c_i, c_dim, keepdims=False)

time: 1070 us -> 1070 us (level)
  blocking collectives: 33.6 us -> 0 us
  Pallas kernels: 36.7 us -> 64.5 us
    all_gather x1 -> x0, blocking collectives: 33.6 us -> none  [step(): small = lax.all_gather(small, ALL, axis=0, tiled=True)]
    pallas_call x0 -> x1, Pallas kernels: none -> 27.7 us  [share(): pl.pallas_call(share_kernel, out_shape=jax.ShapeDtypeStruct((N_DEV,) + sm...]
  transfers between devices with their start and end apart: 30 -> 30, of which waited for: 11 -> 11; matrix products, arithmetic and copies ran while one was open for 49% -> 50% of each run, Pallas kernels for 3% -> 6%
where the time goes in v4:
time: 1070 us; the launch traced here: 1060 us
  waiting for transfers between devices  391 us (37%)
  matrix products  306 us (29%)
  local copies, waits for them, and re-layouts  161 us (15%)
  other arithmetic  90.3 us (8%)
  Pallas kernels  64.5 us (6%)
  starting transfers between devices  30.4 us (3%)
  between operations  16.5 us (2%)
    ppermute x15, waiting for transfers between devices, flip(): return lax.ppermute(a, axis, [(0, 1), (1, 0)])  285 us
    dot_general x23, matrix products, dot(): lax.dot_general(a, b, (((ca,), (cb,)), ((), ())), preferred_element_type=...  265 us
    pallas_call x1, Pallas kernels, row_sums(): pl.pallas_call(row_sum_kernel, out_shape=jax.ShapeDtypeStruct((rows_dev,...  36.7 us
    all_to_all x1, waiting for transfers between devices, step(): lax.all_to_all(jnp.stack([g_gate, g_up], axis=1), PLANE, 0, 0, tiled=True)  35.5 us
    dynamic_update_slice x12, local copies, waits for them, and re-layouts, place_xc(): buf = lax.dynamic_update_slice(buf, piece, at(px, pc))  29.6 us
    pallas_call x1, Pallas kernels, share(): pl.pallas_call(share_kernel, out_shape=jax.ShapeDtypeStruct((N_DEV,) + sm...  27.7 us
    unnamed x185, local copies, waits for them, and re-layouts  26.9 us
    all_to_all x1, waiting for transfers between devices, step(): d_got = lax.all_to_all(d_slot, ALL, 0, 0, tiled=True)  25.7 us
  transfers between devices with their start and end apart: 30, of which 11 were waited for; matrix products, arithmetic and copies ran while one was open for 50% of the time, Pallas kernels for 6%

profile of v4, /device:TPU:0, one launch (start us, length us, event | category | flops | bytes accessed | tf_op | source)
XLA Modules:
  0.0 1060.8 jit_solution(6394268136737680964)
XLA Ops:
  14.2 5.5 all-to-all-start.2
  20.7 27.7 %shard_map.203 = f32[16,8,128]{2,1,0:T(8,128)} custom-call(f32[8,128]{1,0:T(8,128)} %maximum_bitcast_fusion.3.in_ref), custom_call_target="tpu_custom_call" | custom-call | flops 20000000 | bytes 100000 | tf_op jit(solution)/shard_map/pallas_call | solution.py:122
  49.4 4.2 and_reduce_fusion
  55.1 20.7 %gather_fusion.2 = bf16[768,1536]{1,0:T(8,128)(2,1)} fusion(bf16[9496,1536]{1,0:T(8,128)(2,1)} %param.18, s32[1024]{0:T(1024)S(1)} %pad_clamp_fusion.1), kind=kCustom, calls=%fused_computation.2 | custom fusion | bytes 4721664 | tf_op jit(solution)/shard_map/gather | solution.py:193
  84.6 25.7 %all-to-all-done = bf16[16,48,1536]{2,1,0:T(8,128)(2,1)} async-done(((bf16[16,48,1536]{2,1,0:T(8,128)(2,1)}), bf16[16,48,1536]{2,1,0:T(8,128)(2,1)}, u32[]{:S(2)}, u32[]{:S(2)}) %all-to-all-start) | async-done | bytes 2359328 | tf_op jit(solution)/shard_map/all_to_all | solution.py:194
  110.3 5.1 all-to-all-start.1
  118.7 5.2 conditional.2
  135.7 4.8 all-to-all-done.1
  141.2 3.6 broadcast.379.clone
  146.2 3.6 broadcast.379.clone.1
  152.6 12.0 %collective-permute-done.37 = bf16[560,1536]{1,0:T(8,128)(2,1)} collective-permute-done((bf16[560,1536]{1,0:T(8,128)(2,1)}, bf16[560,1536]{1,0:T(8,128)(2,1)}, u32[]{:S(2)}, u32[]{:S(2)}) %collective-permute-start.37) | collective-permute-done | bytes 1720352 | tf_op jit(solution)/shard_map/ppermute | solution.py:63
  170.7 31.8 %collective-permute-done.34 = bf16[4,96,2240]{2,1,0:T(8,128)(2,1)} collective-permute-done((bf16[4,96,2240]{2,1,0:T(8,128)(2,1)}, bf16[4,96,2240]{2,1,0:T(8,128)(2,1)}, u32[]{:S(2)}, u32[]{:S(2)}) %collective-permute-start.34) | collective-permute-done | bytes 1720352 | tf_op jit(solution)/shard_map/ppermute | solution.py:63
  202.5 36.8 %collective-permute-done.31 = bf16[4,96,2240]{2,1,0:T(8,128)(2,1)} collective-permute-done((bf16[4,96,2240]{2,1,0:T(8,128)(2,1)}, bf16[4,96,2240]{2,1,0:T(8,128)(2,1)}, u32[]{:S(2)}, u32[]{:S(2)}) %collective-permute-start.31) | collective-permute-done | bytes 1720352 | tf_op jit(solution)/shard_map/ppermute | solution.py:63
  249.3 5.6 fusion.55
  281.7 3.8 fusion.99
  285.5 5.9 fusion.83
  303.2 3.5 copy.252
  310.2 11.9 %convolution_convert_fusion = bf16[2240,1024]{1,0:T(8,128)(2,1)} fusion(bf16[2240,1536]{1,0:T(8,128)(2,1)} %bitcast.70, bf16[1024,1536]{1,0:T(8,128)(2,1)S(1)} %bitcast.448), kind=kOutput, calls=%fused_computation.125 | convolution fusion | flops 7048724480 | bytes 14614528 | tf_op jit(solution)/shard_map/dot_general | solution.py:59
  322.2 13.8 %all-gather.10.cloned.1.call-done = bf16[1024,1536]{1,0:T(8,128)(2,1)} async-done(((bf16[256,1536]{1,0:T(8,128)(2,1)}), bf16[1024,1536]{1,0:T(8,128)(2,1)}) %all-gather.10.cloned.1.call-update) | async-done | bytes 3145744 | tf_op jit(solution)/shard_map/all_gather | solution.py:247
  336.0 13.3 %fusion.171 = f32[1024,2240]{0,1:T(8,128)} fusion(bf16[1024,1536]{1,0:T(8,128)(2,1)} %all-gather.10.cloned.1.call-done, bf16[1536,2240]{1,0:T(8,128)(2,1)} %bitcast.65), kind=kOutput, calls=%fused_computation.332 | convolution fusion | flops 7046430720 | bytes 19202048 | tf_op jit(solution)/shard_map/dot_general | solution.py:59
  349.3 20.2 %fusion.36 = (bf16[1024,2240]{0,1:T(8,128)(2,1)}, bf16[1024,2240]{0,1:T(8,128)(2,1)}, bf16[1024,2240]{0,1:T(8,128)(2,1)}) fusion(f32[1024,2240]{0,1:T(8,128)} %fusion.171, bf16[2240,1024]{1,0:T(8,128)(2,1)} %convolution_convert_fusion, bf16[1024,1536]{1,0:T(8,128)(2,1)S(1)} %copy-done.31, bf16[1536,2240]{1,0:T(8,128)(2,1)} %bitcast.52), kind=kOutput, calls=%fused_computation.93 | convolution fusion | flops 7085424640 | bytes 37552128 | tf_op jit(solution)/shard_map/dot_general | solution.py:59
  369.6 11.6 %fusion.174 = f32[1024,1536]{1,0:T(8,128)S(1)} fusion(bf16[1024,2240]{0,1:T(8,128)(2,1)} %get-tuple-element.83, bf16[1536,2240]{1,0:T(8,128)(2,1)} %bitcast.65), kind=kOutput, calls=%fused_computation.335 | convolution fusion | flops 7046430720 | bytes 17760256 | tf_op jit(solution)/shard_map/dot_general | solution.py:59
  381.2 11.6 %convolution_add_fusion = f32[1024,1536]{1,0:T(8,128)} fusion(f32[1024,1536]{1,0:T(8,128)S(1)} %fusion.174, bf16[1024,2240]{0,1:T(8,128)(2,1)S(1)} %copy-done.95, bf16[1536,2240]{1,0:T(8,128)(2,1)} %bitcast.52), kind=kOutput, calls=%fused_computation.138 | convolution fusion | flops 7048003584 | bytes 24051712 | tf_op jit(solution)/shard_map/dot_general | solution.py:59
  394.7 12.8 %convolution_convert_fusion.1 = bf16[2240,1024]{1,0:T(8,128)(2,1)} fusion(bf16[2240,1536]{1,0:T(8,128)(2,1)} %bitcast.70, bf16[1024,1536]{1,0:T(8,128)(2,1)S(1)} %bitcast.447), kind=kOutput, calls=%fused_computation.126 | convolution fusion | flops 7048724480 | bytes 14614528 | tf_op jit(solution)/shard_map/dot_general | solution.py:59
  407.6 13.7 %fusion.169 = f32[1024,2240]{0,1:T(8,128)} fusion(bf16[1024,1536]{1,0:T(8,128)(2,1)} %all-gather.8.cloned.1.call-done, bf16[1536,2240]{1,0:T(8,128)(2,1)} %bitcast.65), kind=kOutput, calls=%fused_computation.330 | convolution fusion | flops 7046430720 | bytes 19202048 | tf_op jit(solution)/shard_map/dot_general | solution.py:59
  421.3 20.7 %fusion.33 = (bf16[1024,2240]{0,1:T(8,128)(2,1)}, bf16[1024,2240]{0,1:T(8,128)(2,1)}, bf16[1024,2240]{0,1:T(8,128)(2,1)}) fusion(f32[1024,2240]{0,1:T(8,128)} %fusion.169, bf16[2240,1024]{1,0:T(8,128)(2,1)} %convolution_convert_fusion.1, bf16[1024,1536]{1,0:T(8,128)(2,1)S(1)} %copy-done.33, bf16[1536,2240]{1,0:T(8,128)(2,1)} %bitcast.52), kind=kOutput, calls=%fused_computation.90 | convolution fusion | flops 7085424640 | bytes 37552128 | tf_op jit(solution)/shard_map/dot_general | solution.py:59
  442.0 11.4 %fusion.173 = f32[1024,1536]{1,0:T(8,128)S(1)} fusion(bf16[1024,2240]{0,1:T(8,128)(2,1)} %get-tuple-element.81, bf16[1536,2240]{1,0:T(8,128)(2,1)} %bitcast.65), kind=kOutput, calls=%fused_computation.334 | convolution fusion | flops 7046430720 | bytes 17760256 | tf_op jit(solution)/shard_map/dot_general | solution.py:59
  453.4 12.0 %convolution_add_fusion.1 = f32[1024,1536]{1,0:T(8,128)} fusion(f32[1024,1536]{1,0:T(8,128)S(1)} %fusion.173, bf16[1024,2240]{0,1:T(8,128)(2,1)S(1)} %copy-done.96, bf16[1536,2240]{1,0:T(8,128)(2,1)} %bitcast.52), kind=kOutput, calls=%fused_computation.139 | convolution fusion | flops 7048003584 | bytes 24051712 | tf_op jit(solution)/shard_map/dot_general | solution.py:59
  465.4 13.0 %fusion.172 = f32[1024,1536]{1,0:T(8,128)} fusion(bf16[1024,2240]{0,1:T(8,128)(2,1)} %get-tuple-element.77, bf16[2240,1536]{1,0:T(8,128)(2,1)} %bitcast.70), kind=kOutput, calls=%fused_computation.333 | convolution fusion | flops 7046430720 | bytes 17760256 | tf_op jit(solution)/shard_map/dot_general | solution.py:59
  478.5 13.0 %fusion.170 = f32[1024,1536]{1,0:T(8,128)} fusion(bf16[1024,2240]{0,1:T(8,128)(2,1)} %get-tuple-element.76, bf16[2240,1536]{1,0:T(8,128)(2,1)} %bitcast.70), kind=kOutput, calls=%fused_computation.331 | convolution fusion | flops 7046430720 | bytes 17760256 | tf_op jit(solution)/shard_map/dot_general | solution.py:59
  492.9 9.8 pad_maximum_fusion
  502.7 17.1 %fusion.176 = f32[2,2,560,1536]{3,2,1,0:T(8,128)S(1)} fusion(bf16[2,2,560,2048]{3,2,1,0:T(8,128)(2,1)} %bitcast.439, bf16[2048,1536,1,1]{1,0,3,2:T(8,128)(2,1)S(1)} %bitcast.433), kind=kOutput, calls=%fused_computation.337 | convolution fusion | flops 14092861440 | bytes 29229056 | tf_op jit(solution)/shard_map/dot_general | solution.py:59
  519.8 3.6 dynamic-slice_bitcast_fusion.17
  523.5 4.3 copy-done.9
  529.9 20.2 %fusion.41 = f32[1536,2240]{1,0:T(8,128)S(1)} fusion(bf16[2048,1536]{1,0:T(8,128)(2,1)S(1)} %constant_dynamic-update-slice_fusion.16, bf16[1024,2240]{0,1:T(8,128)(2,1)} %get-tuple-element.83, bf16[1024,2240]{0,1:T(8,128)(2,1)} %get-tuple-element.81), kind=kOutput, calls=%fused_computation.98 | convolution fusion | flops 14111211520 | bytes 29229056 | tf_op jit(solution)/shard_map/dot_general | solution.py:59
  550.1 3.6 dynamic-slice_bitcast_fusion.15
  553.8 4.0 copy-done.7
  565.2 5.1 fusion.175
  570.4 20.0 %fusion.37 = f32[1536,2240]{1,0:T(8,128)S(1)} fusion(bf16[2048,1536]{1,0:T(8,128)(2,1)} %copy-done.37, bf16[1024,2240]{0,1:T(8,128)(2,1)} %get-tuple-element.82, bf16[1024,2240]{0,1:T(8,128)(2,1)} %get-tuple-element.80), kind=kOutput, calls=%fused_computation.94 | convolution fusion | flops 14111211520 | bytes 29229056 | tf_op jit(solution)/shard_map/dot_general | solution.py:59
  593.9 4.1 copy-done.8
  598.3 5.0 fusion.88
  604.2 10.1 fusion.29
  614.4 11.0 %fusion.126 = f32[1,512,2,128]{3,1,2,0:T(8,128)S(1)} fusion(bf16[2,6,512,512]{2,3,1,0:T(8,128)(2,1)} %get-tuple-element.227, f32[2,6,512]{2,1,0:T(8,128)S(1)} %neg.22, f32[2,6,512]{2,1,0:T(8,128)S(1)} %copy-done.70, pred[512,512]{0,1:T(8,128)(4,1)S(1)} %copy-done.27, f32[2,512,512,6]{2,1,3,0:T(8,128)} %copy-done.2, f32[2,6,512]{2,1,0:T(8,128)S(1)} %copy-done.65, ...), kind=kOutput, calls=%fused_computation.225 | convolution fusion | flops 837025792 | bytes 21307392 | tf_op jit(solution)/shard_map/transpose(jvp(bqkgd,bskd->bkgqs))/dot_general | solution.py:45
  625.4 8.0 bitcast_convert_fusion
  633.4 4.2 fusion.114
  643.3 8.3 fusion.130
  651.7 6.2 bitcast_add_fusion.1
  660.2 6.2 bitcast_add_fusion.2
  670.2 9.3 bitcast_add_fusion.3
  679.6 4.3 dynamic-slice_bitcast_fusion.20
  683.9 78.3 %collective-permute-done.42 = f32[4,96,2240]{2,1,0:T(8,128)} collective-permute-done((f32[4,96,2240]{2,1,0:T(8,128)}, f32[4,96,2240]{2,1,0:T(8,128)}, u32[]{:S(2)}, u32[]{:S(2)}) %collective-permute-start.42) | collective-permute-done | bytes 3440672 | tf_op jit(solution)/shard_map/ppermute | solution.py:63
  764.5 100.4 %collective-permute-done.40 = f32[4,96,2240]{2,1,0:T(8,128)} collective-permute-done((f32[4,96,2240]{2,1,0:T(8,128)}, f32[4,96,2240]{2,1,0:T(8,128)}, u32[]{:S(2)}, u32[]{:S(2)}) %collective-permute-start.40) | collective-permute-done | bytes 3440672 | tf_op jit(solution)/shard_map/ppermute | solution.py:63
  869.9 5.0 all-to-all-start.4
  874.9 7.7 fusion.78
  888.1 35.5 %all-to-all-done.4 = bf16[4,2,96,2240]{3,2,1,0:T(8,128)(2,1)} async-done(((bf16[4,2,96,2240]{3,2,1,0:T(8,128)(2,1)}), bf16[4,2,96,2240]{3,2,1,0:T(8,128)(2,1)}, u32[]{:S(2)}, u32[]{:S(2)}) %all-to-all-start.4) | async-done | bytes 3440672 | tf_op jit(solution)/shard_map/all_to_all | solution.py:285
  923.6 4.6 all-to-all-start.3
  928.4 3.8 sort.15
  932.3 25.8 %collective-permute-done.44 = f32[560,1536]{1,0:T(8,128)} collective-permute-done((f32[560,1536]{1,0:T(8,128)}, f32[560,1536]{1,0:T(8,128)}, u32[]{:S(2)}, u32[]{:S(2)}) %collective-permute-start.44) | collective-permute-done | bytes 3440672 | tf_op jit(solution)/shard_map/ppermute | solution.py:63
  958.0 4.7 fusion.71
  971.6 4.1 squeeze.123
  978.3 4.1 squeeze.122
  982.4 25.7 %all-to-all-done.3 = f32[16,48,1536]{2,1,0:T(8,128)} async-done(((f32[16,48,1536]{2,1,0:T(8,128)}), f32[16,48,1536]{2,1,0:T(8,128)}, u32[]{:S(2)}, u32[]{:S(2)}) %all-to-all-start.3) | async-done | bytes 4718624 | tf_op jit(solution)/shard_map/all_to_all | solution.py:304
  1008.1 38.7 %conditional.3 = (bf16[9496,1536]{1,0:T(8,128)(2,1)}) conditional(s32[]{:T(128)} %convert_element_type.246, (s32[76,768]{1,0:T(8,128)S(1)}, f32[16,48,1536]{2,1,0:T(8,128)}, s32[768]{0:T(1024)S(1)}, s32[768]{0:T(1024)S(1)}) %tuple.39, (s32[]{:T(128)}, s32[16,512]{1,0:T(8,128)S(1)}, s32[16,512]{1,0:T(8,128)S(1)}, ...), branch_computations={%region_25.27_spmd, %region_27.29_spmd} | conditional | flops 40000057344 | bytes 372815168 | solution.py:319
  1008.8 36.7 %branch_0_fun.1 = bf16[9496,1536]{1,0:T(8,128)(2,1)} custom-call(s32[76]{0:T(128)} %reduce_sum.90.start_ref, s32[768]{0:T(1024)S(1)} %get-tuple-element.44.slot_ref, s32[768]{0:T(1024)S(1)} %get-tuple-element.45.row_ref, f32[768,1536]{1,0:T(8,128)} %bitcast.17.recv_ref), custom_call_target="tpu_custom_call" | custom-call | flops 40000000000 | bytes 40000000 | tf_op jit(solution)/shard_map/cond/branch_0_fun/pallas_call | solution.py:82
  (361 shorter events, 162.5 us)
Async XLA Ops:
  7.2 242.1 %all-gather.6.cloned.1.call-start = ((), (), s32[]{:S(2)}) async-start(), calls=%async_computation.11 | async-start | bytes 11698176 | tf_op jit(solution)/shard_map/all_gather | solution.py:210
  14.2 61.7 %all-to-all-start.2 = ((bf16[4,96,2240]{2,1,0:T(8,128)(2,1)}), bf16[4,96,2240]{2,1,0:T(8,128)(2,1)S(1)}, u32[]{:S(2)}, u32[]{:S(2)}) async-start(bf16[4,96,2240]{2,1,0:T(8,128)(2,1)} %pad_maximum_fusion.5), calls=%async_computation.2 | async-start | bytes 3538944 | tf_op jit(solution)/shard_map/all_to_all | solution.py:222
  53.7 65.0 %copy-start.59 = (s32[16,512]{1,0:T(8,128)}, s32[16,512]{1,0:T(8,128)S(1)}, u32[]{:S(2)}) copy-start(s32[16,512]{1,0:T(8,128)S(1)} %get-tuple-element.165) | copy-start | bytes 98308
  54.0 64.7 %copy-start.57 = (s32[16,512]{1,0:T(8,128)}, s32[16,512]{1,0:T(8,128)S(1)}, u32[]{:S(2)}) copy-start(s32[16,512]{1,0:T(8,128)S(1)} %broadcast_subtract_fusion) | copy-start | bytes 98308
  54.5 21.4 %copy-start.72 = (s32[16,48]{1,0:T(8,128)}, s32[16,48]{1,0:T(8,128)S(1)}, u32[]{:S(2)}) copy-start(s32[16,48]{1,0:T(8,128)S(1)} %select_reduce_fusion) | copy-start | bytes 9220
  54.9 20.9 %copy-start.82 = (pred[16,48]{1,0:T(8,128)(4,1)}, pred[16,48]{1,0:T(8,128)(4,1)S(1)}, u32[]{:S(2)}) copy-start(pred[16,48]{1,0:T(8,128)(4,1)S(1)} %fusion.105) | copy-start | bytes 2308
  75.8 8.8 copy-start.14
  75.9 34.4 %all-to-all-start = ((bf16[16,48,1536]{2,1,0:T(8,128)(2,1)}), bf16[16,48,1536]{2,1,0:T(8,128)(2,1)}, u32[]{:S(2)}, u32[]{:S(2)}) async-start(bf16[16,48,1536]{2,1,0:T(8,128)(2,1)} %bitcast.24), calls=%async_computation | async-start | bytes 4718592 | tf_op jit(solution)/shard_map/all_to_all | solution.py:194
  81.4 34.1 %copy-start.88 = (s32[512]{0:T(512)}, s32[512]{0:T(512)S(1)}, u32[]{:S(2)}) copy-start(s32[512]{0:T(512)S(1)} %select_reduce_fusion.1) | copy-start | bytes 6148
  110.3 30.2 %all-to-all-start.1 = ((bf16[4,96,2240]{2,1,0:T(8,128)(2,1)}), bf16[4,96,2240]{2,1,0:T(8,128)(2,1)}, u32[]{:S(2)}, u32[]{:S(2)}) async-start(bf16[4,96,2240]{2,1,0:T(8,128)(2,1)} %pad_maximum_fusion.4), calls=%async_computation.1 | async-start | bytes 3538944 | tf_op jit(solution)/shard_map/all_to_all | solution.py:222
  115.4 187.8 %all-gather.12.cloned.1.call-start = ((), (), s32[]{:S(2)}) async-start(), calls=%async_computation.20 | async-start | bytes 7864320 | tf_op jit(solution)/shard_map/all_gather | solution.py:213
  123.9 46.8 %copy-start.80 = (f32[512]{0:T(512)}, f32[512]{0:T(512)S(1)}, u32[]{:S(2)}) copy-start(f32[512]{0:T(512)S(1)} %get-tuple-element.75) | copy-start | bytes 6148
  123.9 125.4 %copy-start.10 = (f32[512,1536]{1,0:T(8,128)}, f32[512,1536]{1,0:T(8,128)S(1)}, u32[]{:S(2)}) copy-start(f32[512,1536]{1,0:T(8,128)S(1)} %get-tuple-element.74) | copy-start | bytes 9437188
  123.9 40.7 %collective-permute-start.37 = (bf16[560,1536]{1,0:T(8,128)(2,1)}, bf16[560,1536]{1,0:T(8,128)(2,1)}, u32[]{:S(2)}, u32[]{:S(2)}) collective-permute-start(bf16[560,1536]{1,0:T(8,128)(2,1)} %param.27), channel_id=1, source_target_pairs={{0,2},{2,0},{1,3},{3,1},{4,6},{6,4},{5,7},{7,5},{8,10},{10,8},{9,1... | collective-permute-start | bytes 5160968 | tf_op jit(solution)/shard_map/ppermute | solution.py:63
  125.4 39.2 %collective-permute-start.36 = (bf16[560,1536]{1,0:T(8,128)(2,1)}, bf16[560,1536]{1,0:T(8,128)(2,1)}, u32[]{:S(2)}, u32[]{:S(2)}) collective-permute-start(bf16[560,1536]{1,0:T(8,128)(2,1)} %param.27), channel_id=1, source_target_pairs={{0,1},{1,0},{2,3},{3,2},{4,5},{5,4},{6,7},{7,6},{8,9},{9,8},{10,11... | collective-permute-start | bytes 5160968 | tf_op jit(solution)/shard_map/ppermute | solution.py:63
  125.4 210.6 %all-gather.10.cloned.1.call-start = ((), (), s32[]{:S(2)}) async-start(), calls=%async_computation.14 | async-start | bytes 3932160 | tf_op jit(solution)/shard_map/all_gather | solution.py:247
  132.2 159.3 %copy-start.66 = (f32[1536]{0:T(1024)}, f32[1536]{0:T(1024)S(1)}, u32[]{:S(2)}) copy-start(f32[1536]{0:T(1024)S(1)} %mul.533) | copy-start | bytes 18436
  132.3 117.0 %copy-start.78 = (f32[1536]{0:T(1024)}, f32[1536]{0:T(1024)S(1)}, u32[]{:S(2)}) copy-start(f32[1536]{0:T(1024)S(1)} %mul.509) | copy-start | bytes 18436
  134.8 144.8 %copy-start.26 = (pred[512,512]{0,1:T(8,128)(4,1)}, pred[512,512]{0,1:T(8,128)(4,1)S(1)}, u32[]{:S(2)}) copy-start(pred[512,512]{0,1:T(8,128)(4,1)S(1)} %iota_compare_fusion.4) | copy-start | bytes 786436
  134.9 67.7 %collective-permute-start.34 = (bf16[4,96,2240]{2,1,0:T(8,128)(2,1)}, bf16[4,96,2240]{2,1,0:T(8,128)(2,1)}, u32[]{:S(2)}, u32[]{:S(2)}) collective-permute-start(bf16[4,96,2240]{2,1,0:T(8,128)(2,1)} %copy-done.14), channel_id=1, source_target_pairs={{0,2},{2,0},{1,3},{3,1},{4,6},{6,4},{5,7},{7,5},{8,10},{10,8},{9,1... | collective-permute-start | bytes 5160968 | tf_op jit(solution)/shard_map/ppermute | solution.py:63
  135.4 103.9 %collective-permute-start.33 = (bf16[4,96,2240]{2,1,0:T(8,128)(2,1)}, bf16[4,96,2240]{2,1,0:T(8,128)(2,1)}, u32[]{:S(2)}, u32[]{:S(2)}) collective-permute-start(bf16[4,96,2240]{2,1,0:T(8,128)(2,1)} %copy-done.14), channel_id=1, source_target_pairs={{0,1},{1,0},{2,3},{3,2},{4,5},{5,4},{6,7},{7,6},{8,9},{9,8},{10,11... | collective-permute-start | bytes 5160968 | tf_op jit(solution)/shard_map/ppermute | solution.py:63
  140.5 98.8 %collective-permute-start.31 = (bf16[4,96,2240]{2,1,0:T(8,128)(2,1)}, bf16[4,96,2240]{2,1,0:T(8,128)(2,1)}, u32[]{:S(2)}, u32[]{:S(2)}) collective-permute-start(bf16[4,96,2240]{2,1,0:T(8,128)(2,1)} %all-to-all-done.1), channel_id=1, source_target_pairs={{0,2},{2,0},{1,3},{3,1},{4,6},{6,4},{5,7},{7,5},{8,10},{10,8},{9,1... | collective-permute-start | bytes 5160968 | tf_op jit(solution)/shard_map/ppermute | solution.py:63
  164.6 80.5 %collective-permute-start.30 = (bf16[4,96,2240]{2,1,0:T(8,128)(2,1)}, bf16[4,96,2240]{2,1,0:T(8,128)(2,1)S(1)}, u32[]{:S(2)}, u32[]{:S(2)}) collective-permute-start(bf16[4,96,2240]{2,1,0:T(8,128)(2,1)} %all-to-all-done.1), channel_id=1, source_target_pairs={{0,1},{1,0},{2,3},{3,2},{4,5},{5,4},{6,7},{7,6},{8,9},{9,8},{10,11... | collective-permute-start | bytes 5160968 | tf_op jit(solution)/shard_map/ppermute | solution.py:63
  164.6 129.9 %collective-permute-start.38 = (bf16[560,1536]{1,0:T(8,128)(2,1)}, bf16[560,1536]{1,0:T(8,128)(2,1)}, u32[]{:S(2)}, u32[]{:S(2)}) collective-permute-start(bf16[560,1536]{1,0:T(8,128)(2,1)} %collective-permute-done.37), channel_id=1, source_target_pairs={{0,1},{1,0},{2,3},{3,2},{4,5},{5,4},{6,7},{7,6},{8,9},{9,8},{10,11... | collective-permute-start | bytes 5160968 | tf_op jit(solution)/shard_map/ppermute | solution.py:63
  170.7 78.6 %copy-start.86 = (f32[512]{0:T(512)}, f32[512]{0:T(512)S(1)}, u32[]{:S(2)}) copy-start(f32[512]{0:T(512)S(1)} %fusion.146) | copy-start | bytes 6148
  202.5 94.7 %collective-permute-start.35 = (bf16[4,96,2240]{2,1,0:T(8,128)(2,1)}, bf16[4,96,2240]{2,1,0:T(8,128)(2,1)}, u32[]{:S(2)}, u32[]{:S(2)}) collective-permute-start(bf16[4,96,2240]{2,1,0:T(8,128)(2,1)} %collective-permute-done.34), channel_id=1, source_target_pairs={{0,1},{1,0},{2,3},{3,2},{4,5},{5,4},{6,7},{7,6},{8,9},{9,8},{10,11... | collective-permute-start | bytes 5160968 | tf_op jit(solution)/shard_map/ppermute | solution.py:63
  239.3 60.8 %collective-permute-start.32 = (bf16[4,96,2240]{2,1,0:T(8,128)(2,1)}, bf16[4,96,2240]{2,1,0:T(8,128)(2,1)}, u32[]{:S(2)}, u32[]{:S(2)}) collective-permute-start(bf16[4,96,2240]{2,1,0:T(8,128)(2,1)} %collective-permute-done.31), channel_id=1, source_target_pairs={{0,1},{1,0},{2,3},{3,2},{4,5},{5,4},{6,7},{7,6},{8,9},{9,8},{10,11... | collective-permute-start | bytes 5160968 | tf_op jit(solution)/shard_map/ppermute | solution.py:63
  267.4 9.5 copy-start.16
  294.3 113.3 %all-gather.8.cloned.1.call-start = ((), (), s32[]{:S(2)}) async-start(), calls=%async_computation.12 | async-start | bytes 3932160 | tf_op jit(solution)/shard_map/all_gather | solution.py:247
  322.2 235.6 %reduce-scatter.13.cloned.1.call-start = ((), (), s32[]{:S(2)}) async-start(), calls=%async_computation.17 | async-start | bytes 7864320 | tf_op jit(solution)/shard_map/reduce_scatter | solution.py:254
  336.0 13.3 %copy-start.31 = (bf16[1024,1536]{1,0:T(8,128)(2,1)S(1)}, bf16[1024,1536]{1,0:T(8,128)(2,1)}, u32[]{:S(2)}) copy-start(bf16[1024,1536]{1,0:T(8,128)(2,1)} %all-gather.10.cloned.1.call-done) | copy-start | bytes 9437188
  369.6 11.6 %copy-start.95 = (bf16[1024,2240]{0,1:T(8,128)(2,1)S(1)}, bf16[1024,2240]{0,1:T(8,128)(2,1)}, u32[]{:S(2)}) copy-start(bf16[1024,2240]{0,1:T(8,128)(2,1)} %get-tuple-element.82) | copy-start | bytes 13762564
  392.9 166.6 %reduce-scatter.11.cloned.1.call-start = ((), (), s32[]{:S(2)}) async-start(), calls=%async_computation.16 | async-start | bytes 7864320 | tf_op jit(solution)/shard_map/reduce_scatter | solution.py:254
  407.6 13.7 %copy-start.33 = (bf16[1024,1536]{1,0:T(8,128)(2,1)S(1)}, bf16[1024,1536]{1,0:T(8,128)(2,1)}, u32[]{:S(2)}) copy-start(bf16[1024,1536]{1,0:T(8,128)(2,1)} %all-gather.8.cloned.1.call-done) | copy-start | bytes 9437188
  442.0 11.4 %copy-start.96 = (bf16[1024,2240]{0,1:T(8,128)(2,1)S(1)}, bf16[1024,2240]{0,1:T(8,128)(2,1)}, u32[]{:S(2)}) copy-start(bf16[1024,2240]{0,1:T(8,128)(2,1)} %get-tuple-element.80) | copy-start | bytes 13762564
  465.4 497.3 %reduce-scatter.9.cloned.1.call-start = ((), (), s32[]{:S(2)}) async-start(), calls=%async_computation.15 | async-start | bytes 7864320 | tf_op jit(solution)/shard_map/reduce_scatter | solution.py:263
  478.5 484.3 %reduce-scatter.7.cloned.1.call-start = ((), (), s32[]{:S(2)}) async-start(), calls=%async_computation.13 | async-start | bytes 7864320 | tf_op jit(solution)/shard_map/reduce_scatter | solution.py:263
  491.5 11.2 %slice-start.3 = ((s8[6291456]{0:T(1024)(128)(4,1)}), s8[2097152]{0:T(1024)(128)(4,1)S(1)}, s32[]{:S(2)}) async-start(s8[6291456]{0:T(1024)(128)(4,1)} %bitcast.431), calls=%async_computation.24 | async-start | bytes 4194304
  491.6 557.1 %reduce-scatter.17.cloned.1.call-start = ((), (), s32[]{:S(2)}) async-start(), calls=%async_computation.19 | async-start | bytes 10027008 | tf_op jit(solution)/shard_map/reduce_scatter | solution.py:291
  492.9 9.8 slice-start.4
  527.8 142.5 %collective-permute-start.43 = (f32[2,560,1536]{2,1,0:T(8,128)}, f32[2,560,1536]{2,1,0:T(8,128)}, u32[]{:S(2)}, u32[]{:S(2)}) collective-permute-start(f32[2,560,1536]{2,1,0:T(8,128)} %dynamic-slice_bitcast_fusion.17), channel_id=1, source_target_pairs={{0,1},{1,0},{2,3},{3,2},{4,5},{5,4},{6,7},{7,6},{8,9},{9,8},{10,11... | collective-permute-start | bytes 20643848 | tf_op jit(solution)/shard_map/ppermute | solution.py:63
  529.9 20.2 %copy-start.37 = (bf16[2048,1536]{1,0:T(8,128)(2,1)}, bf16[2048,1536]{1,0:T(8,128)(2,1)S(1)}, u32[]{:S(2)}) copy-start(bf16[2048,1536]{1,0:T(8,128)(2,1)S(1)} %constant_dynamic-update-slice_fusion.16) | copy-start | bytes 18874372
  557.7 94.0 %collective-permute-start.41 = (f32[4,2,96,2240]{3,2,1,0:T(8,128)}, f32[4,2,96,2240]{3,2,1,0:T(8,128)}, u32[]{:S(2)}, u32[]{:S(2)}) collective-permute-start(f32[4,2,96,2240]{3,2,1,0:T(8,128)} %dynamic-slice_bitcast_fusion.15), channel_id=1, source_target_pairs={{0,1},{1,0},{2,3},{3,2},{4,5},{5,4},{6,7},{7,6},{8,9},{9,8},{10,11... | collective-permute-start | bytes 20643848 | tf_op jit(solution)/shard_map/ppermute | solution.py:63
  570.4 480.2 %reduce-scatter.15.cloned.1.call-start = ((), (), s32[]{:S(2)}) async-start(), calls=%async_computation.18 | async-start | bytes 13369344 | tf_op jit(solution)/shard_map/reduce_scatter | solution.py:296
  598.0 62.2 %collective-permute-start.39 = (f32[4,2,96,2240]{3,2,1,0:T(8,128)}, f32[4,2,96,2240]{3,2,1,0:T(8,128)}, u32[]{:S(2)}, u32[]{:S(2)}) collective-permute-start(f32[4,2,96,2240]{3,2,1,0:T(8,128)} %dynamic-slice_bitcast_fusion.16), channel_id=1, source_target_pairs={{0,1},{1,0},{2,3},{3,2},{4,5},{5,4},{6,7},{7,6},{8,9},{9,8},{10,11... | collective-permute-start | bytes 20643848 | tf_op jit(solution)/shard_map/ppermute | solution.py:63
  604.1 10.2 copy-start.38
  604.1 10.2 copy-start.17
  604.1 10.2 copy-start.19
  604.2 10.2 copy-start.70
  604.2 21.2 %slice-start = ((s8[12582912]{0:T(1024)(128)(4,1)}), s8[4194304]{0:T(1024)(128)(4,1)S(1)}, s32[]{:S(2)}) async-start(s8[12582912]{0:T(1024)(128)(4,1)} %bitcast.428), calls=%async_computation.21 | async-start | bytes 8388608
  614.4 11.0 %slice-start.1 = ((s8[12582912]{0:T(1024)(128)(4,1)}), s8[4194304]{0:T(1024)(128)(4,1)S(1)}, s32[]{:S(2)}) async-start(s8[12582912]{0:T(1024)(128)(4,1)} %bitcast.428), calls=%async_computation.22 | async-start | bytes 8388608
  614.4 11.0 %slice-start.2 = ((s8[12582912]{0:T(1024)(128)(4,1)}), s8[4194304]{0:T(1024)(128)(4,1)S(1)}, s32[]{:S(2)}) async-start(s8[12582912]{0:T(1024)(128)(4,1)} %bitcast.428), calls=%async_computation.23 | async-start | bytes 8388608
  614.4 11.0 %copy-start.54 = (bf16[512,2,64]{2,0,1:T(8,128)(2,1)S(1)}, bf16[512,2,64]{2,0,1:T(8,128)(2,1)}, u32[]{:S(2)}) copy-start(bf16[512,2,64]{2,0,1:T(8,128)(2,1)} %copy-done.53) | copy-start | bytes 393220
  614.4 11.0 %copy-start.56 = (bf16[512,2,64]{2,0,1:T(8,128)(2,1)S(1)}, bf16[512,2,64]{2,0,1:T(8,128)(2,1)}, u32[]{:S(2)}) copy-start(bf16[512,2,64]{2,0,1:T(8,128)(2,1)} %copy-done.55) | copy-start | bytes 393220
  625.4 8.0 copy-start.39
  659.9 102.3 %collective-permute-start.42 = (f32[4,96,2240]{2,1,0:T(8,128)}, f32[4,96,2240]{2,1,0:T(8,128)}, u32[]{:S(2)}, u32[]{:S(2)}) collective-permute-start(f32[4,96,2240]{2,1,0:T(8,128)} %dynamic-slice_bitcast_fusion.18), channel_id=1, source_target_pairs={{0,2},{2,0},{1,3},{3,1},{4,6},{6,4},{5,7},{7,5},{8,10},{10,8},{9,1... | collective-permute-start | bytes 10321928 | tf_op jit(solution)/shard_map/ppermute | solution.py:63
  668.4 196.5 %collective-permute-start.40 = (f32[4,96,2240]{2,1,0:T(8,128)}, f32[4,96,2240]{2,1,0:T(8,128)}, u32[]{:S(2)}, u32[]{:S(2)}) collective-permute-start(f32[4,96,2240]{2,1,0:T(8,128)} %dynamic-slice_bitcast_fusion.19), channel_id=1, source_target_pairs={{0,2},{2,0},{1,3},{3,1},{4,6},{6,4},{5,7},{7,5},{8,10},{10,8},{9,1... | collective-permute-start | bytes 10321928 | tf_op jit(solution)/shard_map/ppermute | solution.py:63
  683.9 274.2 %collective-permute-start.44 = (f32[560,1536]{1,0:T(8,128)}, f32[560,1536]{1,0:T(8,128)}, u32[]{:S(2)}, u32[]{:S(2)}) collective-permute-start(f32[560,1536]{1,0:T(8,128)} %dynamic-slice_bitcast_fusion.20), channel_id=1, source_target_pairs={{0,2},{2,0},{1,3},{3,1},{4,6},{6,4},{5,7},{7,5},{8,10},{10,8},{9,1... | collective-permute-start | bytes 10321928 | tf_op jit(solution)/shard_map/ppermute | solution.py:63
  869.9 53.7 %all-to-all-start.4 = ((bf16[4,2,96,2240]{3,2,1,0:T(8,128)(2,1)}), bf16[4,2,96,2240]{3,2,1,0:T(8,128)(2,1)}, u32[]{:S(2)}, u32[]{:S(2)}) async-start(bf16[4,2,96,2240]{3,2,1,0:T(8,128)(2,1)} %copy.194), calls=%async_computation.10 | async-start | bytes 7077888 | tf_op jit(solution)/shard_map/all_to_all | solution.py:285
  888.1 40.2 %copy-start.73 = (s32[16,48]{1,0:T(8,128)S(1)}, s32[16,48]{1,0:T(8,128)}, u32[]{:S(2)}) copy-start(s32[16,48]{1,0:T(8,128)} %copy-done.72) | copy-start | bytes 9220
  888.1 40.2 %copy-start.83 = (pred[16,48]{1,0:T(8,128)(4,1)S(1)}, pred[16,48]{1,0:T(8,128)(4,1)}, u32[]{:S(2)}) copy-start(pred[16,48]{1,0:T(8,128)(4,1)} %copy-done.82) | copy-start | bytes 2308
  923.6 84.5 %all-to-all-start.3 = ((f32[16,48,1536]{2,1,0:T(8,128)}), f32[16,48,1536]{2,1,0:T(8,128)}, u32[]{:S(2)}, u32[]{:S(2)}) async-start(f32[16,48,1536]{2,1,0:T(8,128)} %select_select_fusion.1), calls=%async_computation.7 | async-start | bytes 9437184 | tf_op jit(solution)/shard_map/all_to_all | solution.py:304
  975.7 32.4 %copy-start.58 = (s32[16,512]{1,0:T(8,128)S(1)}, s32[16,512]{1,0:T(8,128)}, u32[]{:S(2)}) copy-start(s32[16,512]{1,0:T(8,128)} %copy-done.57) | copy-start | bytes 98308
  975.7 32.4 %copy-start.60 = (s32[16,512]{1,0:T(8,128)S(1)}, s32[16,512]{1,0:T(8,128)}, u32[]{:S(2)}) copy-start(s32[16,512]{1,0:T(8,128)} %copy-done.59) | copy-start | bytes 98308
  (57 other events, 250.1 us)
Sparse Core Ops, SparseCore 0:
  11.0 80.9 all-gather.5
  125.5 68.3 all-gather.11
  294.4 41.5 all-gather.9
  338.2 40.0 all-gather.7
  393.0 66.2 reduce-scatter.12
  465.5 65.8 reduce-scatter.10
  534.4 66.2 reduce-scatter.8
  603.7 66.2 reduce-scatter.6
  674.7 109.7 reduce-scatter.16
  788.9 147.9 reduce-scatter.14
